TPU v7x, 32 devices: a whole 2x2x4 slice. The times are simulated.
32 devices in a mesh: shot: 8 (over z, y), depth: 4 (over x, core).
Axes of the slice: x: 2, y: 2, z: 4, core: 2. Of those that a mesh axis runs over, the one named last changes fastest.
Arguments:
- correlation: float32 [16, 16, 32, 512], P('shot', None, None, 'depth'), may hold values from -6 to 6
- illumination: float32 [16, 16, 32, 512], P('shot', None, None, 'depth'), may hold values from 0.25 to 4
- aperture: int32 [16, 4], P('shot'), may hold values from 0 to 32, as said below
Outputs:
- stack: float32 [16, 32, 512], P('shot', None, 'depth')
Inputs may be any that keep to these rules, and one draw needn't show every extreme that they name: For every shot, 0 <= aperture[s,0] < aperture[s,1] <= 16 and 0 <= aperture[s,2] < aperture[s,3] <= 32; each box spans a quarter to a half of the grid along each of the two dimensions.
All inputs are finite; a program needn't handle non-finite values.
Results may differ from a plain program's by a relative error of at most 0.0003.
Values sent between devices are 32-bit elements.
No kernel may reach another device: no remote copies, remote signals or barrier semaphores. Data moves between devices by JAX's collectives and lax.ppermute only.
A program may use at most 64 MiB of HBM per device.

v0:
```python
import math

import jax
import jax.numpy as jnp
from jax import lax
from jax.sharding import PartitionSpec as P


def padded_2(block, sides, width):
    for axis, dim in sides:
        count = lax.axis_size(axis)
        forward = [(i, i + 1) for i in range(count - 1)]
        backward = [(target, source) for source, target in forward]
        low = lax.ppermute(
            lax.slice_in_dim(block, block.shape[dim] - width, None, axis=dim), axis, forward
        )
        high = lax.ppermute(lax.slice_in_dim(block, 0, width, axis=dim), axis, backward)
        block = jnp.concatenate([low, block, high], axis=dim)
    return block


def on_device(correlation, illumination, aperture):
    shots, rows, cols, slab = correlation.shape
    first = lax.broadcasted_iota(jnp.int32, (1, rows, cols, 1), 1)
    second = lax.broadcasted_iota(jnp.int32, (1, rows, cols, 1), 2)
    bounds = aperture.reshape(shots, 4, 1, 1, 1)
    inside = (
        (first >= bounds[:, 0])
        & (first < bounds[:, 1])
        & (second >= bounds[:, 2])
        & (second < bounds[:, 3])
    )
    normalized = inside.astype(jnp.float32) * correlation / (illumination + 0.1)
    padded = padded_2(normalized, (("depth", 3),), 1)
    padded = jnp.pad(padded, ((0, 0), (1, 1), (1, 1), (0, 0)))
    beside = padded[:, 2:, 1:-1, 1:-1] + padded[:, :-2, 1:-1, 1:-1]
    beside = beside + padded[:, 1:-1, 2:, 1:-1] + padded[:, 1:-1, :-2, 1:-1]
    beside = beside + padded[:, 1:-1, 1:-1, 2:] + padded[:, 1:-1, 1:-1, :-2]
    filtered = 6.0 * normalized - beside
    local_energy = jnp.sum(filtered * filtered, axis=(1, 2, 3))
    cells = rows * cols * slab * lax.axis_size("depth")
    total_shots = shots * lax.axis_size("shot")
    meansq = lax.psum(local_energy, "depth") / cells
    peak = lax.pmax(jnp.max(meansq), "shot")
    weight = 1.0 / jnp.sqrt(meansq + 0.5 * peak + 1.0)
    weighted = jnp.sum(weight.reshape(shots, 1, 1, 1) * filtered, axis=0) / math.sqrt(total_shots)
    return lax.psum_scatter(weighted, "shot", scatter_dimension=0, tiled=True)


def solution(mesh):
    return jax.shard_map(
        on_device,
        mesh=mesh,
        in_specs=(P("shot", None, None, "depth"), P("shot", None, None, "depth"), P("shot", None)),
        out_specs=P("shot", None, "depth"),
        check_vma=False,
    )
```

profile of v0, /device:TPU:0, one launch (start us, length us, event | category | flops | bytes accessed | tf_op | source)
XLA Modules:
  0.0 121.8 jit_solution(7367261136840748524)
XLA Ops:
  6.5 0.0 reduce-scatter.2.cloned.1.call-start
  6.5 1.0 slice_reduce_fusion.3
  7.6 0.1 fusion.9
  7.7 1.4 %add_divide_fusion = f32[2,16,32,128]{3,2,1,0:T(8,128)S(1)} fusion(f32[2,16,32,128]{3,2,1,0:T(8,128)} %param.4, f32[2,16,32,128]{3,2,1,0:T(8,128)} %param.3, f32[2,16,32]{2,1,0:T(8,128)S(1)} %fusion.9), kind=kLoop, calls=%fused_computation.19 | loop fusion | flops 393216 | bytes 1576960 | tf_op jit(solution)/shard_map/div | solution.py:33
  9.1 0.2 fusion.11
  9.3 1.3 %collective-permute-start.1 = (f32[2,16,32,1]{3,2,1,0:T(8,128)S(1)}, f32[2,16,32,1]{3,2,1,0:T(8,128)S(1)}, u32[]{:S(2)}, u32[]{:S(2)}) collective-permute-start(f32[2,16,32,1]{3,2,1,0:T(8,128)S(1)} %get-tuple-element.11), channel_id=1, source_target_pairs={{1,0},{2,1},{3,2},{5,4},{6,5},{7,6},{9,8},{10,9},{11,10},{13,12},{... | collective-permute-start | bytes 12296 | tf_op jit(solution)/shard_map/ppermute | solution.py:17
  10.6 3.1 %collective-permute-start = (f32[2,16,32,1]{3,2,1,0:T(8,128)S(1)}, f32[2,16,32,1]{3,2,1,0:T(8,128)S(1)}, u32[]{:S(2)}, u32[]{:S(2)}) collective-permute-start(f32[2,16,32,1]{3,2,1,0:T(8,128)S(1)} %get-tuple-element.12), channel_id=1, source_target_pairs={{0,1},{1,2},{2,3},{4,5},{5,6},{6,7},{8,9},{9,10},{10,11},{12,13},{... | collective-permute-start | bytes 12296 | tf_op jit(solution)/shard_map/ppermute | solution.py:14
  13.7 0.0 collective-permute-done.1
  13.7 1.5 %collective-permute-done = f32[2,16,32,1]{3,2,1,0:T(8,128)S(1)} collective-permute-done((f32[2,16,32,1]{3,2,1,0:T(8,128)S(1)}, f32[2,16,32,1]{3,2,1,0:T(8,128)S(1)}, u32[]{:S(2)}, u32[]{:S(2)}) %collective-permute-start) | collective-permute-done | bytes 4128 | tf_op jit(solution)/shard_map/ppermute | solution.py:14
  15.1 0.6 select_maximum_fusion
  15.7 1.1 multiply_reduce_fusion.1
  16.8 13.1 %psum.7 = f32[2]{0:T(128)S(1)} all-reduce(f32[2]{0:T(128)S(1)} %get-tuple-element.9), channel_id=1, replica_groups=mesh['shot'=8,'depth'=4] {'depth'}, use_global_device_ids=true, to_apply=%region_1.2 | all-reduce | flops 2 | bytes 16 | tf_op jit(solution)/shard_map/psum | solution.py:43
  29.9 0.6 multiply_reduce_fusion.2
  30.5 22.3 %pmax.7 = f32[]{:T(128)} all-reduce(f32[]{:T(128)} %multiply_reduce_fusion.2), channel_id=1, replica_groups=mesh['shot'=8,'depth'=4] {'shot'}, use_global_device_ids=true, to_apply=%region_3.4 | all-reduce | flops 1 | bytes 8 | tf_op jit(solution)/shard_map/pmax | solution.py:44
  53.5 0.1 multiply_reduce_fusion
  53.6 0.7 broadcast_multiply_fusion
  54.3 0.0 reduce-scatter.2.cloned.1.call-update
  54.3 60.6 %reduce-scatter.2.cloned.1.call-done = f32[2,32,128]{2,1,0:T(8,128)} async-done(((f32[16,32,128]{2,1,0:T(8,128)}), f32[2,32,128]{2,1,0:T(8,128)}) %reduce-scatter.2.cloned.1.call-update) | async-done | bytes 32784 | tf_op jit(solution)/shard_map/reduce_scatter | solution.py:47
  (1 shorter events, 0.0 us)
Async XLA Ops:
  6.5 108.4 %reduce-scatter.2.cloned.1.call-start = ((), (), s32[]{:S(2)}) async-start(), calls=%async_computation.1 | async-start | bytes 294912 | tf_op jit(solution)/shard_map/reduce_scatter | solution.py:47
  9.3 4.4 %collective-permute-start.1 = (f32[2,16,32,1]{3,2,1,0:T(8,128)S(1)}, f32[2,16,32,1]{3,2,1,0:T(8,128)S(1)}, u32[]{:S(2)}, u32[]{:S(2)}) collective-permute-start(f32[2,16,32,1]{3,2,1,0:T(8,128)S(1)} %get-tuple-element.11), channel_id=1, source_target_pairs={{1,0},{2,1},{3,2},{5,4},{6,5},{7,6},{9,8},{10,9},{11,10},{13,12},{... | collective-permute-start | bytes 12296 | tf_op jit(solution)/shard_map/ppermute | solution.py:17
  10.6 4.6 %collective-permute-start = (f32[2,16,32,1]{3,2,1,0:T(8,128)S(1)}, f32[2,16,32,1]{3,2,1,0:T(8,128)S(1)}, u32[]{:S(2)}, u32[]{:S(2)}) collective-permute-start(f32[2,16,32,1]{3,2,1,0:T(8,128)S(1)} %get-tuple-element.12), channel_id=1, source_target_pairs={{0,1},{1,2},{2,3},{4,5},{5,6},{6,7},{8,9},{9,10},{10,11},{12,13},{... | collective-permute-start | bytes 12296 | tf_op jit(solution)/shard_map/ppermute | solution.py:14
Sparse Core Ops, SparseCore 0:
  54.4 60.4 reduce-scatter.1
where the time goes:
time: 122 us
  waiting for transfers between devices  62.1 us (51%)
  blocking collectives  35.4 us (29%)
  between operations  14.1 us (12%)
  other arithmetic  4.62 us (4%)
  starting transfers between devices  4.36 us (4%)
  local copies, waits for them, and re-layouts  1.25 us (1%)
    reduce_scatter x1, waiting for transfers between devices, on_device(): return lax.psum_scatter(weighted, 'shot', scatter_dimension=0, tiled=True)  60.6 us
    pmax x1, blocking collectives, on_device(): peak = lax.pmax(jnp.max(meansq), 'shot')  22.3 us
    psum x1, blocking collectives, on_device(): meansq = lax.psum(local_energy, 'depth') / cells  13.1 us
    ppermute x1, starting transfers between devices, padded_2(): lax.ppermute(lax.slice_in_dim(block, block.shape[dim] - width, None, axis...  3.06 us
  transfers between devices with their start and end apart: 3, of which 2 were waited for; matrix products, arithmetic and copies ran while one was open for 0% of the time, Pallas kernels for 0%

commit v1 on v0

v1 whole, which is shorter than its diff:
```python
import math

import jax
import jax.numpy as jnp
from jax import lax
from jax.experimental import pallas as pl
from jax.experimental.pallas import tpu as pltpu
from jax.sharding import PartitionSpec as P


def local_filter_kernel(aperture, correlation, illumination, partial, first_edge, last_edge, padded):
    shots, rows, cols, slab = correlation.shape
    second = lax.broadcasted_iota(jnp.int32, (cols, slab), 0)
    lane = lax.broadcasted_iota(jnp.int32, (cols, slab), 1)
    zero = jnp.zeros((cols, slab), jnp.float32)
    group = 128 // cols
    for s in range(shots):
        padded[0] = zero
        padded[rows + 1] = zero
        in_cols = (second >= aperture[s, 2]) & (second < aperture[s, 3])
        for x in range(rows):
            keep = in_cols & (x >= aperture[s, 0]) & (x < aperture[s, 1])
            padded[x + 1] = jnp.where(keep, correlation[s, x] / (illumination[s, x] + 0.1), 0.0)
        for c in range(rows // group):
            turned = padded[c * group + 1 : (c + 1) * group + 1].reshape(group * cols, slab).T
            at = s * (rows // group) + c
            first_edge[at : at + 1] = turned[0:1]
            last_edge[at : at + 1] = turned[slab - 1 : slab]
        for x in range(rows):
            n = padded[x + 1]
            beside = padded[x] + padded[x + 2]
            beside += jnp.where(second == 0, 0.0, pltpu.roll(n, 1, 0))
            beside += jnp.where(second == cols - 1, 0.0, pltpu.roll(n, cols - 1, 0))
            beside += jnp.where(lane == 0, 0.0, pltpu.roll(n, 1, 1))
            beside += jnp.where(lane == slab - 1, 0.0, pltpu.roll(n, slab - 1, 1))
            partial[s, x] = 6.0 * n - beside


def finish_filter_kernel(partial, low, high, filtered, energy):
    shots, rows, cols, slab = partial.shape
    owners, _, own = filtered.shape[:3]
    group = 128 // cols
    depth = lax.broadcasted_iota(jnp.int32, (slab, 128), 0)
    for s in range(shots):
        total = jnp.zeros((cols, slab), jnp.float32)
        for c in range(rows // group):
            at = s * (rows // group) + c
            halo = jnp.where(depth == 0, low[at : at + 1], jnp.where(depth == slab - 1, high[at : at + 1], 0.0)).T
            for g in range(group):
                x = c * group + g
                value = partial[s, x] - halo[g * cols : (g + 1) * cols]
                filtered[x // own, s, x % own] = value
                total += value * value
        energy[:, s : s + 1, :] = jnp.broadcast_to(jnp.sum(total, axis=0, keepdims=True)[None], (energy.shape[0], 1, slab))


def combine_kernel(cells, total_shots, energy, filtered, stack):
    owners, shots, own, cols, slab = filtered.shape
    slabs = energy.shape[0] // owners
    sums = []
    for g in range(owners):
        part = energy[g * slabs]
        for d in range(1, slabs):
            part = part + energy[g * slabs + d]
        sums.append(part)
    meansq = jnp.sum(jnp.concatenate(sums, axis=0), axis=1, keepdims=True) / cells
    peak = jnp.max(meansq, axis=0, keepdims=True)
    weight = (1.0 / math.sqrt(total_shots)) / jnp.sqrt(meansq + 0.5 * peak + 1.0)
    weight = jnp.broadcast_to(weight, (owners * shots, slab))
    for j in range(own):
        acc = jnp.zeros((cols, slab), jnp.float32)
        for g in range(owners):
            for s in range(shots):
                at = g * shots + s
                acc += weight[at : at + 1] * filtered[g, s, j]
        stack[j] = acc


def on_device(correlation, illumination, aperture):
    shots, rows, cols, slab = correlation.shape
    owners, slabs = lax.axis_size("shot"), lax.axis_size("depth")
    own = rows // owners
    f32 = jnp.float32
    vmem = pl.BlockSpec(memory_space=pltpu.VMEM)
    smem = pl.BlockSpec(memory_space=pltpu.SMEM)
    edge = jax.ShapeDtypeStruct((shots * rows * cols // 128, 128), f32)
    partial, first_edge, last_edge = pl.pallas_call(
        local_filter_kernel,
        out_shape=(jax.ShapeDtypeStruct(correlation.shape, f32), edge, edge),
        in_specs=[smem, vmem, vmem],
        out_specs=(vmem, vmem, vmem),
        scratch_shapes=[pltpu.VMEM((rows + 2, cols, slab), f32)],
        name="local_filter",
    )(aperture, correlation, illumination)
    forward = [(i, i + 1) for i in range(slabs - 1)]
    low = lax.ppermute(last_edge, "depth", forward)
    high = lax.ppermute(first_edge, "depth", [(b, a) for a, b in forward])
    filtered, energy = pl.pallas_call(
        finish_filter_kernel,
        out_shape=(
            jax.ShapeDtypeStruct((owners, shots, own, cols, slab), f32),
            jax.ShapeDtypeStruct((owners * slabs, shots, slab), f32),
        ),
        in_specs=[vmem, vmem, vmem],
        out_specs=(vmem, vmem),
        name="finish_filter",
    )(partial, low, high)
    filtered = lax.all_to_all(filtered, "shot", 0, 0, tiled=True)
    energy = lax.all_to_all(energy, ("shot", "depth"), 0, 0, tiled=True)
    cells = rows * cols * slab * slabs

    def body(*refs):
        combine_kernel(cells, shots * owners, *refs)

    return pl.pallas_call(
        body,
        out_shape=jax.ShapeDtypeStruct((own, cols, slab), f32),
        in_specs=[vmem, vmem],
        out_specs=vmem,
        name="combine",
    )(energy, filtered)


def solution(mesh):
    return jax.shard_map(
        on_device,
        mesh=mesh,
        in_specs=(P("shot", None, None, "depth"), P("shot", None, None, "depth"), P("shot", None)),
        out_specs=P("shot", None, "depth"),
        check_vma=False,
    )
```

time: 122 us -> 48.5 us (0.40)
  waiting for transfers between devices: 62.1 us -> 4.05 us
  between operations: 14.1 us -> 0.04 us
  Pallas kernels: 0 us -> 6.37 us
  other arithmetic: 4.62 us -> 0 us
  blocking collectives: 35.4 us -> 33.4 us
    reduce_scatter x1 -> x0, waiting for transfers between devices: 60.6 us -> none  [on_device(): return lax.psum_scatter(weighted, 'shot', scatter_dimension=0, tiled=True)]
    all_to_all x0 -> x2, blocking collectives: none -> 33.4 us  [the longest x1 19.2 us: on_device(): filtered = lax.all_to_all(filtered, 'shot', 0, 0, tiled=True)]
    pmax x1 -> x0, blocking collectives: 22.3 us -> none  [on_device(): peak = lax.pmax(jnp.max(meansq), 'shot')]
    psum x1 -> x0, blocking collectives: 13.1 us -> none  [on_device(): meansq = lax.psum(local_energy, 'depth') / cells]
    pallas_call x0 -> x3, Pallas kernels: none -> 6.37 us  [the longest x1 2.5 us: on_device(): pl.pallas_call(local_filter_kernel, out_shape=(jax.ShapeDtypeStruct(corre...]
    ppermute x2, waiting for transfers between devices: 1.48 us -> 4.05 us  [the longest x1 4.05 us: on_device(): high = lax.ppermute(first_edge, 'depth', [(b, a) for a, b in forward])]
    div x2 -> x0, other arithmetic: 2.12 us -> none  [the longest x1 1.41 us: on_device(): normalized = inside.astype(jnp.float32) * correlation / (illumination + 0.1)]
    slice x2 -> x0, local copies, waits for them, and re-layouts: 1.25 us -> none  [the longest x1 1.04 us: on_device(): bounds[:, 0]]
  transfers between devices with their start and end apart: 3 -> 2, of which waited for: 2 -> 1; matrix products, arithmetic and copies ran while one was open for 0% -> 0% of each run, Pallas kernels for 0% -> 0%
where the time goes in v1:
time: 48.5 us; the launch traced here: 48.1 us
  blocking collectives  33.4 us (69%)
  Pallas kernels  6.37 us (13%)
  waiting for transfers between devices  4.05 us (8%)
  starting transfers between devices  3.68 us (8%)
  local copies, waits for them, and re-layouts  0.6 us (1%)
    all_to_all x1, blocking collectives, on_device(): filtered = lax.all_to_all(filtered, 'shot', 0, 0, tiled=True)  19.2 us
    all_to_all x1, blocking collectives, on_device(): energy = lax.all_to_all(energy, ('shot', 'depth'), 0, 0, tiled=True)  14.3 us
    ppermute x1, waiting for transfers between devices, on_device(): high = lax.ppermute(first_edge, 'depth', [(b, a) for a, b in forward])  4.05 us
    pallas_call x1, Pallas kernels, on_device(): pl.pallas_call(local_filter_kernel, out_shape=(jax.ShapeDtypeStruct(corre...  2.5 us
    ppermute x1, starting transfers between devices, on_device(): low = lax.ppermute(last_edge, 'depth', forward)  2.38 us
    pallas_call x1, Pallas kernels, on_device(): pl.pallas_call(finish_filter_kernel, out_shape=(jax.ShapeDtypeStruct((own...  2.04 us
    pallas_call x1, Pallas kernels, on_device(): pl.pallas_call(body, out_shape=jax.ShapeDtypeStruct((own, cols, slab), f3...  1.82 us
    ppermute x1, starting transfers between devices, on_device(): high = lax.ppermute(first_edge, 'depth', [(b, a) for a, b in forward])  1.29 us
  transfers between devices with their start and end apart: 2, of which 1 were waited for; matrix products, arithmetic and copies ran while one was open for 0% of the time, Pallas kernels for 0%

profile of v1, /device:TPU:0, one launch (start us, length us, event | category | flops | bytes accessed | tf_op | source)
XLA Modules:
  0.0 48.1 jit_solution(4522608114154138129)
XLA Ops:
  0.0 2.5 %local_filter.1 = (f32[2,16,32,128]{3,2,1,0:T(8,128)}, f32[8,128]{1,0:T(8,128)}, f32[8,128]{1,0:T(8,128)}) custom-call(s32[2,4]{1,0:T(2,128)} %aperture.1, f32[2,16,32,128]{3,2,1,0:T(8,128)} %correlation.1, f32[2,16,32,128]{3,2,1,0:T(8,128)} %illumination.1), custom_call_target="tpu_custom_call" | custom-call | tf_op jit(solution)/shard_map/local_filter/pallas_call | solution.py:87
  2.5 2.4 %collective-permute-start = (f32[8,128]{1,0:T(8,128)}, f32[8,128]{1,0:T(8,128)S(1)}, u32[]{:S(2)}, u32[]{:S(2)}) collective-permute-start(f32[8,128]{1,0:T(8,128)} %get-tuple-element.11), channel_id=1, source_target_pairs={{0,1},{1,2},{2,3},{4,5},{5,6},{6,7},{8,9},{9,10},{10,11},{12,13},{... | collective-permute-start | bytes 12296 | tf_op jit(solution)/shard_map/ppermute | solution.py:96
  4.9 1.3 %collective-permute-start.1 = (f32[8,128]{1,0:T(8,128)}, f32[8,128]{1,0:T(8,128)S(1)}, u32[]{:S(2)}, u32[]{:S(2)}) collective-permute-start(f32[8,128]{1,0:T(8,128)} %get-tuple-element.12), channel_id=1, source_target_pairs={{1,0},{2,1},{3,2},{5,4},{6,5},{7,6},{9,8},{10,9},{11,10},{13,12},{... | collective-permute-start | bytes 12296 | tf_op jit(solution)/shard_map/ppermute | solution.py:97
  6.2 0.0 collective-permute-done.low
  6.2 0.0 copy-start
  6.2 4.0 %collective-permute-done.1.high = f32[8,128]{1,0:T(8,128)S(1)} collective-permute-done((f32[8,128]{1,0:T(8,128)}, f32[8,128]{1,0:T(8,128)S(1)}, u32[]{:S(2)}, u32[]{:S(2)}) %collective-permute-start.1) | collective-permute-done | bytes 4128 | tf_op jit(solution)/shard_map/ppermute | solution.py:97
  10.3 0.0 copy-start.1
  10.3 0.0 copy-done
  10.3 0.6 %copy-done.1 = f32[8,128]{1,0:T(8,128)} copy-done((f32[8,128]{1,0:T(8,128)}, f32[8,128]{1,0:T(8,128)S(1)}, u32[]{:S(2)}) %copy-start.1) | copy-done | bytes 4120
  10.9 2.0 %finish_filter.1 = (f32[8,2,2,32,128]{4,3,2,1,0:T(8,128)}, f32[32,2,128]{2,1,0:T(2,128)}) custom-call(f32[2,16,32,128]{3,2,1,0:T(8,128)} %get-tuple-element.10.partial, f32[8,128]{1,0:T(8,128)} %copy-done, f32[8,128]{1,0:T(8,128)} %copy-done.1), custom_call_target="tpu_custom_call" | custom-call | tf_op jit(solution)/shard_map/finish_filter/pallas_call | solution.py:98
  12.9 14.3 %all_to_all.10.refs_0_ = f32[32,2,128]{2,1,0:T(2,128)} all-to-all(f32[32,2,128]{2,1,0:T(2,128)} %get-tuple-element.13), channel_id=1, replica_groups=mesh['shot'=8,'depth'=4] {'shot','depth'}, dimensions={0} | all-to-all | bytes 65536 | tf_op jit(solution)/shard_map/all_to_all | solution.py:109
  27.2 19.2 %all_to_all.11.refs_1_ = f32[8,2,2,32,128]{4,3,2,1,0:T(8,128)} all-to-all(f32[8,2,2,32,128]{4,3,2,1,0:T(8,128)} %get-tuple-element.14), channel_id=1, replica_groups=mesh['shot'=8,'depth'=4] {'shot'}, dimensions={0} | all-to-all | bytes 1048576 | tf_op jit(solution)/shard_map/all_to_all | solution.py:108
  46.3 1.8 %combine.1 = f32[2,32,128]{2,1,0:T(8,128)} custom-call(f32[32,2,128]{2,1,0:T(2,128)} %all_to_all.10.refs_0_, f32[8,2,2,32,128]{4,3,2,1,0:T(8,128)} %all_to_all.11.refs_1_), custom_call_target="tpu_custom_call" | custom-call | tf_op jit(solution)/shard_map/combine/pallas_call | solution.py:115
Async XLA Ops:
  2.5 3.7 %collective-permute-start = (f32[8,128]{1,0:T(8,128)}, f32[8,128]{1,0:T(8,128)S(1)}, u32[]{:S(2)}, u32[]{:S(2)}) collective-permute-start(f32[8,128]{1,0:T(8,128)} %get-tuple-element.11), channel_id=1, source_target_pairs={{0,1},{1,2},{2,3},{4,5},{5,6},{6,7},{8,9},{9,10},{10,11},{12,13},{... | collective-permute-start | bytes 12296 | tf_op jit(solution)/shard_map/ppermute | solution.py:96
  4.9 5.4 %collective-permute-start.1 = (f32[8,128]{1,0:T(8,128)}, f32[8,128]{1,0:T(8,128)S(1)}, u32[]{:S(2)}, u32[]{:S(2)}) collective-permute-start(f32[8,128]{1,0:T(8,128)} %get-tuple-element.12), channel_id=1, source_target_pairs={{1,0},{2,1},{3,2},{5,4},{6,5},{7,6},{9,8},{10,9},{11,10},{13,12},{... | collective-permute-start | bytes 12296 | tf_op jit(solution)/shard_map/ppermute | solution.py:97
  6.2 4.1 %copy-start = (f32[8,128]{1,0:T(8,128)}, f32[8,128]{1,0:T(8,128)S(1)}, u32[]{:S(2)}) copy-start(f32[8,128]{1,0:T(8,128)S(1)} %collective-permute-done.low) | copy-start | bytes 12292
  10.3 0.6 %copy-start.1 = (f32[8,128]{1,0:T(8,128)}, f32[8,128]{1,0:T(8,128)S(1)}, u32[]{:S(2)}) copy-start(f32[8,128]{1,0:T(8,128)S(1)} %collective-permute-done.1.high) | copy-start | bytes 12292

commit v2 on v1

v2 whole, which is shorter than its diff:
```python
import math

import jax
import jax.numpy as jnp
from jax import lax
from jax.experimental import pallas as pl
from jax.experimental.pallas import tpu as pltpu
from jax.sharding import PartitionSpec as P


def local_filter_kernel(
    aperture, correlation_hbm, illumination_hbm, partial, first_edge, last_edge, padded, correlation, illumination, arrived
):
    shots, rows, cols, slab = correlation.shape
    owners = first_edge.shape[0]
    own = rows // owners
    copies = []
    for s in range(shots):
        copies.append((
            pltpu.make_async_copy(correlation_hbm.at[s], correlation.at[s], arrived.at[0, s]),
            pltpu.make_async_copy(illumination_hbm.at[s], illumination.at[s], arrived.at[1, s]),
        ))
        for copy in copies[s]:
            copy.start()
    second = lax.broadcasted_iota(jnp.int32, (cols, slab), 0)
    lane = lax.broadcasted_iota(jnp.int32, (cols, slab), 1)
    zero = jnp.zeros((cols, slab), jnp.float32)
    for s in range(shots):
        padded[s, 0] = zero
        padded[s, rows + 1] = zero
        for copy in copies[s]:
            copy.wait()
        in_cols = (second >= aperture[s, 2]) & (second < aperture[s, 3])
        for x in range(rows):
            keep = in_cols & (x >= aperture[s, 0]) & (x < aperture[s, 1])
            padded[s, x + 1] = jnp.where(keep, correlation[s, x] / (illumination[s, x] + 0.1), 0.0)
        for x in range(rows):
            n = padded[s, x + 1]
            beside = padded[s, x] + padded[s, x + 2]
            beside += jnp.where(second == 0, 0.0, pltpu.roll(n, 1, 0))
            beside += jnp.where(second == cols - 1, 0.0, pltpu.roll(n, cols - 1, 0))
            beside += jnp.where(lane == 0, 0.0, pltpu.roll(n, 1, 1))
            beside += jnp.where(lane == slab - 1, 0.0, pltpu.roll(n, slab - 1, 1))
            partial[s, x] = 6.0 * n - beside
    for r in range(owners):
        held = jnp.concatenate([padded[s, x + 1] for s in range(shots) for x in range(r * own, (r + 1) * own)], axis=0)
        turned = held.T
        first_edge[r : r + 1] = turned[0:1]
        last_edge[r : r + 1] = turned[slab - 1 : slab]


def finish_filter_kernel(mine, partial, low, high, energy, *blocks):
    shots, rows, cols, slab = partial.shape
    owners = len(blocks)
    own = rows // owners
    depth = lax.broadcasted_iota(jnp.int32, (slab, shots * own * cols), 0)
    totals = [jnp.zeros((cols, slab), jnp.float32) for _ in range(shots)]
    for k in range(owners):
        r = mine[0] ^ k
        halo = jnp.where(depth == 0, low[pl.ds(r, 1)], jnp.where(depth == slab - 1, high[pl.ds(r, 1)], 0.0)).T
        for s in range(shots):
            for j in range(own):
                at = (s * own + j) * cols
                value = partial[s, r * own + j] - halo[at : at + cols]
                blocks[k][s, j] = value
                totals[s] += value * value
    for s in range(shots):
        summed = jnp.sum(totals[s], axis=0, keepdims=True)
        energy[:, s : s + 1, :] = jnp.broadcast_to(summed[None], (energy.shape[0], 1, slab))


def combine_kernel(cells, total_shots, mine, energy, stack, weights, *blocks):
    owners = len(blocks)
    shots, own, cols, slab = blocks[0].shape
    slabs = energy.shape[0] // owners
    sums = []
    for g in range(owners):
        part = energy[g * slabs]
        for d in range(1, slabs):
            part = part + energy[g * slabs + d]
        sums.append(part)
    meansq = jnp.sum(jnp.concatenate(sums, axis=0), axis=1, keepdims=True) / cells
    peak = jnp.max(meansq, axis=0, keepdims=True)
    weight = (1.0 / math.sqrt(total_shots)) / jnp.sqrt(meansq + 0.5 * peak + 1.0)
    weights[...] = jnp.broadcast_to(weight, (owners * shots, slab))
    for j in range(own):
        acc = jnp.zeros((cols, slab), jnp.float32)
        for k in range(owners):
            for s in range(shots):
                acc += weights[pl.ds((mine[0] ^ k) * shots + s, 1)] * blocks[k][s, j]
        stack[j] = acc


def in_hbm(array):
    return pltpu.with_memory_space_constraint(array, pltpu.HBM)


def in_vmem(array):
    return pltpu.with_memory_space_constraint(array, pltpu.VMEM)


def on_device(correlation, illumination, aperture):
    shots, rows, cols, slab = correlation.shape
    owners, slabs = lax.axis_size("shot"), lax.axis_size("depth")
    assert owners & (owners - 1) == 0 and rows % owners == 0
    own = rows // owners
    f32 = jnp.float32
    vmem = pl.BlockSpec(memory_space=pltpu.VMEM)
    hbm = pl.BlockSpec(memory_space=pltpu.HBM)
    smem = pl.BlockSpec(memory_space=pltpu.SMEM)
    params = pltpu.CompilerParams(vmem_limit_bytes=16 << 20)
    edge = pltpu.VMEM((owners, shots * own * cols), f32)
    mine = lax.axis_index("shot").reshape(1)
    partial, first_edge, last_edge = pl.pallas_call(
        local_filter_kernel,
        out_shape=(pltpu.VMEM(correlation.shape, f32), edge, edge),
        in_specs=[smem, hbm, hbm],
        out_specs=(vmem, vmem, vmem),
        scratch_shapes=[
            pltpu.VMEM((shots, rows + 2, cols, slab), f32),
            pltpu.VMEM(correlation.shape, f32),
            pltpu.VMEM(correlation.shape, f32),
            pltpu.SemaphoreType.DMA((2, shots)),
        ],
        compiler_params=params,
        name="local_filter",
    )(aperture, in_hbm(correlation), in_hbm(illumination))
    forward = [(i, i + 1) for i in range(slabs - 1)]
    low = lax.ppermute(last_edge, "depth", forward)
    high = lax.ppermute(first_edge, "depth", [(b, a) for a, b in forward])
    energy, *blocks = pl.pallas_call(
        finish_filter_kernel,
        out_shape=(pltpu.VMEM((owners * slabs, shots, slab), f32),)
        + (pltpu.VMEM((shots, own, cols, slab), f32),) * owners,
        in_specs=[smem, vmem, vmem, vmem],
        out_specs=(vmem,) * (1 + owners),
        compiler_params=params,
        name="finish_filter",
    )(mine, *(in_vmem(v) for v in (partial, low, high)))
    energy = lax.all_to_all(energy, ("shot", "depth"), 0, 0, tiled=True)
    for k in range(1, owners):
        blocks[k] = lax.ppermute(blocks[k], "shot", [(i, i ^ k) for i in range(owners)])
    cells = rows * cols * slab * slabs

    def body(mine, energy, *refs):
        combine_kernel(cells, shots * owners, mine, energy, refs[owners], refs[owners + 1], *refs[:owners])

    return pl.pallas_call(
        body,
        out_shape=jax.ShapeDtypeStruct((own, cols, slab), f32),
        in_specs=[smem] + [vmem] * (1 + owners),
        out_specs=vmem,
        scratch_shapes=[pltpu.VMEM((owners * shots, slab), f32)],
        compiler_params=params,
        name="combine",
    )(mine, *(in_vmem(v) for v in (energy, *blocks)))


def solution(mesh):
    return jax.shard_map(
        on_device,
        mesh=mesh,
        in_specs=(P("shot", None, None, "depth"), P("shot", None, None, "depth"), P("shot", None)),
        out_specs=P("shot", None, "depth"),
        check_vma=False,
    )
```

time: 48.5 us -> 36.6 us (0.75)
  blocking collectives: 33.4 us -> 13.7 us
  starting transfers between devices: 3.68 us -> 14.9 us
  Pallas kernels: 6.37 us -> 3.2 us
    all_to_all x1 -> x0, blocking collectives: 19.2 us -> none  [on_device(): filtered = lax.all_to_all(filtered, 'shot', 0, 0, tiled=True)]
    ppermute x0 -> x7, starting transfers between devices: none -> 11.2 us  [on_device(): lax.ppermute(blocks[k], 'shot', [(i, i ^ k) for i in range(owners)])]
    pallas_call x2, Pallas kernels: 4.54 us -> 2.42 us  [the longest x1 2.2 us: on_device(): pl.pallas_call(local_filter_kernel, out_shape=(pltpu.VMEM(correlation.sha...]
    pallas_call x1, Pallas kernels: 1.82 us -> 0.77 us  [on_device(): pl.pallas_call(body, out_shape=jax.ShapeDtypeStruct((own, cols, slab), f3...]
    all_to_all x1, blocking collectives: 14.3 us -> 13.7 us  [on_device(): energy = lax.all_to_all(energy, ('shot', 'depth'), 0, 0, tiled=True)]
  transfers between devices with their start and end apart: 2 -> 9, of which waited for: 1 -> 1; matrix products, arithmetic and copies ran while one was open for 0% -> 0% of each run, Pallas kernels for 0% -> 0%
where the time goes in v2:
time: 36.6 us; the launch traced here: 36.4 us
  starting transfers between devices  14.9 us (41%)
  blocking collectives  13.7 us (37%)
  waiting for transfers between devices  3.86 us (11%)
  Pallas kernels  3.2 us (9%)
  local copies, waits for them, and re-layouts  0.68 us (2%)
    all_to_all x1, blocking collectives, on_device(): energy = lax.all_to_all(energy, ('shot', 'depth'), 0, 0, tiled=True)  13.7 us
    ppermute x7, starting transfers between devices, on_device(): lax.ppermute(blocks[k], 'shot', [(i, i ^ k) for i in range(owners)])  11.2 us
    ppermute x1, waiting for transfers between devices, on_device(): high = lax.ppermute(first_edge, 'depth', [(b, a) for a, b in forward])  3.84 us
    ppermute x1, starting transfers between devices, on_device(): low = lax.ppermute(last_edge, 'depth', forward)  2.4 us
    pallas_call x1, Pallas kernels, on_device(): pl.pallas_call(local_filter_kernel, out_shape=(pltpu.VMEM(correlation.sha...  2.2 us
    ppermute x1, starting transfers between devices, on_device(): high = lax.ppermute(first_edge, 'depth', [(b, a) for a, b in forward])  1.29 us
    pallas_call x1, Pallas kernels, on_device(): pl.pallas_call(body, out_shape=jax.ShapeDtypeStruct((own, cols, slab), f3...  0.77 us
  transfers between devices with their start and end apart: 9, of which 1 were waited for; matrix products, arithmetic and copies ran while one was open for 0% of the time, Pallas kernels for 0%

profile of v2, /device:TPU:0, one launch (start us, length us, event | category | flops | bytes accessed | tf_op | source)
XLA Modules:
  0.0 36.4 jit_solution(12029524646105698099)
XLA Ops:
  0.0 0.0 copy-start
  0.0 0.7 %copy-done = s32[2,4]{1,0:T(2,128)S(1)} copy-done((s32[2,4]{1,0:T(2,128)S(1)}, s32[2,4]{1,0:T(2,128)}, u32[]{:S(2)}) %copy-start) | copy-done | bytes 56
  0.7 2.2 %local_filter.1 = (f32[2,16,32,128]{3,2,1,0:T(8,128)S(1)}, f32[8,128]{1,0:T(8,128)S(1)}, f32[8,128]{1,0:T(8,128)S(1)}) custom-call(s32[2,4]{1,0:T(2,128)S(1)} %copy-done, f32[2,16,32,128]{3,2,1,0:T(8,128)} %correlation_hbm.1, f32[2,16,32,128]{3,2,1,0:T(8,128)} %illumination_hbm.1), custom_call_target="tpu_custom_call" | custom-call | tf_op jit(solution)/shard_map/local_filter/pallas_call | solution.py:114
  2.9 2.4 %collective-permute-start = (f32[8,128]{1,0:T(8,128)S(1)}, f32[8,128]{1,0:T(8,128)S(1)}, u32[]{:S(2)}, u32[]{:S(2)}) collective-permute-start(f32[8,128]{1,0:T(8,128)S(1)} %get-tuple-element.18), channel_id=1, source_target_pairs={{0,1},{1,2},{2,3},{4,5},{5,6},{6,7},{8,9},{9,10},{10,11},{12,13},{... | collective-permute-start | bytes 12296 | tf_op jit(solution)/shard_map/ppermute | solution.py:129
  5.3 1.3 %collective-permute-start.1 = (f32[8,128]{1,0:T(8,128)S(1)}, f32[8,128]{1,0:T(8,128)S(1)}, u32[]{:S(2)}, u32[]{:S(2)}) collective-permute-start(f32[8,128]{1,0:T(8,128)S(1)} %get-tuple-element.19), channel_id=1, source_target_pairs={{1,0},{2,1},{3,2},{5,4},{6,5},{7,6},{9,8},{10,9},{11,10},{13,12},{... | collective-permute-start | bytes 12296 | tf_op jit(solution)/shard_map/ppermute | solution.py:130
  6.6 0.0 collective-permute-done.low
  6.6 3.8 %collective-permute-done.1.high = f32[8,128]{1,0:T(8,128)S(1)} collective-permute-done((f32[8,128]{1,0:T(8,128)S(1)}, f32[8,128]{1,0:T(8,128)S(1)}, u32[]{:S(2)}, u32[]{:S(2)}) %collective-permute-start.1) | collective-permute-done | bytes 4128 | tf_op jit(solution)/shard_map/ppermute | solution.py:130
  10.5 0.2 finish_filter.1
  10.7 1.6 %collective-permute-start.2 = (f32[2,2,32,128]{3,2,1,0:T(8,128)S(1)}, f32[2,2,32,128]{3,2,1,0:T(8,128)S(1)}, u32[]{:S(2)}, u32[]{:S(2)}) collective-permute-start(f32[2,2,32,128]{3,2,1,0:T(8,128)S(1)} %get-tuple-element.22), channel_id=1, source_target_pairs={{0,4},{4,0},{8,12},{12,8},{16,20},{20,16},{24,28},{28,24},{1,5},{5... | collective-permute-start | bytes 196616 | tf_op jit(solution)/shard_map/ppermute | solution.py:142
  12.3 1.6 %collective-permute-start.3 = (f32[2,2,32,128]{3,2,1,0:T(8,128)S(1)}, f32[2,2,32,128]{3,2,1,0:T(8,128)S(1)}, u32[]{:S(2)}, u32[]{:S(2)}) collective-permute-start(f32[2,2,32,128]{3,2,1,0:T(8,128)S(1)} %get-tuple-element.23), channel_id=1, source_target_pairs={{0,8},{4,12},{8,0},{12,4},{16,24},{20,28},{24,16},{28,20},{1,9},{5... | collective-permute-start | bytes 196616 | tf_op jit(solution)/shard_map/ppermute | solution.py:142
  13.8 0.4 %collective-permute-start.4 = (f32[2,2,32,128]{3,2,1,0:T(8,128)S(1)}, f32[2,2,32,128]{3,2,1,0:T(8,128)S(1)}, u32[]{:S(2)}, u32[]{:S(2)}) collective-permute-start(f32[2,2,32,128]{3,2,1,0:T(8,128)S(1)} %get-tuple-element.24), channel_id=1, source_target_pairs={{0,12},{4,8},{8,4},{12,0},{16,28},{20,24},{24,20},{28,16},{1,13},{... | collective-permute-start | bytes 196616 | tf_op jit(solution)/shard_map/ppermute | solution.py:142
  14.2 2.6 %collective-permute-start.5 = (f32[2,2,32,128]{3,2,1,0:T(8,128)S(1)}, f32[2,2,32,128]{3,2,1,0:T(8,128)S(1)}, u32[]{:S(2)}, u32[]{:S(2)}) collective-permute-start(f32[2,2,32,128]{3,2,1,0:T(8,128)S(1)} %get-tuple-element.25), channel_id=1, source_target_pairs={{0,16},{4,20},{8,24},{12,28},{16,0},{20,4},{24,8},{28,12},{1,17},{... | collective-permute-start | bytes 196616 | tf_op jit(solution)/shard_map/ppermute | solution.py:142
  16.8 1.3 %collective-permute-start.6 = (f32[2,2,32,128]{3,2,1,0:T(8,128)S(1)}, f32[2,2,32,128]{3,2,1,0:T(8,128)S(1)}, u32[]{:S(2)}, u32[]{:S(2)}) collective-permute-start(f32[2,2,32,128]{3,2,1,0:T(8,128)S(1)} %get-tuple-element.26), channel_id=1, source_target_pairs={{0,20},{4,16},{8,28},{12,24},{16,4},{20,0},{24,12},{28,8},{1,21},{... | collective-permute-start | bytes 196616 | tf_op jit(solution)/shard_map/ppermute | solution.py:142
  18.1 0.0 collective-permute-done.2.refs_1_
  18.1 3.6 %collective-permute-start.7 = (f32[2,2,32,128]{3,2,1,0:T(8,128)S(1)}, f32[2,2,32,128]{3,2,1,0:T(8,128)S(1)}, u32[]{:S(2)}, u32[]{:S(2)}) collective-permute-start(f32[2,2,32,128]{3,2,1,0:T(8,128)S(1)} %get-tuple-element.27), channel_id=1, source_target_pairs={{0,24},{4,28},{8,16},{12,20},{16,8},{20,12},{24,0},{28,4},{1,25},{... | collective-permute-start | bytes 196616 | tf_op jit(solution)/shard_map/ppermute | solution.py:142
  21.7 0.0 collective-permute-done.3.refs_2_
  21.7 0.2 collective-permute-start.8
  21.9 13.7 %all_to_all.5.energy = f32[32,2,128]{2,1,0:T(2,128)S(1)} all-to-all(f32[32,2,128]{2,1,0:T(2,128)S(1)} %get-tuple-element.20), channel_id=1, replica_groups=mesh['shot'=8,'depth'=4] {'shot','depth'}, dimensions={0} | all-to-all | bytes 65536 | tf_op jit(solution)/shard_map/all_to_all | solution.py:140
  35.6 0.0 collective-permute-done.4.refs_3_
  35.6 0.0 collective-permute-done.5.refs_4_
  35.6 0.0 collective-permute-done.6.refs_5_
  35.6 0.0 collective-permute-done.7.refs_6_
  35.6 0.0 collective-permute-done.8.refs_7_
  35.6 0.8 %combine.1 = f32[2,32,128]{2,1,0:T(8,128)} custom-call(s32[1]{0:T(128)} %bitcast.mine, f32[32,2,128]{2,1,0:T(2,128)S(1)} %all_to_all.5.energy, f32[2,2,32,128]{3,2,1,0:T(8,128)S(1)} %get-tuple-element.21.refs_0_, f32[2,2,32,128]{3,2,1,0:T(8,128)S(1)} %collective-permute-done.2.refs_1_, f32[2,2,32,128]{3,2,1,0:T(8,128)S(1)} %collective-permute-done.3.refs_2_, ...), custom_call_target="tpu_custom_call" | custom-call | tf_op jit(solution)/shard_map/combine/pallas_call | solution.py:148
Async XLA Ops:
  0.0 0.7 %copy-start = (s32[2,4]{1,0:T(2,128)S(1)}, s32[2,4]{1,0:T(2,128)}, u32[]{:S(2)}) copy-start(s32[2,4]{1,0:T(2,128)} %aperture.1) | copy-start | bytes 100
  2.9 3.7 %collective-permute-start = (f32[8,128]{1,0:T(8,128)S(1)}, f32[8,128]{1,0:T(8,128)S(1)}, u32[]{:S(2)}, u32[]{:S(2)}) collective-permute-start(f32[8,128]{1,0:T(8,128)S(1)} %get-tuple-element.18), channel_id=1, source_target_pairs={{0,1},{1,2},{2,3},{4,5},{5,6},{6,7},{8,9},{9,10},{10,11},{12,13},{... | collective-permute-start | bytes 12296 | tf_op jit(solution)/shard_map/ppermute | solution.py:129
  5.3 5.2 %collective-permute-start.1 = (f32[8,128]{1,0:T(8,128)S(1)}, f32[8,128]{1,0:T(8,128)S(1)}, u32[]{:S(2)}, u32[]{:S(2)}) collective-permute-start(f32[8,128]{1,0:T(8,128)S(1)} %get-tuple-element.19), channel_id=1, source_target_pairs={{1,0},{2,1},{3,2},{5,4},{6,5},{7,6},{9,8},{10,9},{11,10},{13,12},{... | collective-permute-start | bytes 12296 | tf_op jit(solution)/shard_map/ppermute | solution.py:130
  10.7 7.4 %collective-permute-start.2 = (f32[2,2,32,128]{3,2,1,0:T(8,128)S(1)}, f32[2,2,32,128]{3,2,1,0:T(8,128)S(1)}, u32[]{:S(2)}, u32[]{:S(2)}) collective-permute-start(f32[2,2,32,128]{3,2,1,0:T(8,128)S(1)} %get-tuple-element.22), channel_id=1, source_target_pairs={{0,4},{4,0},{8,12},{12,8},{16,20},{20,16},{24,28},{28,24},{1,5},{5... | collective-permute-start | bytes 196616 | tf_op jit(solution)/shard_map/ppermute | solution.py:142
  12.3 9.5 %collective-permute-start.3 = (f32[2,2,32,128]{3,2,1,0:T(8,128)S(1)}, f32[2,2,32,128]{3,2,1,0:T(8,128)S(1)}, u32[]{:S(2)}, u32[]{:S(2)}) collective-permute-start(f32[2,2,32,128]{3,2,1,0:T(8,128)S(1)} %get-tuple-element.23), channel_id=1, source_target_pairs={{0,8},{4,12},{8,0},{12,4},{16,24},{20,28},{24,16},{28,20},{1,9},{5... | collective-permute-start | bytes 196616 | tf_op jit(solution)/shard_map/ppermute | solution.py:142
  13.8 21.8 %collective-permute-start.4 = (f32[2,2,32,128]{3,2,1,0:T(8,128)S(1)}, f32[2,2,32,128]{3,2,1,0:T(8,128)S(1)}, u32[]{:S(2)}, u32[]{:S(2)}) collective-permute-start(f32[2,2,32,128]{3,2,1,0:T(8,128)S(1)} %get-tuple-element.24), channel_id=1, source_target_pairs={{0,12},{4,8},{8,4},{12,0},{16,28},{20,24},{24,20},{28,16},{1,13},{... | collective-permute-start | bytes 196616 | tf_op jit(solution)/shard_map/ppermute | solution.py:142
  14.2 21.4 %collective-permute-start.5 = (f32[2,2,32,128]{3,2,1,0:T(8,128)S(1)}, f32[2,2,32,128]{3,2,1,0:T(8,128)S(1)}, u32[]{:S(2)}, u32[]{:S(2)}) collective-permute-start(f32[2,2,32,128]{3,2,1,0:T(8,128)S(1)} %get-tuple-element.25), channel_id=1, source_target_pairs={{0,16},{4,20},{8,24},{12,28},{16,0},{20,4},{24,8},{28,12},{1,17},{... | collective-permute-start | bytes 196616 | tf_op jit(solution)/shard_map/ppermute | solution.py:142
  16.8 18.8 %collective-permute-start.6 = (f32[2,2,32,128]{3,2,1,0:T(8,128)S(1)}, f32[2,2,32,128]{3,2,1,0:T(8,128)S(1)}, u32[]{:S(2)}, u32[]{:S(2)}) collective-permute-start(f32[2,2,32,128]{3,2,1,0:T(8,128)S(1)} %get-tuple-element.26), channel_id=1, source_target_pairs={{0,20},{4,16},{8,28},{12,24},{16,4},{20,0},{24,12},{28,8},{1,21},{... | collective-permute-start | bytes 196616 | tf_op jit(solution)/shard_map/ppermute | solution.py:142
  18.1 17.5 %collective-permute-start.7 = (f32[2,2,32,128]{3,2,1,0:T(8,128)S(1)}, f32[2,2,32,128]{3,2,1,0:T(8,128)S(1)}, u32[]{:S(2)}, u32[]{:S(2)}) collective-permute-start(f32[2,2,32,128]{3,2,1,0:T(8,128)S(1)} %get-tuple-element.27), channel_id=1, source_target_pairs={{0,24},{4,28},{8,16},{12,20},{16,8},{20,12},{24,0},{28,4},{1,25},{... | collective-permute-start | bytes 196616 | tf_op jit(solution)/shard_map/ppermute | solution.py:142
  21.7 13.9 %collective-permute-start.8 = (f32[2,2,32,128]{3,2,1,0:T(8,128)S(1)}, f32[2,2,32,128]{3,2,1,0:T(8,128)S(1)}, u32[]{:S(2)}, u32[]{:S(2)}) collective-permute-start(f32[2,2,32,128]{3,2,1,0:T(8,128)S(1)} %get-tuple-element.28), channel_id=1, source_target_pairs={{0,28},{4,24},{8,20},{12,16},{16,12},{20,8},{24,4},{28,0},{1,29},{... | collective-permute-start | bytes 196616 | tf_op jit(solution)/shard_map/ppermute | solution.py:142

commit v3 on v2

v3 whole, which is shorter than its diff:
```python
import math

import jax
import jax.numpy as jnp
from jax import lax
from jax.experimental import pallas as pl
from jax.experimental.pallas import tpu as pltpu
from jax.sharding import PartitionSpec as P


def local_filter_kernel(
    aperture_hbm, correlation_hbm, illumination_hbm, partial, message, padded, correlation, illumination, aperture, arrived, read
):
    shots, rows, cols, slab = correlation.shape
    own = message.shape[1] // (shots * cols)
    owners = rows // own
    boxes = pltpu.make_async_copy(aperture_hbm, aperture, read)
    boxes.start()
    copies = []
    for s in range(shots):
        copies.append((
            pltpu.make_async_copy(correlation_hbm.at[s], correlation.at[s], arrived.at[0, s]),
            pltpu.make_async_copy(illumination_hbm.at[s], illumination.at[s], arrived.at[1, s]),
        ))
        for copy in copies[s]:
            copy.start()
    second = lax.broadcasted_iota(jnp.int32, (cols, slab), 0)
    lane = lax.broadcasted_iota(jnp.int32, (cols, slab), 1)
    zero = jnp.zeros((cols, slab), jnp.float32)
    boxes.wait()
    for s in range(shots):
        padded[s, 0] = zero
        padded[s, rows + 1] = zero
        for copy in copies[s]:
            copy.wait()
        in_cols = (second >= aperture[s, 2]) & (second < aperture[s, 3])
        for x in range(rows):
            keep = in_cols & (x >= aperture[s, 0]) & (x < aperture[s, 1])
            padded[s, x + 1] = jnp.where(keep, correlation[s, x] / (illumination[s, x] + 0.1), 0.0)
        total = zero
        for x in range(rows):
            n = padded[s, x + 1]
            beside = padded[s, x] + padded[s, x + 2]
            beside += jnp.where(second == 0, 0.0, pltpu.roll(n, 1, 0))
            beside += jnp.where(second == cols - 1, 0.0, pltpu.roll(n, cols - 1, 0))
            beside += jnp.where(lane == 0, 0.0, pltpu.roll(n, 1, 1))
            beside += jnp.where(lane == slab - 1, 0.0, pltpu.roll(n, slab - 1, 1))
            value = 6.0 * n - beside
            partial[s, x] = value
            total += value * value
        message[4 * owners + s : 4 * owners + s + 1] = jnp.sum(total, axis=0, keepdims=True)
    for r in range(owners):
        for at, image, shift in ((0, padded, 1), (2 * owners, partial, 0)):
            held = [image[s, r * own + j + shift] for s in range(shots) for j in range(own)]
            turned = jnp.concatenate(held, axis=0).T
            message[at + r : at + r + 1] = turned[0:1]
            message[at + owners + r : at + owners + r + 1] = turned[slab - 1 : slab]


def finish_filter_kernel(aperture, place, partial, messages, blocks, slabs_held, filtered):
    shots, rows, cols, slab = partial.shape
    owners, slabs = len(blocks), len(messages)
    own = rows // owners
    window = cols // 2 + 2
    width = shots * own * cols
    here = place[1]
    for k in range(slabs):
        slabs_held[here ^ k] = messages[k][...]
    cross = jnp.zeros((owners, width), jnp.float32)
    for d in range(slabs - 1):
        right = slabs_held[d + 1, 0:owners]
        left = slabs_held[d, owners : 2 * owners]
        cross += right * (right - 2.0 * slabs_held[d, 3 * owners : 4 * owners])
        cross += left * (left - 2.0 * slabs_held[d + 1, 2 * owners : 3 * owners])
    cross = jnp.sum(cross, axis=0, keepdims=True)
    lane = lax.broadcasted_iota(jnp.int32, (1, width), 1)
    tails = []
    starts = []
    for s in range(shots):
        energy = jnp.where((lane >= s * own * cols) & (lane < (s + 1) * own * cols), cross, 0.0)
        for d in range(slabs):
            energy += slabs_held[d, 4 * owners + s : 4 * owners + s + 1]
        tails.append(energy)
    for s in range(shots):
        starts.append(jnp.clip(aperture[s, 2] - 1, 0, cols - window))
        tails.append(jnp.full((1, width), starts[s].astype(jnp.float32)))
    tail = jnp.concatenate(tails, axis=0)
    depth = lax.broadcasted_iota(jnp.int32, (slab, width), 0)
    below = jnp.maximum(here - 1, 0)
    above = jnp.minimum(here + 1, slabs - 1)
    has_below = (depth == 0) & (here > 0)
    has_above = (depth == slab - 1) & (here < slabs - 1)
    for k in range(owners):
        r = place[0] ^ k
        low = slabs_held[below, pl.ds(owners + r, 1)]
        high = slabs_held[above, pl.ds(r, 1)]
        halo = jnp.where(has_below, low, jnp.where(has_above, high, 0.0)).T
        for s in range(shots):
            for j in range(own):
                i = s * own + j
                filtered[k, i] = partial[s, r * own + j] - halo[i * cols : (i + 1) * cols]
                blocks[k][i * window : (i + 1) * window] = filtered[k, i, pl.ds(starts[s], window)]
        blocks[k][shots * own * window :] = tail


def combine_kernel(cells, total_shots, shots, blocks, stack, weights):
    owners = len(blocks)
    own, cols, slab = stack.shape
    window = cols // 2 + 2
    tail = shots * own * window
    energy = jnp.concatenate([block[tail : tail + shots] for block in blocks], axis=0)
    meansq = jnp.sum(energy, axis=1, keepdims=True) / cells
    peak = jnp.max(meansq, axis=0, keepdims=True)
    weight = (1.0 / math.sqrt(total_shots)) / jnp.sqrt(meansq + 0.5 * peak + 1.0)
    weights[...] = jnp.broadcast_to(weight, (owners * shots, slab))
    stack[...] = jnp.zeros(stack.shape, jnp.float32)
    for k in range(owners):
        for s in range(shots):
            start = jnp.max(blocks[k][tail + shots + s : tail + shots + s + 1]).astype(jnp.int32)
            scale = weights[k * shots + s : k * shots + s + 1]
            for j in range(own):
                i = s * own + j
                stack[j, pl.ds(start, window)] += scale * blocks[k][i * window : (i + 1) * window]


def in_hbm(array):
    return pltpu.with_memory_space_constraint(array, pltpu.HBM)


def in_vmem(array):
    return pltpu.with_memory_space_constraint(array, pltpu.VMEM)


def on_device(correlation, illumination, aperture):
    shots, rows, cols, slab = correlation.shape
    owners, slabs = lax.axis_size("shot"), lax.axis_size("depth")
    assert owners & (owners - 1) == 0 and slabs & (slabs - 1) == 0 and rows % owners == 0
    own = rows // owners
    width = shots * own * cols
    assert width == slab == 128
    f32 = jnp.float32
    vmem = pl.BlockSpec(memory_space=pltpu.VMEM)
    hbm = pl.BlockSpec(memory_space=pltpu.HBM)
    smem = pl.BlockSpec(memory_space=pltpu.SMEM)
    params = pltpu.CompilerParams(vmem_limit_bytes=24 << 20)
    partial, message = pl.pallas_call(
        local_filter_kernel,
        out_shape=(pltpu.VMEM(correlation.shape, f32), pltpu.VMEM((4 * owners + shots, width), f32)),
        in_specs=[hbm, hbm, hbm],
        out_specs=(vmem, vmem),
        scratch_shapes=[
            pltpu.VMEM((shots, rows + 2, cols, slab), f32),
            pltpu.VMEM(correlation.shape, f32),
            pltpu.VMEM(correlation.shape, f32),
            pltpu.SMEM(aperture.shape, aperture.dtype),
            pltpu.SemaphoreType.DMA((2, shots)),
            pltpu.SemaphoreType.DMA,
        ],
        compiler_params=params,
        name="local_filter",
    )(in_hbm(aperture), in_hbm(correlation), in_hbm(illumination))
    messages = [message]
    for k in range(1, slabs):
        messages.append(lax.ppermute(message, "depth", [(i, i ^ k) for i in range(slabs)]))
    place = jnp.stack([lax.axis_index("shot"), lax.axis_index("depth")])

    def finish_body(aperture, place, partial, *refs):
        finish_filter_kernel(aperture, place, partial, refs[:slabs], refs[slabs : slabs + owners], *refs[slabs + owners :])

    block = pltpu.VMEM((shots * own * (cols // 2 + 2) + 2 * shots, slab), f32)
    blocks = list(pl.pallas_call(
        finish_body,
        out_shape=(block,) * owners,
        in_specs=[smem, smem] + [vmem] * (1 + slabs),
        out_specs=(vmem,) * owners,
        scratch_shapes=[
            pltpu.VMEM((slabs,) + message.shape, f32),
            pltpu.VMEM((owners, shots * own, cols, slab), f32),
        ],
        compiler_params=params,
        name="finish_filter",
    )(aperture, place, *(in_vmem(v) for v in (partial, *messages))))
    for k in range(1, owners):
        blocks[k] = lax.ppermute(blocks[k], "shot", [(i, i ^ k) for i in range(owners)])
    cells = rows * cols * slab * slabs

    def combine_body(*refs):
        combine_kernel(cells, shots * owners, shots, refs[:owners], *refs[owners:])

    return pl.pallas_call(
        combine_body,
        out_shape=jax.ShapeDtypeStruct((own, cols, slab), f32),
        in_specs=[vmem] * owners,
        out_specs=vmem,
        scratch_shapes=[pltpu.VMEM((owners * shots, slab), f32)],
        compiler_params=params,
        name="combine",
    )(*(in_vmem(v) for v in blocks))


def solution(mesh):
    return jax.shard_map(
        on_device,
        mesh=mesh,
        in_specs=(P("shot", None, None, "depth"), P("shot", None, None, "depth"), P("shot", None)),
        out_specs=P("shot", None, "depth"),
        check_vma=False,
    )
```

time: 36.6 us -> 27.7 us (0.76)
  blocking collectives: 13.7 us -> 0 us
  waiting for transfers between devices: 3.86 us -> 9.57 us
  local copies, waits for them, and re-layouts: 0.68 us -> 0.01 us
  starting transfers between devices: 14.9 us -> 14.3 us
    all_to_all x1 -> x0, blocking collectives: 13.7 us -> none  [on_device(): energy = lax.all_to_all(energy, ('shot', 'depth'), 0, 0, tiled=True)]
    ppermute x7, waiting for transfers between devices: 0.02 us -> 6.54 us  [on_device(): lax.ppermute(blocks[k], 'shot', [(i, i ^ k) for i in range(owners)])]
    ppermute x2 -> x3, waiting for transfers between devices: 3.84 us -> 3.03 us  [on_device(): lax.ppermute(message, 'depth', [(i, i ^ k) for i in range(slabs)])]
    pallas_call x2, Pallas kernels: 0.99 us -> 1.72 us  [the longest x1 0.87 us: on_device(): pl.pallas_call(finish_body, out_shape=(block,) * owners, in_specs=[smem,...]
    unnamed x2, local copies, waits for them, and re-layouts: 0.68 us -> 0.01 us
    ppermute x2 -> x3, starting transfers between devices: 3.69 us -> 3.15 us  [on_device(): lax.ppermute(message, 'depth', [(i, i ^ k) for i in range(slabs)])]
    pallas_call x1, Pallas kernels: 2.2 us -> 1.8 us  [on_device(): pl.pallas_call(local_filter_kernel, out_shape=(pltpu.VMEM(correlation.sha...]
  transfers between devices with their start and end apart: 9 -> 10, of which waited for: 1 -> 5; matrix products, arithmetic and copies ran while one was open for 0% -> 0% of each run, Pallas kernels for 0% -> 0%
where the time goes in v3:
time: 27.7 us; the launch traced here: 27.5 us
  starting transfers between devices  14.3 us (52%)
  waiting for transfers between devices  9.57 us (35%)
  Pallas kernels  3.52 us (13%)
    ppermute x7, starting transfers between devices, on_device(): lax.ppermute(blocks[k], 'shot', [(i, i ^ k) for i in range(owners)])  11.2 us
    ppermute x7, waiting for transfers between devices, on_device(): lax.ppermute(blocks[k], 'shot', [(i, i ^ k) for i in range(owners)])  6.54 us
    ppermute x3, starting transfers between devices, on_device(): lax.ppermute(message, 'depth', [(i, i ^ k) for i in range(slabs)])  3.15 us
    ppermute x3, waiting for transfers between devices, on_device(): lax.ppermute(message, 'depth', [(i, i ^ k) for i in range(slabs)])  3.03 us
    pallas_call x1, Pallas kernels, on_device(): pl.pallas_call(local_filter_kernel, out_shape=(pltpu.VMEM(correlation.sha...  1.8 us
    pallas_call x1, Pallas kernels, on_device(): pl.pallas_call(finish_body, out_shape=(block,) * owners, in_specs=[smem,...  0.87 us
    pallas_call x1, Pallas kernels, on_device(): pl.pallas_call(combine_body, out_shape=jax.ShapeDtypeStruct((own, cols, s...  0.85 us
  transfers between devices with their start and end apart: 10, of which 5 were waited for; matrix products, arithmetic and copies ran while one was open for 0% of the time, Pallas kernels for 0%

profile of v3, /device:TPU:0, one launch (start us, length us, event | category | flops | bytes accessed | tf_op | source)
XLA Modules:
  0.0 27.5 jit_solution(11627681423030626049)
XLA Ops:
  0.0 1.8 %local_filter.1 = (f32[2,16,32,128]{3,2,1,0:T(8,128)S(1)}, f32[34,128]{1,0:T(8,128)S(1)}) custom-call(s32[2,4]{1,0:T(2,128)} %aperture.1, f32[2,16,32,128]{3,2,1,0:T(8,128)} %correlation_hbm.1, f32[2,16,32,128]{3,2,1,0:T(8,128)} %illumination_hbm.1), custom_call_target="tpu_custom_call" | custom-call | tf_op jit(solution)/shard_map/local_filter/pallas_call | solution.py:146
  1.8 2.5 %collective-permute-start.2 = (f32[34,128]{1,0:T(8,128)S(1)}, f32[34,128]{1,0:T(8,128)S(1)}, u32[]{:S(2)}, u32[]{:S(2)}) collective-permute-start(f32[34,128]{1,0:T(8,128)S(1)} %get-tuple-element.16.refs_0_), channel_id=1, source_target_pairs={{0,3},{1,2},{2,1},{3,0},{4,7},{5,6},{6,5},{7,4},{8,11},{9,10},{10,... | collective-permute-start | bytes 52232 | tf_op jit(solution)/shard_map/ppermute | solution.py:164
  4.3 0.6 %collective-permute-start.1 = (f32[34,128]{1,0:T(8,128)S(1)}, f32[34,128]{1,0:T(8,128)S(1)}, u32[]{:S(2)}, u32[]{:S(2)}) collective-permute-start(f32[34,128]{1,0:T(8,128)S(1)} %get-tuple-element.16.refs_0_), channel_id=1, source_target_pairs={{0,2},{1,3},{2,0},{3,1},{4,6},{5,7},{6,4},{7,5},{8,10},{9,11},{10,... | collective-permute-start | bytes 52232 | tf_op jit(solution)/shard_map/ppermute | solution.py:164
  4.9 0.0 collective-permute-start
  5.0 0.1 pad_add_fusion.place
  5.0 0.0 copy-start
  5.0 0.8 %collective-permute-done.2.refs_3_ = f32[34,128]{1,0:T(8,128)S(1)} collective-permute-done((f32[34,128]{1,0:T(8,128)S(1)}, f32[34,128]{1,0:T(8,128)S(1)}, u32[]{:S(2)}, u32[]{:S(2)}) %collective-permute-start.2) | collective-permute-done | bytes 17440 | tf_op jit(solution)/shard_map/ppermute | solution.py:164
  5.8 2.3 %collective-permute-done.1.refs_2_ = f32[34,128]{1,0:T(8,128)S(1)} collective-permute-done((f32[34,128]{1,0:T(8,128)S(1)}, f32[34,128]{1,0:T(8,128)S(1)}, u32[]{:S(2)}, u32[]{:S(2)}) %collective-permute-start.1) | collective-permute-done | bytes 17440 | tf_op jit(solution)/shard_map/ppermute | solution.py:164
  8.1 0.0 collective-permute-done.refs_1_
  8.1 0.0 copy-done
  8.1 0.9 %finish_filter.1 = (f32[76,128]{1,0:T(8,128)S(1)}, f32[76,128]{1,0:T(8,128)S(1)}, f32[76,128]{1,0:T(8,128)S(1)}, f32[76,128]{1,0:T(8,128)S(1)}, f32[76,128]{1,0:...) custom-call(s32[2,4]{1,0:T(2,128)S(1)} %copy-done, s32[2]{0:T(128)S(1)} %pad_add_fusion.place, ...), custom_call_target="tpu_custom_call" | custom-call | tf_op jit(solution)/shard_map/finish_filter/pallas_call | solution.py:171
  8.9 1.6 %collective-permute-start.3 = (f32[76,128]{1,0:T(8,128)S(1)}, f32[76,128]{1,0:T(8,128)S(1)}, u32[]{:S(2)}, u32[]{:S(2)}) collective-permute-start(f32[76,128]{1,0:T(8,128)S(1)} %get-tuple-element.18), channel_id=1, source_target_pairs={{0,4},{4,0},{8,12},{12,8},{16,20},{20,16},{24,28},{28,24},{1,5},{5... | collective-permute-start | bytes 116744 | tf_op jit(solution)/shard_map/ppermute | solution.py:184
  10.5 1.6 %collective-permute-start.4 = (f32[76,128]{1,0:T(8,128)S(1)}, f32[76,128]{1,0:T(8,128)S(1)}, u32[]{:S(2)}, u32[]{:S(2)}) collective-permute-start(f32[76,128]{1,0:T(8,128)S(1)} %get-tuple-element.19), channel_id=1, source_target_pairs={{0,8},{4,12},{8,0},{12,4},{16,24},{20,28},{24,16},{28,20},{1,9},{5... | collective-permute-start | bytes 116744 | tf_op jit(solution)/shard_map/ppermute | solution.py:184
  12.1 0.4 %collective-permute-start.5 = (f32[76,128]{1,0:T(8,128)S(1)}, f32[76,128]{1,0:T(8,128)S(1)}, u32[]{:S(2)}, u32[]{:S(2)}) collective-permute-start(f32[76,128]{1,0:T(8,128)S(1)} %get-tuple-element.20), channel_id=1, source_target_pairs={{0,12},{4,8},{8,4},{12,0},{16,28},{20,24},{24,20},{28,16},{1,13},{... | collective-permute-start | bytes 116744 | tf_op jit(solution)/shard_map/ppermute | solution.py:184
  12.5 2.6 %collective-permute-start.6 = (f32[76,128]{1,0:T(8,128)S(1)}, f32[76,128]{1,0:T(8,128)S(1)}, u32[]{:S(2)}, u32[]{:S(2)}) collective-permute-start(f32[76,128]{1,0:T(8,128)S(1)} %get-tuple-element.21), channel_id=1, source_target_pairs={{0,16},{4,20},{8,24},{12,28},{16,0},{20,4},{24,8},{28,12},{1,17},{... | collective-permute-start | bytes 116744 | tf_op jit(solution)/shard_map/ppermute | solution.py:184
  15.1 1.3 %collective-permute-start.7 = (f32[76,128]{1,0:T(8,128)S(1)}, f32[76,128]{1,0:T(8,128)S(1)}, u32[]{:S(2)}, u32[]{:S(2)}) collective-permute-start(f32[76,128]{1,0:T(8,128)S(1)} %get-tuple-element.22), channel_id=1, source_target_pairs={{0,20},{4,16},{8,28},{12,24},{16,4},{20,0},{24,12},{28,8},{1,21},{... | collective-permute-start | bytes 116744 | tf_op jit(solution)/shard_map/ppermute | solution.py:184
  16.4 0.0 collective-permute-done.3.refs_1_
  16.4 3.6 %collective-permute-start.8 = (f32[76,128]{1,0:T(8,128)S(1)}, f32[76,128]{1,0:T(8,128)S(1)}, u32[]{:S(2)}, u32[]{:S(2)}) collective-permute-start(f32[76,128]{1,0:T(8,128)S(1)} %get-tuple-element.23), channel_id=1, source_target_pairs={{0,24},{4,28},{8,16},{12,20},{16,8},{20,12},{24,0},{28,4},{1,25},{... | collective-permute-start | bytes 116744 | tf_op jit(solution)/shard_map/ppermute | solution.py:184
  20.0 0.0 collective-permute-done.4.refs_2_
  20.0 0.2 collective-permute-start.9
  20.2 0.0 collective-permute-done.5.refs_3_
  20.2 0.0 collective-permute-done.6.refs_4_
  20.2 1.2 %collective-permute-done.7.refs_5_ = f32[76,128]{1,0:T(8,128)S(1)} collective-permute-done((f32[76,128]{1,0:T(8,128)S(1)}, f32[76,128]{1,0:T(8,128)S(1)}, u32[]{:S(2)}, u32[]{:S(2)}) %collective-permute-start.7) | collective-permute-done | bytes 38944 | tf_op jit(solution)/shard_map/ppermute | solution.py:184
  21.3 1.3 %collective-permute-done.8.refs_6_ = f32[76,128]{1,0:T(8,128)S(1)} collective-permute-done((f32[76,128]{1,0:T(8,128)S(1)}, f32[76,128]{1,0:T(8,128)S(1)}, u32[]{:S(2)}, u32[]{:S(2)}) %collective-permute-start.8) | collective-permute-done | bytes 38944 | tf_op jit(solution)/shard_map/ppermute | solution.py:184
  22.6 4.1 %collective-permute-done.9.refs_7_ = f32[76,128]{1,0:T(8,128)S(1)} collective-permute-done((f32[76,128]{1,0:T(8,128)S(1)}, f32[76,128]{1,0:T(8,128)S(1)}, u32[]{:S(2)}, u32[]{:S(2)}) %collective-permute-start.9) | collective-permute-done | bytes 38944 | tf_op jit(solution)/shard_map/ppermute | solution.py:184
  26.7 0.8 %combine.1 = f32[2,32,128]{2,1,0:T(8,128)} custom-call(f32[76,128]{1,0:T(8,128)S(1)} %get-tuple-element.17.refs_0_, f32[76,128]{1,0:T(8,128)S(1)} %collective-permute-done.3.refs_1_, f32[76,128]{1,0:T(8,128)S(1)} %collective-permute-done.4.refs_2_, f32[76,128]{1,0:T(8,128)S(1)} %collective-permute-done.5.refs_3_, ...), custom_call_target="tpu_custom_call" | custom-call | tf_op jit(solution)/shard_map/combine/pallas_call | solution.py:190
Async XLA Ops:
  1.8 4.0 %collective-permute-start.2 = (f32[34,128]{1,0:T(8,128)S(1)}, f32[34,128]{1,0:T(8,128)S(1)}, u32[]{:S(2)}, u32[]{:S(2)}) collective-permute-start(f32[34,128]{1,0:T(8,128)S(1)} %get-tuple-element.16.refs_0_), channel_id=1, source_target_pairs={{0,3},{1,2},{2,1},{3,0},{4,7},{5,6},{6,5},{7,4},{8,11},{9,10},{10,... | collective-permute-start | bytes 52232 | tf_op jit(solution)/shard_map/ppermute | solution.py:164
  4.3 3.8 %collective-permute-start.1 = (f32[34,128]{1,0:T(8,128)S(1)}, f32[34,128]{1,0:T(8,128)S(1)}, u32[]{:S(2)}, u32[]{:S(2)}) collective-permute-start(f32[34,128]{1,0:T(8,128)S(1)} %get-tuple-element.16.refs_0_), channel_id=1, source_target_pairs={{0,2},{1,3},{2,0},{3,1},{4,6},{5,7},{6,4},{7,5},{8,10},{9,11},{10,... | collective-permute-start | bytes 52232 | tf_op jit(solution)/shard_map/ppermute | solution.py:164
  4.9 3.1 %collective-permute-start = (f32[34,128]{1,0:T(8,128)S(1)}, f32[34,128]{1,0:T(8,128)S(1)}, u32[]{:S(2)}, u32[]{:S(2)}) collective-permute-start(f32[34,128]{1,0:T(8,128)S(1)} %get-tuple-element.16.refs_0_), channel_id=1, source_target_pairs={{0,1},{1,0},{2,3},{3,2},{4,5},{5,4},{6,7},{7,6},{8,9},{9,8},{10,11... | collective-permute-start | bytes 52232 | tf_op jit(solution)/shard_map/ppermute | solution.py:164
  5.0 3.0 %copy-start = (s32[2,4]{1,0:T(2,128)S(1)}, s32[2,4]{1,0:T(2,128)}, u32[]{:S(2)}) copy-start(s32[2,4]{1,0:T(2,128)} %aperture.1) | copy-start | bytes 100
  8.9 7.4 %collective-permute-start.3 = (f32[76,128]{1,0:T(8,128)S(1)}, f32[76,128]{1,0:T(8,128)S(1)}, u32[]{:S(2)}, u32[]{:S(2)}) collective-permute-start(f32[76,128]{1,0:T(8,128)S(1)} %get-tuple-element.18), channel_id=1, source_target_pairs={{0,4},{4,0},{8,12},{12,8},{16,20},{20,16},{24,28},{28,24},{1,5},{5... | collective-permute-start | bytes 116744 | tf_op jit(solution)/shard_map/ppermute | solution.py:184
  10.5 9.5 %collective-permute-start.4 = (f32[76,128]{1,0:T(8,128)S(1)}, f32[76,128]{1,0:T(8,128)S(1)}, u32[]{:S(2)}, u32[]{:S(2)}) collective-permute-start(f32[76,128]{1,0:T(8,128)S(1)} %get-tuple-element.19), channel_id=1, source_target_pairs={{0,8},{4,12},{8,0},{12,4},{16,24},{20,28},{24,16},{28,20},{1,9},{5... | collective-permute-start | bytes 116744 | tf_op jit(solution)/shard_map/ppermute | solution.py:184
  12.1 8.1 %collective-permute-start.5 = (f32[76,128]{1,0:T(8,128)S(1)}, f32[76,128]{1,0:T(8,128)S(1)}, u32[]{:S(2)}, u32[]{:S(2)}) collective-permute-start(f32[76,128]{1,0:T(8,128)S(1)} %get-tuple-element.20), channel_id=1, source_target_pairs={{0,12},{4,8},{8,4},{12,0},{16,28},{20,24},{24,20},{28,16},{1,13},{... | collective-permute-start | bytes 116744 | tf_op jit(solution)/shard_map/ppermute | solution.py:184
  12.5 7.7 %collective-permute-start.6 = (f32[76,128]{1,0:T(8,128)S(1)}, f32[76,128]{1,0:T(8,128)S(1)}, u32[]{:S(2)}, u32[]{:S(2)}) collective-permute-start(f32[76,128]{1,0:T(8,128)S(1)} %get-tuple-element.21), channel_id=1, source_target_pairs={{0,16},{4,20},{8,24},{12,28},{16,0},{20,4},{24,8},{28,12},{1,17},{... | collective-permute-start | bytes 116744 | tf_op jit(solution)/shard_map/ppermute | solution.py:184
  15.1 6.2 %collective-permute-start.7 = (f32[76,128]{1,0:T(8,128)S(1)}, f32[76,128]{1,0:T(8,128)S(1)}, u32[]{:S(2)}, u32[]{:S(2)}) collective-permute-start(f32[76,128]{1,0:T(8,128)S(1)} %get-tuple-element.22), channel_id=1, source_target_pairs={{0,20},{4,16},{8,28},{12,24},{16,4},{20,0},{24,12},{28,8},{1,21},{... | collective-permute-start | bytes 116744 | tf_op jit(solution)/shard_map/ppermute | solution.py:184
  16.4 6.2 %collective-permute-start.8 = (f32[76,128]{1,0:T(8,128)S(1)}, f32[76,128]{1,0:T(8,128)S(1)}, u32[]{:S(2)}, u32[]{:S(2)}) collective-permute-start(f32[76,128]{1,0:T(8,128)S(1)} %get-tuple-element.23), channel_id=1, source_target_pairs={{0,24},{4,28},{8,16},{12,20},{16,8},{20,12},{24,0},{28,4},{1,25},{... | collective-permute-start | bytes 116744 | tf_op jit(solution)/shard_map/ppermute | solution.py:184
  20.0 6.7 %collective-permute-start.9 = (f32[76,128]{1,0:T(8,128)S(1)}, f32[76,128]{1,0:T(8,128)S(1)}, u32[]{:S(2)}, u32[]{:S(2)}) collective-permute-start(f32[76,128]{1,0:T(8,128)S(1)} %get-tuple-element.24), channel_id=1, source_target_pairs={{0,28},{4,24},{8,20},{12,16},{16,12},{20,8},{24,4},{28,0},{1,29},{... | collective-permute-start | bytes 116744 | tf_op jit(solution)/shard_map/ppermute | solution.py:184

commit v4 on v3

--- a/solution.py
+++ b/solution.py
@@ -9,13 +9,16 @@
 
 
 def local_filter_kernel(
-    aperture_hbm, correlation_hbm, illumination_hbm, partial, message, padded, correlation, illumination, aperture, arrived, read
+    aperture_hbm, correlation_hbm, illumination_hbm, place_hbm, partial, message, handed,
+    padded, correlation, illumination, aperture, place, arrived, read,
 ):
     shots, rows, cols, slab = correlation.shape
     own = message.shape[1] // (shots * cols)
     owners = rows // own
-    boxes = pltpu.make_async_copy(aperture_hbm, aperture, read)
+    boxes = pltpu.make_async_copy(aperture_hbm, aperture, read.at[0])
     boxes.start()
+    where = pltpu.make_async_copy(place_hbm, place, read.at[1])
+    where.start()
     copies = []
     for s in range(shots):
         copies.append((
@@ -55,17 +58,33 @@
             turned = jnp.concatenate(held, axis=0).T
             message[at + r : at + r + 1] = turned[0:1]
             message[at + owners + r : at + owners + r + 1] = turned[slab - 1 : slab]
-
-
-def finish_filter_kernel(aperture, place, partial, messages, blocks, slabs_held, filtered):
+    edges = 4 * owners + shots
+    handed[0:edges] = message[...]
+    window = cols // 2 + 2
+    where.wait()
+    partner_first = (1 - place[1] % 2) * (owners // 2)
+    for k in range(owners // 2):
+        r = place[0] ^ (partner_first + k)
+        for s in range(shots):
+            for j in range(own):
+                at = edges + (k * shots * own + s * own + j) * window
+                handed[at : at + window] = partial[s, r * own + j, pl.ds(window_start(aperture, s, cols), window)]
+
+
+def window_start(aperture, s, cols):
+    return jnp.clip(aperture[s, 2] - 1, 0, cols // 2 - 2)
+
+
+def finish_filter_kernel(aperture, place, partial, handed, messages, blocks, slabs_held, halo):
     shots, rows, cols, slab = partial.shape
-    owners, slabs = len(blocks), len(messages)
-    own = rows // owners
+    slabs = len(messages)
+    edges, width = messages[0].shape
+    own = width // (shots * cols)
+    owners = rows // own
     window = cols // 2 + 2
-    width = shots * own * cols
     here = place[1]
     for k in range(slabs):
-        slabs_held[here ^ k] = messages[k][...]
+        slabs_held[here ^ k] = messages[k][...] if k != 1 else handed[0:edges]
     cross = jnp.zeros((owners, width), jnp.float32)
     for d in range(slabs - 1):
         right = slabs_held[d + 1, 0:owners]
@@ -74,33 +93,38 @@
         cross += left * (left - 2.0 * slabs_held[d + 1, 2 * owners : 3 * owners])
     cross = jnp.sum(cross, axis=0, keepdims=True)
     lane = lax.broadcasted_iota(jnp.int32, (1, width), 1)
+    starts = [window_start(aperture, s, cols) for s in range(shots)]
     tails = []
-    starts = []
     for s in range(shots):
         energy = jnp.where((lane >= s * own * cols) & (lane < (s + 1) * own * cols), cross, 0.0)
         for d in range(slabs):
             energy += slabs_held[d, 4 * owners + s : 4 * owners + s + 1]
         tails.append(energy)
-    for s in range(shots):
-        starts.append(jnp.clip(aperture[s, 2] - 1, 0, cols - window))
-        tails.append(jnp.full((1, width), starts[s].astype(jnp.float32)))
+    tails += [jnp.full((1, width), start.astype(jnp.float32)) for start in starts]
     tail = jnp.concatenate(tails, axis=0)
     depth = lax.broadcasted_iota(jnp.int32, (slab, width), 0)
-    below = jnp.maximum(here - 1, 0)
-    above = jnp.minimum(here + 1, slabs - 1)
-    has_below = (depth == 0) & (here > 0)
-    has_above = (depth == slab - 1) & (here < slabs - 1)
-    for k in range(owners):
-        r = place[0] ^ k
-        low = slabs_held[below, pl.ds(owners + r, 1)]
-        high = slabs_held[above, pl.ds(r, 1)]
-        halo = jnp.where(has_below, low, jnp.where(has_above, high, 0.0)).T
-        for s in range(shots):
-            for j in range(own):
-                i = s * own + j
-                filtered[k, i] = partial[s, r * own + j] - halo[i * cols : (i + 1) * cols]
-                blocks[k][i * window : (i + 1) * window] = filtered[k, i, pl.ds(starts[s], window)]
-        blocks[k][shots * own * window :] = tail
+    first = (here % 2) * (owners // 2)
+    for whose in range(2):
+        d = here ^ whose
+        below = jnp.maximum(d - 1, 0)
+        above = jnp.minimum(d + 1, slabs - 1)
+        has_below = (depth == 0) & (d > 0)
+        has_above = (depth == slab - 1) & (d < slabs - 1)
+        for k in range(owners // 2):
+            r = place[0] ^ (first + k)
+            low = slabs_held[below, pl.ds(owners + r, 1)]
+            high = slabs_held[above, pl.ds(r, 1)]
+            halo[whose, k] = jnp.where(has_below, low, jnp.where(has_above, high, 0.0)).T
+            for s in range(shots):
+                for j in range(own):
+                    i = s * own + j
+                    if whose:
+                        at = edges + (k * shots * own + i) * window
+                        value = handed[at : at + window]
+                    else:
+                        value = partial[s, r * own + j, pl.ds(starts[s], window)]
+                    blocks[k][whose, i * window : (i + 1) * window] = value - halo[whose, k, pl.ds(i * cols + starts[s], window)]
+            blocks[k][whose, shots * own * window :] = tail
 
 
 def combine_kernel(cells, total_shots, shots, blocks, stack, weights):
@@ -143,49 +167,70 @@
     hbm = pl.BlockSpec(memory_space=pltpu.HBM)
     smem = pl.BlockSpec(memory_space=pltpu.SMEM)
     params = pltpu.CompilerParams(vmem_limit_bytes=24 << 20)
-    partial, message = pl.pallas_call(
+    half = owners // 2
+    edges, window = 4 * owners + shots, cols // 2 + 2
+    sent = shots * own * window
+    place = jnp.stack([lax.axis_index("shot"), lax.axis_index("depth")])
+    partial, message, handed = pl.pallas_call(
         local_filter_kernel,
-        out_shape=(pltpu.VMEM(correlation.shape, f32), pltpu.VMEM((4 * owners + shots, width), f32)),
-        in_specs=[hbm, hbm, hbm],
-        out_specs=(vmem, vmem),
+        out_shape=(
+            pltpu.VMEM(correlation.shape, f32),
+            pltpu.VMEM((edges, width), f32),
+            pltpu.VMEM((edges + half * sent, width), f32),
+        ),
+        in_specs=[hbm, hbm, hbm, hbm],
+        out_specs=(vmem, vmem, vmem),
         scratch_shapes=[
             pltpu.VMEM((shots, rows + 2, cols, slab), f32),
             pltpu.VMEM(correlation.shape, f32),
             pltpu.VMEM(correlation.shape, f32),
             pltpu.SMEM(aperture.shape, aperture.dtype),
+            pltpu.SMEM(place.shape, place.dtype),
             pltpu.SemaphoreType.DMA((2, shots)),
-            pltpu.SemaphoreType.DMA,
+            pltpu.SemaphoreType.DMA((2,)),
         ],
         compiler_params=params,
         name="local_filter",
-    )(in_hbm(aperture), in_hbm(correlation), in_hbm(illumination))
+    )(in_hbm(aperture), in_hbm(correlation), in_hbm(illumination), place)
     messages = [message]
     for k in range(1, slabs):
-        messages.append(lax.ppermute(message, "depth", [(i, i ^ k) for i in range(slabs)]))
-    place = jnp.stack([lax.axis_index("shot"), lax.axis_index("depth")])
-
-    def finish_body(aperture, place, partial, *refs):
-        finish_filter_kernel(aperture, place, partial, refs[:slabs], refs[slabs : slabs + owners], *refs[slabs + owners :])
-
-    block = pltpu.VMEM((shots * own * (cols // 2 + 2) + 2 * shots, slab), f32)
+        pairs = [(i, i ^ k) for i in range(slabs)]
+        if k == 1:
+            handed = lax.ppermute(handed, "depth", pairs)
+            messages.append(message)
+        else:
+            messages.append(lax.ppermute(message, "depth", pairs))
+
+    def finish_body(aperture, place, partial, handed, *refs):
+        finish_filter_kernel(
+            aperture, place, partial, handed, (refs[0], None) + refs[1 : slabs - 1], refs[slabs - 1 : slabs - 1 + half], *refs[slabs - 1 + half :]
+        )
+
     blocks = list(pl.pallas_call(
         finish_body,
-        out_shape=(block,) * owners,
+        out_shape=(pltpu.VMEM((2, sent + 2 * shots, slab), f32),) * half,
         in_specs=[smem, smem] + [vmem] * (1 + slabs),
-        out_specs=(vmem,) * owners,
+        out_specs=(vmem,) * half,
         scratch_shapes=[
             pltpu.VMEM((slabs,) + message.shape, f32),
-            pltpu.VMEM((owners, shots * own, cols, slab), f32),
+            pltpu.VMEM((2, half, width, slab), f32),
         ],
         compiler_params=params,
         name="finish_filter",
-    )(aperture, place, *(in_vmem(v) for v in (partial, *messages))))
-    for k in range(1, owners):
-        blocks[k] = lax.ppermute(blocks[k], "shot", [(i, i ^ k) for i in range(owners)])
+    )(aperture, place, *(in_vmem(v) for v in (partial, handed, messages[0], *messages[2:]))))
+    passed = []
+    for k in range(half):
+        pairs = []
+        for g in range(owners):
+            for d in range(slabs):
+                pairs.append((g * slabs + d, (g ^ (d % 2 * half + k)) * slabs + d))
+        blocks[k] = lax.ppermute(blocks[k], ("shot", "depth"), pairs)
+        passed.append(lax.ppermute(blocks[k], "depth", [(i, i ^ 1) for i in range(slabs)]))
     cells = rows * cols * slab * slabs
 
     def combine_body(*refs):
-        combine_kernel(cells, shots * owners, shots, refs[:owners], *refs[owners:])
+        received = [ref.at[0] for ref in refs[:half]] + [ref.at[1] for ref in refs[half:owners]]
+        combine_kernel(cells, shots * owners, shots, received, *refs[owners:])
 
     return pl.pallas_call(
         combine_body,
@@ -195,7 +240,7 @@
         scratch_shapes=[pltpu.VMEM((owners * shots, slab), f32)],
         compiler_params=params,
         name="combine",
-    )(*(in_vmem(v) for v in blocks))
+    )(*(in_vmem(v) for v in blocks + passed))
 
 
 def solution(mesh):

time: 27.7 us -> 25.2 us (0.910)
  waiting for transfers between devices: 9.57 us -> 4.66 us
  starting transfers between devices: 14.3 us -> 16.7 us
    ppermute x10 -> x11, waiting for transfers between devices: 9.57 us -> 4.66 us  [the longest x2 3.73 us: on_device(): messages.append(lax.ppermute(message, 'depth', pairs))]
    ppermute x10 -> x11, starting transfers between devices: 14.3 us -> 16.7 us  [the longest x4 9.31 us: on_device(): lax.ppermute(blocks[k], 'depth', [(i, i ^ 1) for i in range(slabs)])]
  transfers between devices with their start and end apart: 10 -> 11, of which waited for: 5 -> 3; matrix products, arithmetic and copies ran while one was open for 0% -> 0% of each run, Pallas kernels for 0% -> 0%
where the time goes in v4:
time: 25.2 us; the launch traced here: 25 us
  starting transfers between devices  16.7 us (66%)
  waiting for transfers between devices  4.66 us (18%)
  Pallas kernels  3.51 us (14%)
    ppermute x4, starting transfers between devices, on_device(): lax.ppermute(blocks[k], 'depth', [(i, i ^ 1) for i in range(slabs)])  9.31 us
    ppermute x4, starting transfers between devices, on_device(): blocks[k] = lax.ppermute(blocks[k], ('shot', 'depth'), pairs)  4.22 us
    ppermute x2, waiting for transfers between devices, on_device(): messages.append(lax.ppermute(message, 'depth', pairs))  3.73 us
    ppermute x2, starting transfers between devices, on_device(): messages.append(lax.ppermute(message, 'depth', pairs))  2.64 us
    pallas_call x1, Pallas kernels, on_device(): pl.pallas_call(local_filter_kernel, out_shape=(pltpu.VMEM(correlation.sha...  1.86 us
    ppermute x4, waiting for transfers between devices, on_device(): lax.ppermute(blocks[k], 'depth', [(i, i ^ 1) for i in range(slabs)])  0.92 us
    pallas_call x1, Pallas kernels, on_device(): pl.pallas_call(combine_body, out_shape=jax.ShapeDtypeStruct((own, cols, s...  0.85 us
    pallas_call x1, Pallas kernels, on_device(): pl.pallas_call(finish_body, out_shape=(pltpu.VMEM((2, sent + 2 * shots, s...  0.8 us
  transfers between devices with their start and end apart: 11, of which 3 were waited for; matrix products, arithmetic and copies ran while one was open for 0% of the time, Pallas kernels for 0%

profile of v4, /device:TPU:0, one launch (start us, length us, event | category | flops | bytes accessed | tf_op | source)
XLA Modules:
  0.0 25.0 jit_solution(9872773731721544212)
XLA Ops:
  0.0 0.1 pad_add_fusion.place_hbm.place
  0.1 1.9 %local_filter.1 = (f32[2,16,32,128]{3,2,1,0:T(8,128)S(1)}, f32[34,128]{1,0:T(8,128)S(1)}, f32[322,128]{1,0:T(8,128)S(1)}) custom-call(s32[2,4]{1,0:T(2,128)} %aperture.1, f32[2,16,32,128]{3,2,1,0:T(8,128)} %correlation_hbm.1, f32[2,16,32,128]{3,2,1,0:T(8,128)} %illumination_hbm.1, s32[2]{0:T(128)S(1)} %pad_add_fusion.place_hbm.place), custom_call_target="tpu_custom_call" | custom-call | tf_op jit(solution)/shard_map/local_filter/pallas_call | solution.py:174
  1.9 0.6 %collective-permute-start = (f32[322,128]{1,0:T(8,128)S(1)}, f32[322,128]{1,0:T(8,128)S(1)}, u32[]{:S(2)}, u32[]{:S(2)}) collective-permute-start(f32[322,128]{1,0:T(8,128)S(1)} %get-tuple-element.13), channel_id=1, source_target_pairs={{0,1},{1,0},{2,3},{3,2},{4,5},{5,4},{6,7},{7,6},{8,9},{9,8},{10,11... | collective-permute-start | bytes 494600 | tf_op jit(solution)/shard_map/ppermute | solution.py:199
  2.5 0.0 copy-start
  2.5 2.6 %collective-permute-start.2 = (f32[34,128]{1,0:T(8,128)S(1)}, f32[34,128]{1,0:T(8,128)S(1)}, u32[]{:S(2)}, u32[]{:S(2)}) collective-permute-start(f32[34,128]{1,0:T(8,128)S(1)} %get-tuple-element.14.refs_0_), channel_id=1, source_target_pairs={{0,3},{1,2},{2,1},{3,0},{4,7},{5,6},{6,5},{7,4},{8,11},{9,10},{10,... | collective-permute-start | bytes 52232 | tf_op jit(solution)/shard_map/ppermute | solution.py:202
  5.1 0.1 collective-permute-start.1
  5.1 1.4 %collective-permute-done.2.refs_2_ = f32[34,128]{1,0:T(8,128)S(1)} collective-permute-done((f32[34,128]{1,0:T(8,128)S(1)}, f32[34,128]{1,0:T(8,128)S(1)}, u32[]{:S(2)}, u32[]{:S(2)}) %collective-permute-start.2) | collective-permute-done | bytes 17440 | tf_op jit(solution)/shard_map/ppermute | solution.py:202
  6.6 2.3 %collective-permute-done.1.refs_1_ = f32[34,128]{1,0:T(8,128)S(1)} collective-permute-done((f32[34,128]{1,0:T(8,128)S(1)}, f32[34,128]{1,0:T(8,128)S(1)}, u32[]{:S(2)}, u32[]{:S(2)}) %collective-permute-start.1) | collective-permute-done | bytes 17440 | tf_op jit(solution)/shard_map/ppermute | solution.py:202
  8.9 0.0 collective-permute-done.handed
  8.9 0.0 copy-done
  8.9 0.8 %finish_filter.1 = (f32[2,76,128]{2,1,0:T(8,128)S(1)}, f32[2,76,128]{2,1,0:T(8,128)S(1)}, f32[2,76,128]{2,1,0:T(8,128)S(1)}, f32[2,76,128]{2,1,0:T(8,128)S(1)}) custom-call(s32[2,4]{1,0:T(2,128)S(1)} %copy-done, s32[2]{0:T(128)S(1)} %pad_add_fusion.place_hbm.place, f32[2,16,32,128]{3,2,1,0:T(8,128)S(1)} %get-tuple-element.12.partial, ...), custom_call_target="tpu_custom_call" | custom-call | tf_op jit(solution)/shard_map/finish_filter/pallas_call | solution.py:209
  9.7 0.7 %collective-permute-start.3 = (f32[2,76,128]{2,1,0:T(8,128)S(1)}, f32[2,76,128]{2,1,0:T(8,128)S(1)}, u32[]{:S(2)}, u32[]{:S(2)}) collective-permute-start(f32[2,76,128]{2,1,0:T(8,128)S(1)} %get-tuple-element.15), channel_id=1, source_target_pairs={{0,0},{1,17},{2,2},{3,19},{4,4},{5,21},{6,6},{7,23},{8,8},{9,25},{... | collective-permute-start | bytes 233480 | tf_op jit(solution)/shard_map/ppermute | solution.py:227
  10.4 1.6 %collective-permute-start.4 = (f32[2,76,128]{2,1,0:T(8,128)S(1)}, f32[2,76,128]{2,1,0:T(8,128)S(1)}, u32[]{:S(2)}, u32[]{:S(2)}) collective-permute-start(f32[2,76,128]{2,1,0:T(8,128)S(1)} %get-tuple-element.16), channel_id=1, source_target_pairs={{0,4},{1,21},{2,6},{3,23},{4,0},{5,17},{6,2},{7,19},{8,12},{9,29},... | collective-permute-start | bytes 233480 | tf_op jit(solution)/shard_map/ppermute | solution.py:227
  11.9 1.6 %collective-permute-start.5 = (f32[2,76,128]{2,1,0:T(8,128)S(1)}, f32[2,76,128]{2,1,0:T(8,128)S(1)}, u32[]{:S(2)}, u32[]{:S(2)}) collective-permute-start(f32[2,76,128]{2,1,0:T(8,128)S(1)} %get-tuple-element.17), channel_id=1, source_target_pairs={{0,8},{1,25},{2,10},{3,27},{4,12},{5,29},{6,14},{7,31},{8,0},{9,17... | collective-permute-start | bytes 233480 | tf_op jit(solution)/shard_map/ppermute | solution.py:227
  13.5 0.4 %collective-permute-start.6 = (f32[2,76,128]{2,1,0:T(8,128)S(1)}, f32[2,76,128]{2,1,0:T(8,128)S(1)}, u32[]{:S(2)}, u32[]{:S(2)}) collective-permute-start(f32[2,76,128]{2,1,0:T(8,128)S(1)} %get-tuple-element.18), channel_id=1, source_target_pairs={{0,12},{1,29},{2,14},{3,31},{4,8},{5,25},{6,10},{7,27},{8,4},{9,21... | collective-permute-start | bytes 233480 | tf_op jit(solution)/shard_map/ppermute | solution.py:227
  13.9 0.0 collective-permute-done.3.refs_0_
  13.9 3.3 %collective-permute-start.7 = (f32[2,76,128]{2,1,0:T(8,128)S(1)}, f32[2,76,128]{2,1,0:T(8,128)S(1)}, u32[]{:S(2)}, u32[]{:S(2)}) collective-permute-start(f32[2,76,128]{2,1,0:T(8,128)S(1)} %collective-permute-done.3.refs_0_), channel_id=1, source_target_pairs={{0,1},{1,0},{2,3},{3,2},{4,5},{5,4},{6,7},{7,6},{8,9},{9,8},{10,11... | collective-permute-start | bytes 233480 | tf_op jit(solution)/shard_map/ppermute | solution.py:228
  17.3 0.0 collective-permute-done.4.refs_1_
  17.3 0.8 %collective-permute-start.8 = (f32[2,76,128]{2,1,0:T(8,128)S(1)}, f32[2,76,128]{2,1,0:T(8,128)S(1)}, u32[]{:S(2)}, u32[]{:S(2)}) collective-permute-start(f32[2,76,128]{2,1,0:T(8,128)S(1)} %collective-permute-done.4.refs_1_), channel_id=1, source_target_pairs={{0,1},{1,0},{2,3},{3,2},{4,5},{5,4},{6,7},{7,6},{8,9},{9,8},{10,11... | collective-permute-start | bytes 233480 | tf_op jit(solution)/shard_map/ppermute | solution.py:228
  18.0 0.0 collective-permute-done.5.refs_2_
  18.0 2.8 %collective-permute-start.9 = (f32[2,76,128]{2,1,0:T(8,128)S(1)}, f32[2,76,128]{2,1,0:T(8,128)S(1)}, u32[]{:S(2)}, u32[]{:S(2)}) collective-permute-start(f32[2,76,128]{2,1,0:T(8,128)S(1)} %collective-permute-done.5.refs_2_), channel_id=1, source_target_pairs={{0,1},{1,0},{2,3},{3,2},{4,5},{5,4},{6,7},{7,6},{8,9},{9,8},{10,11... | collective-permute-start | bytes 233480 | tf_op jit(solution)/shard_map/ppermute | solution.py:228
  20.9 0.0 collective-permute-done.6.refs_3_
  20.9 2.4 %collective-permute-start.10 = (f32[2,76,128]{2,1,0:T(8,128)S(1)}, f32[2,76,128]{2,1,0:T(8,128)S(1)}, u32[]{:S(2)}, u32[]{:S(2)}) collective-permute-start(f32[2,76,128]{2,1,0:T(8,128)S(1)} %collective-permute-done.6.refs_3_), channel_id=1, source_target_pairs={{0,1},{1,0},{2,3},{3,2},{4,5},{5,4},{6,7},{7,6},{8,9},{9,8},{10,11... | collective-permute-start | bytes 233480 | tf_op jit(solution)/shard_map/ppermute | solution.py:228
  23.2 0.0 collective-permute-done.7.refs_4_
  23.2 0.0 collective-permute-done.8.refs_5_
  23.3 0.0 collective-permute-done.9.refs_6_
  23.3 0.9 %collective-permute-done.10.refs_7_ = f32[2,76,128]{2,1,0:T(8,128)S(1)} collective-permute-done((f32[2,76,128]{2,1,0:T(8,128)S(1)}, f32[2,76,128]{2,1,0:T(8,128)S(1)}, u32[]{:S(2)}, u32[]{:S(2)}) %collective-permute-start.10) | collective-permute-done | bytes 77856 | tf_op jit(solution)/shard_map/ppermute | solution.py:228
  24.2 0.8 %combine.1 = f32[2,32,128]{2,1,0:T(8,128)} custom-call(f32[2,76,128]{2,1,0:T(8,128)S(1)} %collective-permute-done.3.refs_0_, f32[2,76,128]{2,1,0:T(8,128)S(1)} %collective-permute-done.4.refs_1_, f32[2,76,128]{2,1,0:T(8,128)S(1)} %collective-permute-done.5.refs_2_, f32[2,76,128]{2,1,0:T(8,128)S(1)} %collective-permute-done.6.refs_3_, ...), custom_call_target="tpu_custom_call" | custom-call | tf_op jit(solution)/shard_map/combine/pallas_call | solution.py:235
Async XLA Ops:
  1.9 6.9 %collective-permute-start = (f32[322,128]{1,0:T(8,128)S(1)}, f32[322,128]{1,0:T(8,128)S(1)}, u32[]{:S(2)}, u32[]{:S(2)}) collective-permute-start(f32[322,128]{1,0:T(8,128)S(1)} %get-tuple-element.13), channel_id=1, source_target_pairs={{0,1},{1,0},{2,3},{3,2},{4,5},{5,4},{6,7},{7,6},{8,9},{9,8},{10,11... | collective-permute-start | bytes 494600 | tf_op jit(solution)/shard_map/ppermute | solution.py:199
  2.5 6.4 %copy-start = (s32[2,4]{1,0:T(2,128)S(1)}, s32[2,4]{1,0:T(2,128)}, u32[]{:S(2)}) copy-start(s32[2,4]{1,0:T(2,128)} %aperture.1) | copy-start | bytes 100
  2.5 4.1 %collective-permute-start.2 = (f32[34,128]{1,0:T(8,128)S(1)}, f32[34,128]{1,0:T(8,128)S(1)}, u32[]{:S(2)}, u32[]{:S(2)}) collective-permute-start(f32[34,128]{1,0:T(8,128)S(1)} %get-tuple-element.14.refs_0_), channel_id=1, source_target_pairs={{0,3},{1,2},{2,1},{3,0},{4,7},{5,6},{6,5},{7,4},{8,11},{9,10},{10,... | collective-permute-start | bytes 52232 | tf_op jit(solution)/shard_map/ppermute | solution.py:202
  5.1 3.8 %collective-permute-start.1 = (f32[34,128]{1,0:T(8,128)S(1)}, f32[34,128]{1,0:T(8,128)S(1)}, u32[]{:S(2)}, u32[]{:S(2)}) collective-permute-start(f32[34,128]{1,0:T(8,128)S(1)} %get-tuple-element.14.refs_0_), channel_id=1, source_target_pairs={{0,2},{1,3},{2,0},{3,1},{4,6},{5,7},{6,4},{7,5},{8,10},{9,11},{10,... | collective-permute-start | bytes 52232 | tf_op jit(solution)/shard_map/ppermute | solution.py:202
  9.7 4.2 %collective-permute-start.3 = (f32[2,76,128]{2,1,0:T(8,128)S(1)}, f32[2,76,128]{2,1,0:T(8,128)S(1)}, u32[]{:S(2)}, u32[]{:S(2)}) collective-permute-start(f32[2,76,128]{2,1,0:T(8,128)S(1)} %get-tuple-element.15), channel_id=1, source_target_pairs={{0,0},{1,17},{2,2},{3,19},{4,4},{5,21},{6,6},{7,23},{8,8},{9,25},{... | collective-permute-start | bytes 233480 | tf_op jit(solution)/shard_map/ppermute | solution.py:227
  10.4 6.9 %collective-permute-start.4 = (f32[2,76,128]{2,1,0:T(8,128)S(1)}, f32[2,76,128]{2,1,0:T(8,128)S(1)}, u32[]{:S(2)}, u32[]{:S(2)}) collective-permute-start(f32[2,76,128]{2,1,0:T(8,128)S(1)} %get-tuple-element.16), channel_id=1, source_target_pairs={{0,4},{1,21},{2,6},{3,23},{4,0},{5,17},{6,2},{7,19},{8,12},{9,29},... | collective-permute-start | bytes 233480 | tf_op jit(solution)/shard_map/ppermute | solution.py:227
  11.9 6.1 %collective-permute-start.5 = (f32[2,76,128]{2,1,0:T(8,128)S(1)}, f32[2,76,128]{2,1,0:T(8,128)S(1)}, u32[]{:S(2)}, u32[]{:S(2)}) collective-permute-start(f32[2,76,128]{2,1,0:T(8,128)S(1)} %get-tuple-element.17), channel_id=1, source_target_pairs={{0,8},{1,25},{2,10},{3,27},{4,12},{5,29},{6,14},{7,31},{8,0},{9,17... | collective-permute-start | bytes 233480 | tf_op jit(solution)/shard_map/ppermute | solution.py:227
  13.5 7.3 %collective-permute-start.6 = (f32[2,76,128]{2,1,0:T(8,128)S(1)}, f32[2,76,128]{2,1,0:T(8,128)S(1)}, u32[]{:S(2)}, u32[]{:S(2)}) collective-permute-start(f32[2,76,128]{2,1,0:T(8,128)S(1)} %get-tuple-element.18), channel_id=1, source_target_pairs={{0,12},{1,29},{2,14},{3,31},{4,8},{5,25},{6,10},{7,27},{8,4},{9,21... | collective-permute-start | bytes 233480 | tf_op jit(solution)/shard_map/ppermute | solution.py:227
  13.9 9.3 %collective-permute-start.7 = (f32[2,76,128]{2,1,0:T(8,128)S(1)}, f32[2,76,128]{2,1,0:T(8,128)S(1)}, u32[]{:S(2)}, u32[]{:S(2)}) collective-permute-start(f32[2,76,128]{2,1,0:T(8,128)S(1)} %collective-permute-done.3.refs_0_), channel_id=1, source_target_pairs={{0,1},{1,0},{2,3},{3,2},{4,5},{5,4},{6,7},{7,6},{8,9},{9,8},{10,11... | collective-permute-start | bytes 233480 | tf_op jit(solution)/shard_map/ppermute | solution.py:228
  17.3 6.0 %collective-permute-start.8 = (f32[2,76,128]{2,1,0:T(8,128)S(1)}, f32[2,76,128]{2,1,0:T(8,128)S(1)}, u32[]{:S(2)}, u32[]{:S(2)}) collective-permute-start(f32[2,76,128]{2,1,0:T(8,128)S(1)} %collective-permute-done.4.refs_1_), channel_id=1, source_target_pairs={{0,1},{1,0},{2,3},{3,2},{4,5},{5,4},{6,7},{7,6},{8,9},{9,8},{10,11... | collective-permute-start | bytes 233480 | tf_op jit(solution)/shard_map/ppermute | solution.py:228
  18.0 5.2 %collective-permute-start.9 = (f32[2,76,128]{2,1,0:T(8,128)S(1)}, f32[2,76,128]{2,1,0:T(8,128)S(1)}, u32[]{:S(2)}, u32[]{:S(2)}) collective-permute-start(f32[2,76,128]{2,1,0:T(8,128)S(1)} %collective-permute-done.5.refs_2_), channel_id=1, source_target_pairs={{0,1},{1,0},{2,3},{3,2},{4,5},{5,4},{6,7},{7,6},{8,9},{9,8},{10,11... | collective-permute-start | bytes 233480 | tf_op jit(solution)/shard_map/ppermute | solution.py:228
  20.9 3.3 %collective-permute-start.10 = (f32[2,76,128]{2,1,0:T(8,128)S(1)}, f32[2,76,128]{2,1,0:T(8,128)S(1)}, u32[]{:S(2)}, u32[]{:S(2)}) collective-permute-start(f32[2,76,128]{2,1,0:T(8,128)S(1)} %collective-permute-done.6.refs_3_), channel_id=1, source_target_pairs={{0,1},{1,0},{2,3},{3,2},{4,5},{5,4},{6,7},{7,6},{8,9},{9,8},{10,11... | collective-permute-start | bytes 233480 | tf_op jit(solution)/shard_map/ppermute | solution.py:228

commit v5 on v4

v5 whole, which is shorter than its diff:
```python
import math

import jax
import jax.numpy as jnp
from jax import lax
from jax.experimental import pallas as pl
from jax.experimental.pallas import tpu as pltpu
from jax.sharding import PartitionSpec as P


def partner_of(here, core, k):
    return here ^ (2 * k + core)


def local_filter_kernel(
    aperture_hbm, correlation_hbm, illumination_hbm, partial, message, handed, early,
    padded, correlation, illumination, aperture, arrived, read,
):
    shots, rows, cols, slab = correlation.shape
    own = message.shape[1] // (shots * cols)
    owners = rows // own
    window = cols // 2 + 2
    boxes = pltpu.make_async_copy(aperture_hbm, aperture, read)
    boxes.start()
    copies = []
    for s in range(shots):
        copies.append((
            pltpu.make_async_copy(correlation_hbm.at[s], correlation.at[s], arrived.at[0, s]),
            pltpu.make_async_copy(illumination_hbm.at[s], illumination.at[s], arrived.at[1, s]),
        ))
        for copy in copies[s]:
            copy.start()
    second = lax.broadcasted_iota(jnp.int32, (cols, slab), 0)
    lane = lax.broadcasted_iota(jnp.int32, (cols, slab), 1)
    zero = jnp.zeros((cols, slab), jnp.float32)
    boxes.wait()
    starts = [jnp.clip(aperture[s, 2] - 1, 0, cols - window) for s in range(shots)]
    for s in range(shots):
        padded[s, 0] = zero
        padded[s, rows + 1] = zero
        for copy in copies[s]:
            copy.wait()
        in_cols = (second >= aperture[s, 2]) & (second < aperture[s, 3])
        for x in range(rows):
            keep = in_cols & (x >= aperture[s, 0]) & (x < aperture[s, 1])
            padded[s, x + 1] = jnp.where(keep, correlation[s, x] / (illumination[s, x] + 0.1), 0.0)
        total = zero
        for x in range(rows):
            n = padded[s, x + 1]
            beside = padded[s, x] + padded[s, x + 2]
            beside += jnp.where(second == 0, 0.0, pltpu.roll(n, 1, 0))
            beside += jnp.where(second == cols - 1, 0.0, pltpu.roll(n, cols - 1, 0))
            beside += jnp.where(lane == 0, 0.0, pltpu.roll(n, 1, 1))
            beside += jnp.where(lane == slab - 1, 0.0, pltpu.roll(n, slab - 1, 1))
            value = 6.0 * n - beside
            partial[s, x] = value
            total += value * value
        message[4 * owners + s : 4 * owners + s + 1] = jnp.sum(total, axis=0, keepdims=True)
        at = 4 * owners + shots + s
        message[at : at + 1] = jnp.full((1, slab), starts[s].astype(jnp.float32))
    for r in range(owners):
        for at, image, shift in ((0, padded, 1), (2 * owners, partial, 0)):
            held = [image[s, r * own + j + shift] for s in range(shots) for j in range(own)]
            turned = jnp.concatenate(held, axis=0).T
            message[at + r : at + r + 1] = turned[0:1]
            message[at + owners + r : at + owners + r + 1] = turned[slab - 1 : slab]
    edges = message.shape[0]
    handed[0:edges] = message[...]
    mine, core = lax.axis_index("shot"), lax.axis_index("depth") % 2
    for k in range(owners // 2):
        r = partner_of(mine, 1 - core, k)
        for s in range(shots):
            for j in range(own):
                at = edges + (k * shots * own + s * own + j) * window
                handed[at : at + window] = partial[s, r * own + j, pl.ds(starts[s], window)]
    r = partner_of(mine, core, owners // 2 - 1)
    for s in range(shots):
        for j in range(own):
            at = (s * own + j) * window
            early[at : at + window] = partial[s, r * own + j, pl.ds(starts[s], window)]


def finish_filter_kernel(partial, handed, messages, blocks, slabs_held, halo):
    shots, rows, cols, slab = partial.shape
    slabs = len(messages)
    edges, width = messages[0].shape
    own = width // (shots * cols)
    owners = rows // own
    half = owners // 2
    window = cols // 2 + 2
    sent = shots * own * window
    mine, here = lax.axis_index("shot"), lax.axis_index("depth")
    for k in range(slabs):
        slabs_held[here ^ k] = messages[k][...] if k != 1 else handed[0:edges]
    cross = jnp.zeros((owners, width), jnp.float32)
    for d in range(slabs - 1):
        right = slabs_held[d + 1, 0:owners]
        left = slabs_held[d, owners : 2 * owners]
        cross += right * (right - 2.0 * slabs_held[d, 3 * owners : 4 * owners])
        cross += left * (left - 2.0 * slabs_held[d + 1, 2 * owners : 3 * owners])
    cross = jnp.sum(cross, axis=0, keepdims=True)
    lane = lax.broadcasted_iota(jnp.int32, (1, width), 1)
    tails = []
    starts = []
    for s in range(shots):
        energy = jnp.where((lane >= s * own * cols) & (lane < (s + 1) * own * cols), cross, 0.0)
        for d in range(slabs):
            energy += slabs_held[d, 4 * owners + s : 4 * owners + s + 1]
        tails.append(energy)
        starts.append(jnp.max(messages[0][4 * owners + shots + s : 4 * owners + shots + s + 1]).astype(jnp.int32))
    tails.append(messages[0][4 * owners + shots :])
    tail = jnp.concatenate(tails, axis=0)
    depth = lax.broadcasted_iota(jnp.int32, (slab, width), 0)
    for whose in range(2):
        d = here ^ whose
        below = jnp.maximum(d - 1, 0)
        above = jnp.minimum(d + 1, slabs - 1)
        for k in range(half):
            r = partner_of(mine, here % 2, k)
            low = jnp.where(d > 0, slabs_held[below, pl.ds(owners + r, 1)], 0.0)
            high = jnp.where(d < slabs - 1, slabs_held[above, pl.ds(r, 1)], 0.0)
            last = k == half - 1
            if last and not whose:
                blocks[k][0:1] = low
                blocks[k][1:2] = high
                continue
            halo[whose, k] = jnp.where(depth == 0, low, jnp.where(depth == slab - 1, high, 0.0)).T
            for s in range(shots):
                for j in range(own):
                    i = s * own + j
                    if whose:
                        at = edges + (k * shots * own + i) * window
                        value = handed[at : at + window]
                        at = (2 if last else sent) + i * window
                    else:
                        value = partial[s, r * own + j, pl.ds(starts[s], window)]
                        at = i * window
                    blocks[k][at : at + window] = value - halo[whose, k, pl.ds(i * cols + starts[s], window)]
    for k in range(half):
        blocks[k][blocks[k].shape[0] - 2 * shots :] = tail


def combine_kernel(cells, total_shots, shots, parts, early, layers, stack, weights, halo):
    own, cols, slab = stack.shape
    window = cols // 2 + 2
    tails = [block.shape[0] - 2 * shots for block, _ in parts]
    energy = jnp.concatenate([block[at : at + shots] for (block, _), at in zip(parts, tails)], axis=0)
    meansq = jnp.sum(energy, axis=1, keepdims=True) / cells
    peak = jnp.max(meansq, axis=0, keepdims=True)
    weight = (1.0 / math.sqrt(total_shots)) / jnp.sqrt(meansq + 0.5 * peak + 1.0)
    weights[...] = jnp.broadcast_to(weight, weights.shape)
    stack[...] = jnp.zeros(stack.shape, jnp.float32)
    width = shots * own * cols
    depth = lax.broadcasted_iota(jnp.int32, (slab, width), 0)
    halo[...] = jnp.where(depth == 0, layers[0:1], jnp.where(depth == slab - 1, layers[1:2], 0.0)).T
    for k, ((block, rows), tail) in enumerate(zip(parts, tails)):
        for s in range(shots):
            at = tail + shots + s
            start = jnp.max(block[at : at + 1]).astype(jnp.int32)
            scale = weights[k * shots + s : k * shots + s + 1]
            for j in range(own):
                i = s * own + j
                if rows is None:
                    value = early[i * window : (i + 1) * window] - halo[pl.ds(i * cols + start, window)]
                else:
                    value = block[rows + i * window : rows + (i + 1) * window]
                stack[j, pl.ds(start, window)] += scale * value


def in_hbm(array):
    return pltpu.with_memory_space_constraint(array, pltpu.HBM)


def in_vmem(array):
    return pltpu.with_memory_space_constraint(array, pltpu.VMEM)


def on_device(correlation, illumination, aperture):
    shots, rows, cols, slab = correlation.shape
    owners, slabs = lax.axis_size("shot"), lax.axis_size("depth")
    assert owners & (owners - 1) == 0 and slabs & (slabs - 1) == 0 and rows % owners == 0
    own = rows // owners
    width = shots * own * cols
    assert width == slab == 128
    half = owners // 2
    edges, window = 4 * owners + 2 * shots, cols // 2 + 2
    sent = shots * own * window
    f32 = jnp.float32
    vmem = pl.BlockSpec(memory_space=pltpu.VMEM)
    hbm = pl.BlockSpec(memory_space=pltpu.HBM)
    params = pltpu.CompilerParams(vmem_limit_bytes=24 << 20)
    partial, message, handed, early = pl.pallas_call(
        local_filter_kernel,
        out_shape=(
            pltpu.VMEM(correlation.shape, f32),
            pltpu.VMEM((edges, width), f32),
            pltpu.VMEM((edges + half * sent, width), f32),
            pltpu.VMEM((sent, width), f32),
        ),
        in_specs=[hbm, hbm, hbm],
        out_specs=(vmem, vmem, vmem, vmem),
        scratch_shapes=[
            pltpu.VMEM((shots, rows + 2, cols, slab), f32),
            pltpu.VMEM(correlation.shape, f32),
            pltpu.VMEM(correlation.shape, f32),
            pltpu.SMEM(aperture.shape, aperture.dtype),
            pltpu.SemaphoreType.DMA((2, shots)),
            pltpu.SemaphoreType.DMA,
        ],
        compiler_params=params,
        name="local_filter",
    )(in_hbm(aperture), in_hbm(correlation), in_hbm(illumination))

    def round_pairs(k):
        pairs = []
        for g in range(owners):
            for d in range(slabs):
                pairs.append((g * slabs + d, partner_of(g, d % 2, k) * slabs + d))
        return pairs

    messages = [message]
    for k in range(1, slabs):
        pairs = [(i, i ^ k) for i in range(slabs)]
        if k == 1:
            handed = lax.ppermute(handed, "depth", pairs)
            messages.append(message)
        else:
            messages.append(lax.ppermute(message, "depth", pairs))
    early = lax.ppermute(early, ("shot", "depth"), round_pairs(half - 1))

    def finish_body(partial, handed, *refs):
        finish_filter_kernel(
            partial, handed, (refs[0], None) + refs[1 : slabs - 1], refs[slabs - 1 : slabs - 1 + half], *refs[slabs - 1 + half :]
        )

    block = pltpu.VMEM((2 * sent + 2 * shots, slab), f32)
    light = pltpu.VMEM((2 + sent + 2 * shots, slab), f32)
    blocks = list(pl.pallas_call(
        finish_body,
        out_shape=(block,) * (half - 1) + (light,),
        in_specs=[vmem] * (1 + slabs),
        out_specs=(vmem,) * half,
        scratch_shapes=[
            pltpu.VMEM((slabs,) + message.shape, f32),
            pltpu.VMEM((2, half, width, slab), f32),
        ],
        compiler_params=params,
        name="finish_filter",
    )(*(in_vmem(v) for v in (partial, handed, messages[0], *messages[2:]))))
    passed = []
    for k in range(half):
        blocks[k] = lax.ppermute(blocks[k], ("shot", "depth"), round_pairs(k))
        passed.append(lax.ppermute(blocks[k], "depth", [(i, i ^ 1) for i in range(slabs)]))
    cells = rows * cols * slab * slabs

    def combine_body(early, *refs):
        ours, theirs = refs[:half], refs[half:owners]
        parts = [(ref, None if k == half - 1 else 0) for k, ref in enumerate(ours)]
        parts += [(ref, 2 if k == half - 1 else sent) for k, ref in enumerate(theirs)]
        combine_kernel(cells, shots * owners, shots, parts, early, ours[half - 1], *refs[owners:])

    return pl.pallas_call(
        combine_body,
        out_shape=jax.ShapeDtypeStruct((own, cols, slab), f32),
        in_specs=[vmem] * (1 + owners),
        out_specs=vmem,
        scratch_shapes=[pltpu.VMEM((owners * shots, slab), f32), pltpu.VMEM((width, slab), f32)],
        compiler_params=params,
        name="combine",
    )(*(in_vmem(v) for v in [early] + blocks + passed))


def solution(mesh):
    return jax.shard_map(
        on_device,
        mesh=mesh,
        in_specs=(P("shot", None, None, "depth"), P("shot", None, None, "depth"), P("shot", None)),
        out_specs=P("shot", None, "depth"),
        check_vma=False,
    )
```

time: 25.2 us -> 28 us (1.11)
  waiting for transfers between devices: 4.66 us -> 7.95 us
  Pallas kernels: 3.51 us -> 2.93 us
    ppermute x4 -> x5, waiting for transfers between devices: 0.01 us -> 4.2 us  [the longest x1 3.63 us: on_device(): early = lax.ppermute(early, ('shot', 'depth'), round_pairs(half - 1))]
    ppermute x4 -> x5, starting transfers between devices: 4.22 us -> 7.25 us  [the longest x4 5.12 us: on_device(): blocks[k] = lax.ppermute(blocks[k], ('shot', 'depth'), round_pairs(k))]
    ppermute x4, starting transfers between devices: 9.31 us -> 6.51 us  [on_device(): lax.ppermute(blocks[k], 'depth', [(i, i ^ 1) for i in range(slabs)])]
    ppermute x4, waiting for transfers between devices: 0.92 us -> 0.01 us  [on_device(): lax.ppermute(blocks[k], 'depth', [(i, i ^ 1) for i in range(slabs)])]
    pallas_call x1, Pallas kernels: 0.8 us -> 0.25 us  [on_device(): pl.pallas_call(finish_body, out_shape=(block,) * (half - 1) + (light,), i...]
  transfers between devices with their start and end apart: 11 -> 12, of which waited for: 3 -> 4; matrix products, arithmetic and copies ran while one was open for 0% -> 0% of each run, Pallas kernels for 0% -> 0%
where the time goes in v5:
time: 28 us; the launch traced here: 27.9 us
  starting transfers between devices  16.9 us (60%)
  waiting for transfers between devices  7.95 us (28%)
  Pallas kernels  2.93 us (10%)
    ppermute x4, starting transfers between devices, on_device(): lax.ppermute(blocks[k], 'depth', [(i, i ^ 1) for i in range(slabs)])  6.51 us
    ppermute x4, starting transfers between devices, on_device(): blocks[k] = lax.ppermute(blocks[k], ('shot', 'depth'), round_pairs(k))  5.12 us
    ppermute x2, waiting for transfers between devices, on_device(): messages.append(lax.ppermute(message, 'depth', pairs))  3.74 us
    ppermute x1, waiting for transfers between devices, on_device(): early = lax.ppermute(early, ('shot', 'depth'), round_pairs(half - 1))  3.63 us
    ppermute x2, starting transfers between devices, on_device(): messages.append(lax.ppermute(message, 'depth', pairs))  2.63 us
    ppermute x1, starting transfers between devices, on_device(): early = lax.ppermute(early, ('shot', 'depth'), round_pairs(half - 1))  2.13 us
    pallas_call x1, Pallas kernels, on_device(): pl.pallas_call(local_filter_kernel, out_shape=(pltpu.VMEM(correlation.sha...  1.82 us
    pallas_call x1, Pallas kernels, on_device(): pl.pallas_call(combine_body, out_shape=jax.ShapeDtypeStruct((own, cols, s...  0.85 us
  transfers between devices with their start and end apart: 12, of which 4 were waited for; matrix products, arithmetic and copies ran while one was open for 0% of the time, Pallas kernels for 0%

profile of v5, /device:TPU:0, one launch (start us, length us, event | category | flops | bytes accessed | tf_op | source)
XLA Modules:
  0.0 27.9 jit_solution(3262077876499849207)
XLA Ops:
  0.0 1.8 %local_filter.1 = (f32[2,16,32,128]{3,2,1,0:T(8,128)S(1)}, f32[36,128]{1,0:T(8,128)S(1)}, f32[324,128]{1,0:T(8,128)S(1)}, f32[72,128]{1,0:T(8,128)S(1)}) custom-call(s32[2,4]{1,0:T(2,128)} %aperture_hbm.1, f32[2,16,32,128]{3,2,1,0:T(8,128)} %correlation_hbm.1, f32[2,16,32,128]{3,2,1,0:T(8,128)} %illumination_hbm.1), custom_call_target="tpu_custom_call" | custom-call | tf_op jit(solution)/shard_map/local_filter/pallas_call | solution.py:192
  1.8 0.6 %collective-permute-start.1 = (f32[324,128]{1,0:T(8,128)S(1)}, f32[324,128]{1,0:T(8,128)S(1)}, u32[]{:S(2)}, u32[]{:S(2)}) collective-permute-start(f32[324,128]{1,0:T(8,128)S(1)} %get-tuple-element.15), channel_id=1, source_target_pairs={{0,1},{1,0},{2,3},{3,2},{4,5},{5,4},{6,7},{7,6},{8,9},{9,8},{10,11... | collective-permute-start | bytes 497672 | tf_op jit(solution)/shard_map/ppermute | solution.py:225
  2.4 2.6 %collective-permute-start.3 = (f32[36,128]{1,0:T(8,128)S(1)}, f32[36,128]{1,0:T(8,128)S(1)}, u32[]{:S(2)}, u32[]{:S(2)}) collective-permute-start(f32[36,128]{1,0:T(8,128)S(1)} %get-tuple-element.16.refs_0_), channel_id=1, source_target_pairs={{0,3},{1,2},{2,1},{3,0},{4,7},{5,6},{6,5},{7,4},{8,11},{9,10},{10,... | collective-permute-start | bytes 55304 | tf_op jit(solution)/shard_map/ppermute | solution.py:228
  5.0 0.0 collective-permute-start.2
  5.0 1.4 %collective-permute-done.3.refs_2_ = f32[36,128]{1,0:T(8,128)S(1)} collective-permute-done((f32[36,128]{1,0:T(8,128)S(1)}, f32[36,128]{1,0:T(8,128)S(1)}, u32[]{:S(2)}, u32[]{:S(2)}) %collective-permute-start.3) | collective-permute-done | bytes 18464 | tf_op jit(solution)/shard_map/ppermute | solution.py:228
  6.5 2.3 %collective-permute-done.2.refs_1_ = f32[36,128]{1,0:T(8,128)S(1)} collective-permute-done((f32[36,128]{1,0:T(8,128)S(1)}, f32[36,128]{1,0:T(8,128)S(1)}, u32[]{:S(2)}, u32[]{:S(2)}) %collective-permute-start.2) | collective-permute-done | bytes 18464 | tf_op jit(solution)/shard_map/ppermute | solution.py:228
  8.8 0.0 collective-permute-done.1.handed
  8.8 0.3 finish_filter.1
  9.0 0.7 %collective-permute-start.4 = (f32[148,128]{1,0:T(8,128)S(1)}, f32[148,128]{1,0:T(8,128)S(1)}, u32[]{:S(2)}, u32[]{:S(2)}) collective-permute-start(f32[148,128]{1,0:T(8,128)S(1)} %get-tuple-element.17), channel_id=1, source_target_pairs={{0,0},{1,5},{2,2},{3,7},{4,4},{5,1},{6,6},{7,3},{8,8},{9,13},{10,1... | collective-permute-start | bytes 227336 | tf_op jit(solution)/shard_map/ppermute | solution.py:252
  9.7 1.6 %collective-permute-start.5 = (f32[148,128]{1,0:T(8,128)S(1)}, f32[148,128]{1,0:T(8,128)S(1)}, u32[]{:S(2)}, u32[]{:S(2)}) collective-permute-start(f32[148,128]{1,0:T(8,128)S(1)} %get-tuple-element.18), channel_id=1, source_target_pairs={{0,8},{1,13},{2,10},{3,15},{4,12},{5,9},{6,14},{7,11},{8,0},{9,5},... | collective-permute-start | bytes 227336 | tf_op jit(solution)/shard_map/ppermute | solution.py:252
  11.3 2.6 %collective-permute-start.6 = (f32[148,128]{1,0:T(8,128)S(1)}, f32[148,128]{1,0:T(8,128)S(1)}, u32[]{:S(2)}, u32[]{:S(2)}) collective-permute-start(f32[148,128]{1,0:T(8,128)S(1)} %get-tuple-element.19), channel_id=1, source_target_pairs={{0,16},{1,21},{2,18},{3,23},{4,20},{5,17},{6,22},{7,19},{8,24},{9,... | collective-permute-start | bytes 227336 | tf_op jit(solution)/shard_map/ppermute | solution.py:252
  13.9 0.2 collective-permute-start.7
  14.1 0.0 collective-permute-done.4.refs_0_
  14.2 1.5 %collective-permute-start.8 = (f32[148,128]{1,0:T(8,128)S(1)}, f32[148,128]{1,0:T(8,128)S(1)}, u32[]{:S(2)}, u32[]{:S(2)}) collective-permute-start(f32[148,128]{1,0:T(8,128)S(1)} %collective-permute-done.4.refs_0_), channel_id=1, source_target_pairs={{0,1},{1,0},{2,3},{3,2},{4,5},{5,4},{6,7},{7,6},{8,9},{9,8},{10,11... | collective-permute-start | bytes 227336 | tf_op jit(solution)/shard_map/ppermute | solution.py:253
  15.7 0.0 collective-permute-done.5.refs_1_
  15.7 0.4 %collective-permute-start.9 = (f32[148,128]{1,0:T(8,128)S(1)}, f32[148,128]{1,0:T(8,128)S(1)}, u32[]{:S(2)}, u32[]{:S(2)}) collective-permute-start(f32[148,128]{1,0:T(8,128)S(1)} %collective-permute-done.5.refs_1_), channel_id=1, source_target_pairs={{0,1},{1,0},{2,3},{3,2},{4,5},{5,4},{6,7},{7,6},{8,9},{9,8},{10,11... | collective-permute-start | bytes 227336 | tf_op jit(solution)/shard_map/ppermute | solution.py:253
  16.1 0.6 %collective-permute-done.6.refs_2_ = f32[148,128]{1,0:T(8,128)S(1)} collective-permute-done((f32[148,128]{1,0:T(8,128)S(1)}, f32[148,128]{1,0:T(8,128)S(1)}, u32[]{:S(2)}, u32[]{:S(2)}) %collective-permute-start.6) | collective-permute-done | bytes 75808 | tf_op jit(solution)/shard_map/ppermute | solution.py:252
  16.6 3.3 %collective-permute-start.10 = (f32[148,128]{1,0:T(8,128)S(1)}, f32[148,128]{1,0:T(8,128)S(1)}, u32[]{:S(2)}, u32[]{:S(2)}) collective-permute-start(f32[148,128]{1,0:T(8,128)S(1)} %collective-permute-done.6.refs_2_), channel_id=1, source_target_pairs={{0,1},{1,0},{2,3},{3,2},{4,5},{5,4},{6,7},{7,6},{8,9},{9,8},{10,11... | collective-permute-start | bytes 227336 | tf_op jit(solution)/shard_map/ppermute | solution.py:253
  20.0 0.0 collective-permute-done.7.refs_3_
  20.0 1.3 %collective-permute-start.11 = (f32[78,128]{1,0:T(8,128)S(1)}, f32[78,128]{1,0:T(8,128)S(1)}, u32[]{:S(2)}, u32[]{:S(2)}) collective-permute-start(f32[78,128]{1,0:T(8,128)S(1)} %collective-permute-done.7.refs_3_), channel_id=1, source_target_pairs={{0,1},{1,0},{2,3},{3,2},{4,5},{5,4},{6,7},{7,6},{8,9},{9,8},{10,11... | collective-permute-start | bytes 119816 | tf_op jit(solution)/shard_map/ppermute | solution.py:253
  21.2 2.1 %collective-permute-start = (f32[72,128]{1,0:T(8,128)S(1)}, f32[72,128]{1,0:T(8,128)S(1)}, u32[]{:S(2)}, u32[]{:S(2)}) collective-permute-start(f32[72,128]{1,0:T(8,128)S(1)} %get-tuple-element.13), channel_id=1, source_target_pairs={{0,24},{1,29},{2,26},{3,31},{4,28},{5,25},{6,30},{7,27},{8,16},{9,... | collective-permute-start | bytes 110600 | tf_op jit(solution)/shard_map/ppermute | solution.py:229
  23.4 3.6 %collective-permute-done.early = f32[72,128]{1,0:T(8,128)S(1)} collective-permute-done((f32[72,128]{1,0:T(8,128)S(1)}, f32[72,128]{1,0:T(8,128)S(1)}, u32[]{:S(2)}, u32[]{:S(2)}) %collective-permute-start) | collective-permute-done | bytes 36896 | tf_op jit(solution)/shard_map/ppermute | solution.py:229
  27.0 0.0 collective-permute-done.11.refs_7_
  27.0 0.0 collective-permute-done.8.refs_4_
  27.0 0.0 collective-permute-done.9.refs_5_
  27.0 0.0 collective-permute-done.10.refs_6_
  27.0 0.9 %combine.1 = f32[2,32,128]{2,1,0:T(8,128)} custom-call(f32[72,128]{1,0:T(8,128)S(1)} %collective-permute-done.early, f32[148,128]{1,0:T(8,128)S(1)} %collective-permute-done.4.refs_0_, f32[148,128]{1,0:T(8,128)S(1)} %collective-permute-done.5.refs_1_, f32[148,128]{1,0:T(8,128)S(1)} %collective-permute-done.6.refs_2_, ...), custom_call_target="tpu_custom_call" | custom-call | tf_op jit(solution)/shard_map/combine/pallas_call | solution.py:262
Async XLA Ops:
  1.8 6.9 %collective-permute-start.1 = (f32[324,128]{1,0:T(8,128)S(1)}, f32[324,128]{1,0:T(8,128)S(1)}, u32[]{:S(2)}, u32[]{:S(2)}) collective-permute-start(f32[324,128]{1,0:T(8,128)S(1)} %get-tuple-element.15), channel_id=1, source_target_pairs={{0,1},{1,0},{2,3},{3,2},{4,5},{5,4},{6,7},{7,6},{8,9},{9,8},{10,11... | collective-permute-start | bytes 497672 | tf_op jit(solution)/shard_map/ppermute | solution.py:225
  2.4 4.1 %collective-permute-start.3 = (f32[36,128]{1,0:T(8,128)S(1)}, f32[36,128]{1,0:T(8,128)S(1)}, u32[]{:S(2)}, u32[]{:S(2)}) collective-permute-start(f32[36,128]{1,0:T(8,128)S(1)} %get-tuple-element.16.refs_0_), channel_id=1, source_target_pairs={{0,3},{1,2},{2,1},{3,0},{4,7},{5,6},{6,5},{7,4},{8,11},{9,10},{10,... | collective-permute-start | bytes 55304 | tf_op jit(solution)/shard_map/ppermute | solution.py:228
  5.0 3.8 %collective-permute-start.2 = (f32[36,128]{1,0:T(8,128)S(1)}, f32[36,128]{1,0:T(8,128)S(1)}, u32[]{:S(2)}, u32[]{:S(2)}) collective-permute-start(f32[36,128]{1,0:T(8,128)S(1)} %get-tuple-element.16.refs_0_), channel_id=1, source_target_pairs={{0,2},{1,3},{2,0},{3,1},{4,6},{5,7},{6,4},{7,5},{8,10},{9,11},{10,... | collective-permute-start | bytes 55304 | tf_op jit(solution)/shard_map/ppermute | solution.py:228
  9.0 5.1 %collective-permute-start.4 = (f32[148,128]{1,0:T(8,128)S(1)}, f32[148,128]{1,0:T(8,128)S(1)}, u32[]{:S(2)}, u32[]{:S(2)}) collective-permute-start(f32[148,128]{1,0:T(8,128)S(1)} %get-tuple-element.17), channel_id=1, source_target_pairs={{0,0},{1,5},{2,2},{3,7},{4,4},{5,1},{6,6},{7,3},{8,8},{9,13},{10,1... | collective-permute-start | bytes 227336 | tf_op jit(solution)/shard_map/ppermute | solution.py:252
  9.7 6.0 %collective-permute-start.5 = (f32[148,128]{1,0:T(8,128)S(1)}, f32[148,128]{1,0:T(8,128)S(1)}, u32[]{:S(2)}, u32[]{:S(2)}) collective-permute-start(f32[148,128]{1,0:T(8,128)S(1)} %get-tuple-element.18), channel_id=1, source_target_pairs={{0,8},{1,13},{2,10},{3,15},{4,12},{5,9},{6,14},{7,11},{8,0},{9,5},... | collective-permute-start | bytes 227336 | tf_op jit(solution)/shard_map/ppermute | solution.py:252
  11.3 5.3 %collective-permute-start.6 = (f32[148,128]{1,0:T(8,128)S(1)}, f32[148,128]{1,0:T(8,128)S(1)}, u32[]{:S(2)}, u32[]{:S(2)}) collective-permute-start(f32[148,128]{1,0:T(8,128)S(1)} %get-tuple-element.19), channel_id=1, source_target_pairs={{0,16},{1,21},{2,18},{3,23},{4,20},{5,17},{6,22},{7,19},{8,24},{9,... | collective-permute-start | bytes 227336 | tf_op jit(solution)/shard_map/ppermute | solution.py:252
  13.9 6.0 %collective-permute-start.7 = (f32[78,128]{1,0:T(8,128)S(1)}, f32[78,128]{1,0:T(8,128)S(1)}, u32[]{:S(2)}, u32[]{:S(2)}) collective-permute-start(f32[78,128]{1,0:T(8,128)S(1)} %get-tuple-element.20), channel_id=1, source_target_pairs={{0,24},{1,29},{2,26},{3,31},{4,28},{5,25},{6,30},{7,27},{8,16},{9,... | collective-permute-start | bytes 119816 | tf_op jit(solution)/shard_map/ppermute | solution.py:252
  14.2 12.8 %collective-permute-start.8 = (f32[148,128]{1,0:T(8,128)S(1)}, f32[148,128]{1,0:T(8,128)S(1)}, u32[]{:S(2)}, u32[]{:S(2)}) collective-permute-start(f32[148,128]{1,0:T(8,128)S(1)} %collective-permute-done.4.refs_0_), channel_id=1, source_target_pairs={{0,1},{1,0},{2,3},{3,2},{4,5},{5,4},{6,7},{7,6},{8,9},{9,8},{10,11... | collective-permute-start | bytes 227336 | tf_op jit(solution)/shard_map/ppermute | solution.py:253
  15.7 11.3 %collective-permute-start.9 = (f32[148,128]{1,0:T(8,128)S(1)}, f32[148,128]{1,0:T(8,128)S(1)}, u32[]{:S(2)}, u32[]{:S(2)}) collective-permute-start(f32[148,128]{1,0:T(8,128)S(1)} %collective-permute-done.5.refs_1_), channel_id=1, source_target_pairs={{0,1},{1,0},{2,3},{3,2},{4,5},{5,4},{6,7},{7,6},{8,9},{9,8},{10,11... | collective-permute-start | bytes 227336 | tf_op jit(solution)/shard_map/ppermute | solution.py:253
  16.6 10.4 %collective-permute-start.10 = (f32[148,128]{1,0:T(8,128)S(1)}, f32[148,128]{1,0:T(8,128)S(1)}, u32[]{:S(2)}, u32[]{:S(2)}) collective-permute-start(f32[148,128]{1,0:T(8,128)S(1)} %collective-permute-done.6.refs_2_), channel_id=1, source_target_pairs={{0,1},{1,0},{2,3},{3,2},{4,5},{5,4},{6,7},{7,6},{8,9},{9,8},{10,11... | collective-permute-start | bytes 227336 | tf_op jit(solution)/shard_map/ppermute | solution.py:253
  20.0 7.0 %collective-permute-start.11 = (f32[78,128]{1,0:T(8,128)S(1)}, f32[78,128]{1,0:T(8,128)S(1)}, u32[]{:S(2)}, u32[]{:S(2)}) collective-permute-start(f32[78,128]{1,0:T(8,128)S(1)} %collective-permute-done.7.refs_3_), channel_id=1, source_target_pairs={{0,1},{1,0},{2,3},{3,2},{4,5},{5,4},{6,7},{7,6},{8,9},{9,8},{10,11... | collective-permute-start | bytes 119816 | tf_op jit(solution)/shard_map/ppermute | solution.py:253
  21.2 5.8 %collective-permute-start = (f32[72,128]{1,0:T(8,128)S(1)}, f32[72,128]{1,0:T(8,128)S(1)}, u32[]{:S(2)}, u32[]{:S(2)}) collective-permute-start(f32[72,128]{1,0:T(8,128)S(1)} %get-tuple-element.13), channel_id=1, source_target_pairs={{0,24},{1,29},{2,26},{3,31},{4,28},{5,25},{6,30},{7,27},{8,16},{9,... | collective-permute-start | bytes 110600 | tf_op jit(solution)/shard_map/ppermute | solution.py:229

commit v6 on v5

--- a/solution.py
+++ b/solution.py
@@ -8,8 +8,11 @@
 from jax.sharding import PartitionSpec as P
 
 
+EARLY_ROUNDS = 1
+
+
 def partner_of(here, core, k):
-    return here ^ (2 * k + core)
+    return here ^ (2 * k + (core + k + k // 2) % 2)
 
 
 def local_filter_kernel(
@@ -73,14 +76,15 @@
             for j in range(own):
                 at = edges + (k * shots * own + s * own + j) * window
                 handed[at : at + window] = partial[s, r * own + j, pl.ds(starts[s], window)]
-    r = partner_of(mine, core, owners // 2 - 1)
-    for s in range(shots):
-        for j in range(own):
-            at = (s * own + j) * window
-            early[at : at + window] = partial[s, r * own + j, pl.ds(starts[s], window)]
-
-
-def finish_filter_kernel(partial, handed, messages, blocks, slabs_held, halo):
+    for k, block in early.items():
+        r = partner_of(mine, core, k)
+        for s in range(shots):
+            for j in range(own):
+                at = (s * own + j) * window
+                block[at : at + window] = partial[s, r * own + j, pl.ds(starts[s], window)]
+
+
+def finish_filter_kernel(ahead, partial, handed, messages, blocks, slabs_held, halo):
     shots, rows, cols, slab = partial.shape
     slabs = len(messages)
     edges, width = messages[0].shape
@@ -119,8 +123,7 @@
             r = partner_of(mine, here % 2, k)
             low = jnp.where(d > 0, slabs_held[below, pl.ds(owners + r, 1)], 0.0)
             high = jnp.where(d < slabs - 1, slabs_held[above, pl.ds(r, 1)], 0.0)
-            last = k == half - 1
-            if last and not whose:
+            if k in ahead and not whose:
                 blocks[k][0:1] = low
                 blocks[k][1:2] = high
                 continue
@@ -131,7 +134,7 @@
                     if whose:
                         at = edges + (k * shots * own + i) * window
                         value = handed[at : at + window]
-                        at = (2 if last else sent) + i * window
+                        at = (2 if k in ahead else sent) + i * window
                     else:
                         value = partial[s, r * own + j, pl.ds(starts[s], window)]
                         at = i * window
@@ -140,28 +143,28 @@
         blocks[k][blocks[k].shape[0] - 2 * shots :] = tail
 
 
-def combine_kernel(cells, total_shots, shots, parts, early, layers, stack, weights, halo):
+def combine_kernel(cells, total_shots, shots, parts, stack, weights, halo):
     own, cols, slab = stack.shape
     window = cols // 2 + 2
-    tails = [block.shape[0] - 2 * shots for block, _ in parts]
-    energy = jnp.concatenate([block[at : at + shots] for (block, _), at in zip(parts, tails)], axis=0)
+    tails = [block.shape[0] - 2 * shots for block, _, _ in parts]
+    energy = jnp.concatenate([part[0][at : at + shots] for part, at in zip(parts, tails)], axis=0)
     meansq = jnp.sum(energy, axis=1, keepdims=True) / cells
     peak = jnp.max(meansq, axis=0, keepdims=True)
     weight = (1.0 / math.sqrt(total_shots)) / jnp.sqrt(meansq + 0.5 * peak + 1.0)
     weights[...] = jnp.broadcast_to(weight, weights.shape)
     stack[...] = jnp.zeros(stack.shape, jnp.float32)
-    width = shots * own * cols
-    depth = lax.broadcasted_iota(jnp.int32, (slab, width), 0)
-    halo[...] = jnp.where(depth == 0, layers[0:1], jnp.where(depth == slab - 1, layers[1:2], 0.0)).T
-    for k, ((block, rows), tail) in enumerate(zip(parts, tails)):
+    depth = lax.broadcasted_iota(jnp.int32, (slab, shots * own * cols), 0)
+    for k, ((block, rows, early), tail) in enumerate(zip(parts, tails)):
+        if early is not None:
+            halo[k] = jnp.where(depth == 0, block[0:1], jnp.where(depth == slab - 1, block[1:2], 0.0)).T
         for s in range(shots):
             at = tail + shots + s
             start = jnp.max(block[at : at + 1]).astype(jnp.int32)
             scale = weights[k * shots + s : k * shots + s + 1]
             for j in range(own):
                 i = s * own + j
-                if rows is None:
-                    value = early[i * window : (i + 1) * window] - halo[pl.ds(i * cols + start, window)]
+                if early is not None:
+                    value = early[i * window : (i + 1) * window] - halo[k, pl.ds(i * cols + start, window)]
                 else:
                     value = block[rows + i * window : rows + (i + 1) * window]
                 stack[j, pl.ds(start, window)] += scale * value
@@ -189,16 +192,22 @@
     vmem = pl.BlockSpec(memory_space=pltpu.VMEM)
     hbm = pl.BlockSpec(memory_space=pltpu.HBM)
     params = pltpu.CompilerParams(vmem_limit_bytes=24 << 20)
-    partial, message, handed, early = pl.pallas_call(
-        local_filter_kernel,
+    ahead = range(half - EARLY_ROUNDS, half)
+
+    def local_body(aperture, correlation, illumination, partial, message, handed, *refs):
+        early = dict(zip(ahead, refs))
+        local_filter_kernel(aperture, correlation, illumination, partial, message, handed, early, *refs[len(ahead) :])
+
+    partial, message, handed, *early = pl.pallas_call(
+        local_body,
         out_shape=(
             pltpu.VMEM(correlation.shape, f32),
             pltpu.VMEM((edges, width), f32),
             pltpu.VMEM((edges + half * sent, width), f32),
-            pltpu.VMEM((sent, width), f32),
+            *(pltpu.VMEM((sent, width), f32) for _ in ahead),
         ),
         in_specs=[hbm, hbm, hbm],
-        out_specs=(vmem, vmem, vmem, vmem),
+        out_specs=(vmem,) * (3 + len(ahead)),
         scratch_shapes=[
             pltpu.VMEM((shots, rows + 2, cols, slab), f32),
             pltpu.VMEM(correlation.shape, f32),
@@ -226,18 +235,19 @@
             messages.append(message)
         else:
             messages.append(lax.ppermute(message, "depth", pairs))
-    early = lax.ppermute(early, ("shot", "depth"), round_pairs(half - 1))
+    for at, k in enumerate(ahead):
+        early[at] = lax.ppermute(early[at], ("shot", "depth"), round_pairs(k))
 
     def finish_body(partial, handed, *refs):
         finish_filter_kernel(
-            partial, handed, (refs[0], None) + refs[1 : slabs - 1], refs[slabs - 1 : slabs - 1 + half], *refs[slabs - 1 + half :]
+            ahead, partial, handed, (refs[0], None) + refs[1 : slabs - 1], refs[slabs - 1 : slabs - 1 + half], *refs[slabs - 1 + half :]
         )
 
     block = pltpu.VMEM((2 * sent + 2 * shots, slab), f32)
     light = pltpu.VMEM((2 + sent + 2 * shots, slab), f32)
     blocks = list(pl.pallas_call(
         finish_body,
-        out_shape=(block,) * (half - 1) + (light,),
+        out_shape=(block,) * (half - len(ahead)) + (light,) * len(ahead),
         in_specs=[vmem] * (1 + slabs),
         out_specs=(vmem,) * half,
         scratch_shapes=[
@@ -253,21 +263,22 @@
         passed.append(lax.ppermute(blocks[k], "depth", [(i, i ^ 1) for i in range(slabs)]))
     cells = rows * cols * slab * slabs
 
-    def combine_body(early, *refs):
-        ours, theirs = refs[:half], refs[half:owners]
-        parts = [(ref, None if k == half - 1 else 0) for k, ref in enumerate(ours)]
-        parts += [(ref, 2 if k == half - 1 else sent) for k, ref in enumerate(theirs)]
-        combine_kernel(cells, shots * owners, shots, parts, early, ours[half - 1], *refs[owners:])
+    def combine_body(*refs):
+        early = dict(zip(ahead, refs))
+        ours, theirs, rest = (refs[len(ahead) + at :] for at in (0, half, owners))
+        parts = [(ours[k], 0, early.get(k)) for k in range(half)]
+        parts += [(theirs[k], 2 if k in early else sent, None) for k in range(half)]
+        combine_kernel(cells, shots * owners, shots, parts, *rest)
 
     return pl.pallas_call(
         combine_body,
         out_shape=jax.ShapeDtypeStruct((own, cols, slab), f32),
-        in_specs=[vmem] * (1 + owners),
+        in_specs=[vmem] * (len(ahead) + owners),
         out_specs=vmem,
-        scratch_shapes=[pltpu.VMEM((owners * shots, slab), f32), pltpu.VMEM((width, slab), f32)],
+        scratch_shapes=[pltpu.VMEM((owners * shots, slab), f32), pltpu.VMEM((half, width, slab), f32)],
         compiler_params=params,
         name="combine",
-    )(*(in_vmem(v) for v in [early] + blocks + passed))
+    )(*(in_vmem(v) for v in early + blocks + passed))
 
 
 def solution(mesh):

time: 28 us -> 28.3 us (1.011)
  waiting for transfers between devices: 7.95 us -> 12.8 us
  starting transfers between devices: 16.9 us -> 12.4 us
    ppermute x4, starting transfers between devices: 6.51 us -> 0.63 us  [on_device(): lax.ppermute(blocks[k], 'depth', [(i, i ^ 1) for i in range(slabs)])]
    ppermute x4, waiting for transfers between devices: 0.57 us -> 5.48 us  [on_device(): blocks[k] = lax.ppermute(blocks[k], ('shot', 'depth'), round_pairs(k))]
    ppermute x4, starting transfers between devices: 5.12 us -> 6.02 us  [on_device(): blocks[k] = lax.ppermute(blocks[k], ('shot', 'depth'), round_pairs(k))]
    ppermute x1, starting transfers between devices: 2.13 us -> 2.56 us  [on_device(): early[at] = lax.ppermute(early[at], ('shot', 'depth'), round_pairs(k))]
  transfers between devices with their start and end apart: 12 -> 12, of which waited for: 4 -> 6; matrix products, arithmetic and copies ran while one was open for 0% -> 0% of each run, Pallas kernels for 0% -> 0%
where the time goes in v6:
time: 28.3 us; the launch traced here: 28.2 us
  waiting for transfers between devices  12.8 us (45%)
  starting transfers between devices  12.4 us (44%)
  Pallas kernels  2.95 us (10%)
    ppermute x4, starting transfers between devices, on_device(): blocks[k] = lax.ppermute(blocks[k], ('shot', 'depth'), round_pairs(k))  6.02 us
    ppermute x4, waiting for transfers between devices, on_device(): blocks[k] = lax.ppermute(blocks[k], ('shot', 'depth'), round_pairs(k))  5.48 us
    ppermute x2, waiting for transfers between devices, on_device(): messages.append(lax.ppermute(message, 'depth', pairs))  3.74 us
    ppermute x1, waiting for transfers between devices, on_device(): early[at] = lax.ppermute(early[at], ('shot', 'depth'), round_pairs(k))  3.55 us
    ppermute x2, starting transfers between devices, on_device(): messages.append(lax.ppermute(message, 'depth', pairs))  2.63 us
    ppermute x1, starting transfers between devices, on_device(): early[at] = lax.ppermute(early[at], ('shot', 'depth'), round_pairs(k))  2.56 us
    pallas_call x1, Pallas kernels, on_device(): pl.pallas_call(local_body, out_shape=(pltpu.VMEM(correlation.shape, f32),...  1.84 us
    pallas_call x1, Pallas kernels, on_device(): pl.pallas_call(combine_body, out_shape=jax.ShapeDtypeStruct((own, cols, s...  0.85 us
  transfers between devices with their start and end apart: 12, of which 6 were waited for; matrix products, arithmetic and copies ran while one was open for 0% of the time, Pallas kernels for 0%

profile of v6, /device:TPU:0, one launch (start us, length us, event | category | flops | bytes accessed | tf_op | source)
XLA Modules:
  0.0 28.2 jit_solution(9587859484476085594)
XLA Ops:
  0.0 1.8 %local_filter.1 = (f32[2,16,32,128]{3,2,1,0:T(8,128)S(1)}, f32[36,128]{1,0:T(8,128)S(1)}, f32[324,128]{1,0:T(8,128)S(1)}, f32[72,128]{1,0:T(8,128)S(1)}) custom-call(s32[2,4]{1,0:T(2,128)} %aperture.1, f32[2,16,32,128]{3,2,1,0:T(8,128)} %correlation.1, f32[2,16,32,128]{3,2,1,0:T(8,128)} %illumination.1), custom_call_target="tpu_custom_call" | custom-call | tf_op jit(solution)/shard_map/local_filter/pallas_call | solution.py:201
  1.8 0.6 %collective-permute-start.1 = (f32[324,128]{1,0:T(8,128)S(1)}, f32[324,128]{1,0:T(8,128)S(1)}, u32[]{:S(2)}, u32[]{:S(2)}) collective-permute-start(f32[324,128]{1,0:T(8,128)S(1)} %get-tuple-element.15), channel_id=1, source_target_pairs={{0,1},{1,0},{2,3},{3,2},{4,5},{5,4},{6,7},{7,6},{8,9},{9,8},{10,11... | collective-permute-start | bytes 497672 | tf_op jit(solution)/shard_map/ppermute | solution.py:234
  2.4 2.6 %collective-permute-start.3 = (f32[36,128]{1,0:T(8,128)S(1)}, f32[36,128]{1,0:T(8,128)S(1)}, u32[]{:S(2)}, u32[]{:S(2)}) collective-permute-start(f32[36,128]{1,0:T(8,128)S(1)} %get-tuple-element.16.refs_0_), channel_id=1, source_target_pairs={{0,3},{1,2},{2,1},{3,0},{4,7},{5,6},{6,5},{7,4},{8,11},{9,10},{10,... | collective-permute-start | bytes 55304 | tf_op jit(solution)/shard_map/ppermute | solution.py:237
  5.0 0.0 collective-permute-start.2
  5.0 1.4 %collective-permute-done.3.refs_2_ = f32[36,128]{1,0:T(8,128)S(1)} collective-permute-done((f32[36,128]{1,0:T(8,128)S(1)}, f32[36,128]{1,0:T(8,128)S(1)}, u32[]{:S(2)}, u32[]{:S(2)}) %collective-permute-start.3) | collective-permute-done | bytes 18464 | tf_op jit(solution)/shard_map/ppermute | solution.py:237
  6.5 2.3 %collective-permute-done.2.refs_1_ = f32[36,128]{1,0:T(8,128)S(1)} collective-permute-done((f32[36,128]{1,0:T(8,128)S(1)}, f32[36,128]{1,0:T(8,128)S(1)}, u32[]{:S(2)}, u32[]{:S(2)}) %collective-permute-start.2) | collective-permute-done | bytes 18464 | tf_op jit(solution)/shard_map/ppermute | solution.py:237
  8.8 0.0 collective-permute-done.1.handed
  8.8 0.3 finish_filter.1
  9.0 0.7 %collective-permute-start.4 = (f32[148,128]{1,0:T(8,128)S(1)}, f32[148,128]{1,0:T(8,128)S(1)}, u32[]{:S(2)}, u32[]{:S(2)}) collective-permute-start(f32[148,128]{1,0:T(8,128)S(1)} %get-tuple-element.17), channel_id=1, source_target_pairs={{0,0},{1,5},{2,2},{3,7},{4,4},{5,1},{6,6},{7,3},{8,8},{9,13},{10,1... | collective-permute-start | bytes 227336 | tf_op jit(solution)/shard_map/ppermute | solution.py:262
  9.7 2.6 %collective-permute-start.5 = (f32[148,128]{1,0:T(8,128)S(1)}, f32[148,128]{1,0:T(8,128)S(1)}, u32[]{:S(2)}, u32[]{:S(2)}) collective-permute-start(f32[148,128]{1,0:T(8,128)S(1)} %get-tuple-element.18), channel_id=1, source_target_pairs={{0,12},{1,9},{2,14},{3,11},{4,8},{5,13},{6,10},{7,15},{8,4},{9,1},... | collective-permute-start | bytes 227336 | tf_op jit(solution)/shard_map/ppermute | solution.py:262
  12.3 2.5 %collective-permute-start.6 = (f32[148,128]{1,0:T(8,128)S(1)}, f32[148,128]{1,0:T(8,128)S(1)}, u32[]{:S(2)}, u32[]{:S(2)}) collective-permute-start(f32[148,128]{1,0:T(8,128)S(1)} %get-tuple-element.19), channel_id=1, source_target_pairs={{0,20},{1,17},{2,22},{3,19},{4,16},{5,21},{6,18},{7,23},{8,28},{9,... | collective-permute-start | bytes 227336 | tf_op jit(solution)/shard_map/ppermute | solution.py:262
  14.8 0.2 collective-permute-start.7
  15.1 0.0 collective-permute-done.4.refs_1_
  15.1 0.0 collective-permute-start.8
  15.1 0.3 %collective-permute-done.5.refs_2_ = f32[148,128]{1,0:T(8,128)S(1)} collective-permute-done((f32[148,128]{1,0:T(8,128)S(1)}, f32[148,128]{1,0:T(8,128)S(1)}, u32[]{:S(2)}, u32[]{:S(2)}) %collective-permute-start.5) | collective-permute-done | bytes 75808 | tf_op jit(solution)/shard_map/ppermute | solution.py:262
  15.4 0.2 collective-permute-start.9
  15.6 5.1 %collective-permute-done.6.refs_3_ = f32[148,128]{1,0:T(8,128)S(1)} collective-permute-done((f32[148,128]{1,0:T(8,128)S(1)}, f32[148,128]{1,0:T(8,128)S(1)}, u32[]{:S(2)}, u32[]{:S(2)}) %collective-permute-start.6) | collective-permute-done | bytes 75808 | tf_op jit(solution)/shard_map/ppermute | solution.py:262
  20.7 0.0 collective-permute-start.10
  20.7 0.1 collective-permute-done.7.refs_4_
  20.7 0.4 %collective-permute-start.11 = (f32[78,128]{1,0:T(8,128)S(1)}, f32[78,128]{1,0:T(8,128)S(1)}, u32[]{:S(2)}, u32[]{:S(2)}) collective-permute-start(f32[78,128]{1,0:T(8,128)S(1)} %collective-permute-done.7.refs_4_), channel_id=1, source_target_pairs={{0,1},{1,0},{2,3},{3,2},{4,5},{5,4},{6,7},{7,6},{8,9},{9,8},{10,11... | collective-permute-start | bytes 119816 | tf_op jit(solution)/shard_map/ppermute | solution.py:263
  21.2 2.6 %collective-permute-start = (f32[72,128]{1,0:T(8,128)S(1)}, f32[72,128]{1,0:T(8,128)S(1)}, u32[]{:S(2)}, u32[]{:S(2)}) collective-permute-start(f32[72,128]{1,0:T(8,128)S(1)} %get-tuple-element.13), channel_id=1, source_target_pairs={{0,24},{1,29},{2,26},{3,31},{4,28},{5,25},{6,30},{7,27},{8,16},{9,... | collective-permute-start | bytes 110600 | tf_op jit(solution)/shard_map/ppermute | solution.py:239
  23.7 3.5 %collective-permute-done.refs_0_ = f32[72,128]{1,0:T(8,128)S(1)} collective-permute-done((f32[72,128]{1,0:T(8,128)S(1)}, f32[72,128]{1,0:T(8,128)S(1)}, u32[]{:S(2)}, u32[]{:S(2)}) %collective-permute-start) | collective-permute-done | bytes 36896 | tf_op jit(solution)/shard_map/ppermute | solution.py:239
  27.3 0.0 collective-permute-done.11.refs_8_
  27.3 0.0 collective-permute-done.8.refs_5_
  27.3 0.0 collective-permute-done.9.refs_6_
  27.3 0.0 collective-permute-done.10.refs_7_
  27.3 0.9 %combine.1 = f32[2,32,128]{2,1,0:T(8,128)} custom-call(f32[72,128]{1,0:T(8,128)S(1)} %collective-permute-done.refs_0_, f32[148,128]{1,0:T(8,128)S(1)} %collective-permute-done.4.refs_1_, f32[148,128]{1,0:T(8,128)S(1)} %collective-permute-done.5.refs_2_, f32[148,128]{1,0:T(8,128)S(1)} %collective-permute-done.6.refs_3_, ...), custom_call_target="tpu_custom_call" | custom-call | tf_op jit(solution)/shard_map/combine/pallas_call | solution.py:273
Async XLA Ops:
  1.8 6.9 %collective-permute-start.1 = (f32[324,128]{1,0:T(8,128)S(1)}, f32[324,128]{1,0:T(8,128)S(1)}, u32[]{:S(2)}, u32[]{:S(2)}) collective-permute-start(f32[324,128]{1,0:T(8,128)S(1)} %get-tuple-element.15), channel_id=1, source_target_pairs={{0,1},{1,0},{2,3},{3,2},{4,5},{5,4},{6,7},{7,6},{8,9},{9,8},{10,11... | collective-permute-start | bytes 497672 | tf_op jit(solution)/shard_map/ppermute | solution.py:234
  2.4 4.1 %collective-permute-start.3 = (f32[36,128]{1,0:T(8,128)S(1)}, f32[36,128]{1,0:T(8,128)S(1)}, u32[]{:S(2)}, u32[]{:S(2)}) collective-permute-start(f32[36,128]{1,0:T(8,128)S(1)} %get-tuple-element.16.refs_0_), channel_id=1, source_target_pairs={{0,3},{1,2},{2,1},{3,0},{4,7},{5,6},{6,5},{7,4},{8,11},{9,10},{10,... | collective-permute-start | bytes 55304 | tf_op jit(solution)/shard_map/ppermute | solution.py:237
  5.0 3.8 %collective-permute-start.2 = (f32[36,128]{1,0:T(8,128)S(1)}, f32[36,128]{1,0:T(8,128)S(1)}, u32[]{:S(2)}, u32[]{:S(2)}) collective-permute-start(f32[36,128]{1,0:T(8,128)S(1)} %get-tuple-element.16.refs_0_), channel_id=1, source_target_pairs={{0,2},{1,3},{2,0},{3,1},{4,6},{5,7},{6,4},{7,5},{8,10},{9,11},{10,... | collective-permute-start | bytes 55304 | tf_op jit(solution)/shard_map/ppermute | solution.py:237
  9.0 6.0 %collective-permute-start.4 = (f32[148,128]{1,0:T(8,128)S(1)}, f32[148,128]{1,0:T(8,128)S(1)}, u32[]{:S(2)}, u32[]{:S(2)}) collective-permute-start(f32[148,128]{1,0:T(8,128)S(1)} %get-tuple-element.17), channel_id=1, source_target_pairs={{0,0},{1,5},{2,2},{3,7},{4,4},{5,1},{6,6},{7,3},{8,8},{9,13},{10,1... | collective-permute-start | bytes 227336 | tf_op jit(solution)/shard_map/ppermute | solution.py:262
  9.7 5.7 %collective-permute-start.5 = (f32[148,128]{1,0:T(8,128)S(1)}, f32[148,128]{1,0:T(8,128)S(1)}, u32[]{:S(2)}, u32[]{:S(2)}) collective-permute-start(f32[148,128]{1,0:T(8,128)S(1)} %get-tuple-element.18), channel_id=1, source_target_pairs={{0,12},{1,9},{2,14},{3,11},{4,8},{5,13},{6,10},{7,15},{8,4},{9,1},... | collective-permute-start | bytes 227336 | tf_op jit(solution)/shard_map/ppermute | solution.py:262
  12.3 8.4 %collective-permute-start.6 = (f32[148,128]{1,0:T(8,128)S(1)}, f32[148,128]{1,0:T(8,128)S(1)}, u32[]{:S(2)}, u32[]{:S(2)}) collective-permute-start(f32[148,128]{1,0:T(8,128)S(1)} %get-tuple-element.19), channel_id=1, source_target_pairs={{0,20},{1,17},{2,22},{3,19},{4,16},{5,21},{6,18},{7,23},{8,28},{9,... | collective-permute-start | bytes 227336 | tf_op jit(solution)/shard_map/ppermute | solution.py:262
  14.8 5.9 %collective-permute-start.7 = (f32[78,128]{1,0:T(8,128)S(1)}, f32[78,128]{1,0:T(8,128)S(1)}, u32[]{:S(2)}, u32[]{:S(2)}) collective-permute-start(f32[78,128]{1,0:T(8,128)S(1)} %get-tuple-element.20), channel_id=1, source_target_pairs={{0,24},{1,29},{2,26},{3,31},{4,28},{5,25},{6,30},{7,27},{8,16},{9,... | collective-permute-start | bytes 119816 | tf_op jit(solution)/shard_map/ppermute | solution.py:262
  15.1 12.2 %collective-permute-start.8 = (f32[148,128]{1,0:T(8,128)S(1)}, f32[148,128]{1,0:T(8,128)S(1)}, u32[]{:S(2)}, u32[]{:S(2)}) collective-permute-start(f32[148,128]{1,0:T(8,128)S(1)} %collective-permute-done.4.refs_1_), channel_id=1, source_target_pairs={{0,1},{1,0},{2,3},{3,2},{4,5},{5,4},{6,7},{7,6},{8,9},{9,8},{10,11... | collective-permute-start | bytes 227336 | tf_op jit(solution)/shard_map/ppermute | solution.py:263
  15.4 11.9 %collective-permute-start.9 = (f32[148,128]{1,0:T(8,128)S(1)}, f32[148,128]{1,0:T(8,128)S(1)}, u32[]{:S(2)}, u32[]{:S(2)}) collective-permute-start(f32[148,128]{1,0:T(8,128)S(1)} %collective-permute-done.5.refs_2_), channel_id=1, source_target_pairs={{0,1},{1,0},{2,3},{3,2},{4,5},{5,4},{6,7},{7,6},{8,9},{9,8},{10,11... | collective-permute-start | bytes 227336 | tf_op jit(solution)/shard_map/ppermute | solution.py:263
  20.7 6.6 %collective-permute-start.10 = (f32[148,128]{1,0:T(8,128)S(1)}, f32[148,128]{1,0:T(8,128)S(1)}, u32[]{:S(2)}, u32[]{:S(2)}) collective-permute-start(f32[148,128]{1,0:T(8,128)S(1)} %collective-permute-done.6.refs_3_), channel_id=1, source_target_pairs={{0,1},{1,0},{2,3},{3,2},{4,5},{5,4},{6,7},{7,6},{8,9},{9,8},{10,11... | collective-permute-start | bytes 227336 | tf_op jit(solution)/shard_map/ppermute | solution.py:263
  20.7 6.6 %collective-permute-start.11 = (f32[78,128]{1,0:T(8,128)S(1)}, f32[78,128]{1,0:T(8,128)S(1)}, u32[]{:S(2)}, u32[]{:S(2)}) collective-permute-start(f32[78,128]{1,0:T(8,128)S(1)} %collective-permute-done.7.refs_4_), channel_id=1, source_target_pairs={{0,1},{1,0},{2,3},{3,2},{4,5},{5,4},{6,7},{7,6},{8,9},{9,8},{10,11... | collective-permute-start | bytes 119816 | tf_op jit(solution)/shard_map/ppermute | solution.py:263
  21.2 6.1 %collective-permute-start = (f32[72,128]{1,0:T(8,128)S(1)}, f32[72,128]{1,0:T(8,128)S(1)}, u32[]{:S(2)}, u32[]{:S(2)}) collective-permute-start(f32[72,128]{1,0:T(8,128)S(1)} %get-tuple-element.13), channel_id=1, source_target_pairs={{0,24},{1,29},{2,26},{3,31},{4,28},{5,25},{6,30},{7,27},{8,16},{9,... | collective-permute-start | bytes 110600 | tf_op jit(solution)/shard_map/ppermute | solution.py:239

commit v7 on v6

--- a/solution.py
+++ b/solution.py
@@ -36,23 +36,26 @@
     second = lax.broadcasted_iota(jnp.int32, (cols, slab), 0)
     lane = lax.broadcasted_iota(jnp.int32, (cols, slab), 1)
     zero = jnp.zeros((cols, slab), jnp.float32)
+    rim = jnp.zeros((cols + 16, slab), jnp.float32)
     boxes.wait()
     starts = [jnp.clip(aperture[s, 2] - 1, 0, cols - window) for s in range(shots)]
     for s in range(shots):
-        padded[s, 0] = zero
-        padded[s, rows + 1] = zero
+        padded[s, 0] = rim
+        padded[s, rows + 1] = rim
+        for x in range(rows):
+            padded[s, x + 1, 0:8] = rim[0:8]
+            padded[s, x + 1, cols + 8 : cols + 16] = rim[0:8]
         for copy in copies[s]:
             copy.wait()
         in_cols = (second >= aperture[s, 2]) & (second < aperture[s, 3])
         for x in range(rows):
             keep = in_cols & (x >= aperture[s, 0]) & (x < aperture[s, 1])
-            padded[s, x + 1] = jnp.where(keep, correlation[s, x] / (illumination[s, x] + 0.1), 0.0)
+            padded[s, x + 1, 8 : cols + 8] = jnp.where(keep, correlation[s, x] / (illumination[s, x] + 0.1), 0.0)
         total = zero
         for x in range(rows):
-            n = padded[s, x + 1]
-            beside = padded[s, x] + padded[s, x + 2]
-            beside += jnp.where(second == 0, 0.0, pltpu.roll(n, 1, 0))
-            beside += jnp.where(second == cols - 1, 0.0, pltpu.roll(n, cols - 1, 0))
+            n = padded[s, x + 1, 8 : cols + 8]
+            beside = padded[s, x, 8 : cols + 8] + padded[s, x + 2, 8 : cols + 8]
+            beside += padded[s, x + 1, 7 : cols + 7] + padded[s, x + 1, 9 : cols + 9]
             beside += jnp.where(lane == 0, 0.0, pltpu.roll(n, 1, 1))
             beside += jnp.where(lane == slab - 1, 0.0, pltpu.roll(n, slab - 1, 1))
             value = 6.0 * n - beside
@@ -62,8 +65,8 @@
         at = 4 * owners + shots + s
         message[at : at + 1] = jnp.full((1, slab), starts[s].astype(jnp.float32))
     for r in range(owners):
-        for at, image, shift in ((0, padded, 1), (2 * owners, partial, 0)):
-            held = [image[s, r * own + j + shift] for s in range(shots) for j in range(own)]
+        for at, image, shift, top in ((0, padded, 1, 8), (2 * owners, partial, 0, 0)):
+            held = [image[s, r * own + j + shift, top : top + cols] for s in range(shots) for j in range(own)]
             turned = jnp.concatenate(held, axis=0).T
             message[at + r : at + r + 1] = turned[0:1]
             message[at + owners + r : at + owners + r + 1] = turned[slab - 1 : slab]
@@ -209,7 +212,7 @@
         in_specs=[hbm, hbm, hbm],
         out_specs=(vmem,) * (3 + len(ahead)),
         scratch_shapes=[
-            pltpu.VMEM((shots, rows + 2, cols, slab), f32),
+            pltpu.VMEM((shots, rows + 2, cols + 16, slab), f32),
             pltpu.VMEM(correlation.shape, f32),
             pltpu.VMEM(correlation.shape, f32),
             pltpu.SMEM(aperture.shape, aperture.dtype),

time: 28.3 us -> 28.3 us (level)
  no operation moved by 1% of the time
where the time goes in v7:
time: 28.3 us; the launch traced here: 28.2 us
  waiting for transfers between devices  12.8 us (45%)
  starting transfers between devices  12.4 us (44%)
  Pallas kernels  2.94 us (10%)
    ppermute x4, starting transfers between devices, on_device(): blocks[k] = lax.ppermute(blocks[k], ('shot', 'depth'), round_pairs(k))  6.02 us
    ppermute x4, waiting for transfers between devices, on_device(): blocks[k] = lax.ppermute(blocks[k], ('shot', 'depth'), round_pairs(k))  5.48 us
    ppermute x2, waiting for transfers between devices, on_device(): messages.append(lax.ppermute(message, 'depth', pairs))  3.74 us
    ppermute x1, waiting for transfers between devices, on_device(): early[at] = lax.ppermute(early[at], ('shot', 'depth'), round_pairs(k))  3.55 us
    ppermute x2, starting transfers between devices, on_device(): messages.append(lax.ppermute(message, 'depth', pairs))  2.63 us
    ppermute x1, starting transfers between devices, on_device(): early[at] = lax.ppermute(early[at], ('shot', 'depth'), round_pairs(k))  2.56 us
    pallas_call x1, Pallas kernels, on_device(): pl.pallas_call(local_body, out_shape=(pltpu.VMEM(correlation.shape, f32),...  1.83 us
    pallas_call x1, Pallas kernels, on_device(): pl.pallas_call(combine_body, out_shape=jax.ShapeDtypeStruct((own, cols, s...  0.85 us
  transfers between devices with their start and end apart: 12, of which 6 were waited for; matrix products, arithmetic and copies ran while one was open for 0% of the time, Pallas kernels for 0%

profile of v7, /device:TPU:0, one launch (start us, length us, event | category | flops | bytes accessed | tf_op | source)
XLA Modules:
  0.0 28.2 jit_solution(16211363025479011107)
XLA Ops:
  0.0 1.8 %local_filter.1 = (f32[2,16,32,128]{3,2,1,0:T(8,128)S(1)}, f32[36,128]{1,0:T(8,128)S(1)}, f32[324,128]{1,0:T(8,128)S(1)}, f32[72,128]{1,0:T(8,128)S(1)}) custom-call(s32[2,4]{1,0:T(2,128)} %aperture.1, f32[2,16,32,128]{3,2,1,0:T(8,128)} %correlation.1, f32[2,16,32,128]{3,2,1,0:T(8,128)} %illumination.1), custom_call_target="tpu_custom_call" | custom-call | tf_op jit(solution)/shard_map/local_filter/pallas_call | solution.py:204
  1.8 0.6 %collective-permute-start.1 = (f32[324,128]{1,0:T(8,128)S(1)}, f32[324,128]{1,0:T(8,128)S(1)}, u32[]{:S(2)}, u32[]{:S(2)}) collective-permute-start(f32[324,128]{1,0:T(8,128)S(1)} %get-tuple-element.15), channel_id=1, source_target_pairs={{0,1},{1,0},{2,3},{3,2},{4,5},{5,4},{6,7},{7,6},{8,9},{9,8},{10,11... | collective-permute-start | bytes 497672 | tf_op jit(solution)/shard_map/ppermute | solution.py:237
  2.4 2.6 %collective-permute-start.3 = (f32[36,128]{1,0:T(8,128)S(1)}, f32[36,128]{1,0:T(8,128)S(1)}, u32[]{:S(2)}, u32[]{:S(2)}) collective-permute-start(f32[36,128]{1,0:T(8,128)S(1)} %get-tuple-element.16.refs_0_), channel_id=1, source_target_pairs={{0,3},{1,2},{2,1},{3,0},{4,7},{5,6},{6,5},{7,4},{8,11},{9,10},{10,... | collective-permute-start | bytes 55304 | tf_op jit(solution)/shard_map/ppermute | solution.py:240
  5.0 0.0 collective-permute-start.2
  5.0 1.4 %collective-permute-done.3.refs_2_ = f32[36,128]{1,0:T(8,128)S(1)} collective-permute-done((f32[36,128]{1,0:T(8,128)S(1)}, f32[36,128]{1,0:T(8,128)S(1)}, u32[]{:S(2)}, u32[]{:S(2)}) %collective-permute-start.3) | collective-permute-done | bytes 18464 | tf_op jit(solution)/shard_map/ppermute | solution.py:240
  6.5 2.3 %collective-permute-done.2.refs_1_ = f32[36,128]{1,0:T(8,128)S(1)} collective-permute-done((f32[36,128]{1,0:T(8,128)S(1)}, f32[36,128]{1,0:T(8,128)S(1)}, u32[]{:S(2)}, u32[]{:S(2)}) %collective-permute-start.2) | collective-permute-done | bytes 18464 | tf_op jit(solution)/shard_map/ppermute | solution.py:240
  8.8 0.0 collective-permute-done.1.handed
  8.8 0.3 finish_filter.1
  9.0 0.7 %collective-permute-start.4 = (f32[148,128]{1,0:T(8,128)S(1)}, f32[148,128]{1,0:T(8,128)S(1)}, u32[]{:S(2)}, u32[]{:S(2)}) collective-permute-start(f32[148,128]{1,0:T(8,128)S(1)} %get-tuple-element.17), channel_id=1, source_target_pairs={{0,0},{1,5},{2,2},{3,7},{4,4},{5,1},{6,6},{7,3},{8,8},{9,13},{10,1... | collective-permute-start | bytes 227336 | tf_op jit(solution)/shard_map/ppermute | solution.py:265
  9.7 2.6 %collective-permute-start.5 = (f32[148,128]{1,0:T(8,128)S(1)}, f32[148,128]{1,0:T(8,128)S(1)}, u32[]{:S(2)}, u32[]{:S(2)}) collective-permute-start(f32[148,128]{1,0:T(8,128)S(1)} %get-tuple-element.18), channel_id=1, source_target_pairs={{0,12},{1,9},{2,14},{3,11},{4,8},{5,13},{6,10},{7,15},{8,4},{9,1},... | collective-permute-start | bytes 227336 | tf_op jit(solution)/shard_map/ppermute | solution.py:265
  12.3 2.5 %collective-permute-start.6 = (f32[148,128]{1,0:T(8,128)S(1)}, f32[148,128]{1,0:T(8,128)S(1)}, u32[]{:S(2)}, u32[]{:S(2)}) collective-permute-start(f32[148,128]{1,0:T(8,128)S(1)} %get-tuple-element.19), channel_id=1, source_target_pairs={{0,20},{1,17},{2,22},{3,19},{4,16},{5,21},{6,18},{7,23},{8,28},{9,... | collective-permute-start | bytes 227336 | tf_op jit(solution)/shard_map/ppermute | solution.py:265
  14.8 0.2 collective-permute-start.7
  15.1 0.0 collective-permute-done.4.refs_1_
  15.1 0.0 collective-permute-start.8
  15.1 0.3 %collective-permute-done.5.refs_2_ = f32[148,128]{1,0:T(8,128)S(1)} collective-permute-done((f32[148,128]{1,0:T(8,128)S(1)}, f32[148,128]{1,0:T(8,128)S(1)}, u32[]{:S(2)}, u32[]{:S(2)}) %collective-permute-start.5) | collective-permute-done | bytes 75808 | tf_op jit(solution)/shard_map/ppermute | solution.py:265
  15.4 0.2 collective-permute-start.9
  15.6 5.1 %collective-permute-done.6.refs_3_ = f32[148,128]{1,0:T(8,128)S(1)} collective-permute-done((f32[148,128]{1,0:T(8,128)S(1)}, f32[148,128]{1,0:T(8,128)S(1)}, u32[]{:S(2)}, u32[]{:S(2)}) %collective-permute-start.6) | collective-permute-done | bytes 75808 | tf_op jit(solution)/shard_map/ppermute | solution.py:265
  20.7 0.0 collective-permute-start.10
  20.7 0.1 collective-permute-done.7.refs_4_
  20.7 0.4 %collective-permute-start.11 = (f32[78,128]{1,0:T(8,128)S(1)}, f32[78,128]{1,0:T(8,128)S(1)}, u32[]{:S(2)}, u32[]{:S(2)}) collective-permute-start(f32[78,128]{1,0:T(8,128)S(1)} %collective-permute-done.7.refs_4_), channel_id=1, source_target_pairs={{0,1},{1,0},{2,3},{3,2},{4,5},{5,4},{6,7},{7,6},{8,9},{9,8},{10,11... | collective-permute-start | bytes 119816 | tf_op jit(solution)/shard_map/ppermute | solution.py:266
  21.2 2.6 %collective-permute-start = (f32[72,128]{1,0:T(8,128)S(1)}, f32[72,128]{1,0:T(8,128)S(1)}, u32[]{:S(2)}, u32[]{:S(2)}) collective-permute-start(f32[72,128]{1,0:T(8,128)S(1)} %get-tuple-element.13), channel_id=1, source_target_pairs={{0,24},{1,29},{2,26},{3,31},{4,28},{5,25},{6,30},{7,27},{8,16},{9,... | collective-permute-start | bytes 110600 | tf_op jit(solution)/shard_map/ppermute | solution.py:242
  23.7 3.5 %collective-permute-done.refs_0_ = f32[72,128]{1,0:T(8,128)S(1)} collective-permute-done((f32[72,128]{1,0:T(8,128)S(1)}, f32[72,128]{1,0:T(8,128)S(1)}, u32[]{:S(2)}, u32[]{:S(2)}) %collective-permute-start) | collective-permute-done | bytes 36896 | tf_op jit(solution)/shard_map/ppermute | solution.py:242
  27.3 0.0 collective-permute-done.11.refs_8_
  27.3 0.0 collective-permute-done.8.refs_5_
  27.3 0.0 collective-permute-done.9.refs_6_
  27.3 0.0 collective-permute-done.10.refs_7_
  27.3 0.9 %combine.1 = f32[2,32,128]{2,1,0:T(8,128)} custom-call(f32[72,128]{1,0:T(8,128)S(1)} %collective-permute-done.refs_0_, f32[148,128]{1,0:T(8,128)S(1)} %collective-permute-done.4.refs_1_, f32[148,128]{1,0:T(8,128)S(1)} %collective-permute-done.5.refs_2_, f32[148,128]{1,0:T(8,128)S(1)} %collective-permute-done.6.refs_3_, ...), custom_call_target="tpu_custom_call" | custom-call | tf_op jit(solution)/shard_map/combine/pallas_call | solution.py:276
Async XLA Ops:
  1.8 6.9 %collective-permute-start.1 = (f32[324,128]{1,0:T(8,128)S(1)}, f32[324,128]{1,0:T(8,128)S(1)}, u32[]{:S(2)}, u32[]{:S(2)}) collective-permute-start(f32[324,128]{1,0:T(8,128)S(1)} %get-tuple-element.15), channel_id=1, source_target_pairs={{0,1},{1,0},{2,3},{3,2},{4,5},{5,4},{6,7},{7,6},{8,9},{9,8},{10,11... | collective-permute-start | bytes 497672 | tf_op jit(solution)/shard_map/ppermute | solution.py:237
  2.4 4.1 %collective-permute-start.3 = (f32[36,128]{1,0:T(8,128)S(1)}, f32[36,128]{1,0:T(8,128)S(1)}, u32[]{:S(2)}, u32[]{:S(2)}) collective-permute-start(f32[36,128]{1,0:T(8,128)S(1)} %get-tuple-element.16.refs_0_), channel_id=1, source_target_pairs={{0,3},{1,2},{2,1},{3,0},{4,7},{5,6},{6,5},{7,4},{8,11},{9,10},{10,... | collective-permute-start | bytes 55304 | tf_op jit(solution)/shard_map/ppermute | solution.py:240
  5.0 3.8 %collective-permute-start.2 = (f32[36,128]{1,0:T(8,128)S(1)}, f32[36,128]{1,0:T(8,128)S(1)}, u32[]{:S(2)}, u32[]{:S(2)}) collective-permute-start(f32[36,128]{1,0:T(8,128)S(1)} %get-tuple-element.16.refs_0_), channel_id=1, source_target_pairs={{0,2},{1,3},{2,0},{3,1},{4,6},{5,7},{6,4},{7,5},{8,10},{9,11},{10,... | collective-permute-start | bytes 55304 | tf_op jit(solution)/shard_map/ppermute | solution.py:240
  9.0 6.0 %collective-permute-start.4 = (f32[148,128]{1,0:T(8,128)S(1)}, f32[148,128]{1,0:T(8,128)S(1)}, u32[]{:S(2)}, u32[]{:S(2)}) collective-permute-start(f32[148,128]{1,0:T(8,128)S(1)} %get-tuple-element.17), channel_id=1, source_target_pairs={{0,0},{1,5},{2,2},{3,7},{4,4},{5,1},{6,6},{7,3},{8,8},{9,13},{10,1... | collective-permute-start | bytes 227336 | tf_op jit(solution)/shard_map/ppermute | solution.py:265
  9.7 5.7 %collective-permute-start.5 = (f32[148,128]{1,0:T(8,128)S(1)}, f32[148,128]{1,0:T(8,128)S(1)}, u32[]{:S(2)}, u32[]{:S(2)}) collective-permute-start(f32[148,128]{1,0:T(8,128)S(1)} %get-tuple-element.18), channel_id=1, source_target_pairs={{0,12},{1,9},{2,14},{3,11},{4,8},{5,13},{6,10},{7,15},{8,4},{9,1},... | collective-permute-start | bytes 227336 | tf_op jit(solution)/shard_map/ppermute | solution.py:265
  12.3 8.4 %collective-permute-start.6 = (f32[148,128]{1,0:T(8,128)S(1)}, f32[148,128]{1,0:T(8,128)S(1)}, u32[]{:S(2)}, u32[]{:S(2)}) collective-permute-start(f32[148,128]{1,0:T(8,128)S(1)} %get-tuple-element.19), channel_id=1, source_target_pairs={{0,20},{1,17},{2,22},{3,19},{4,16},{5,21},{6,18},{7,23},{8,28},{9,... | collective-permute-start | bytes 227336 | tf_op jit(solution)/shard_map/ppermute | solution.py:265
  14.8 5.9 %collective-permute-start.7 = (f32[78,128]{1,0:T(8,128)S(1)}, f32[78,128]{1,0:T(8,128)S(1)}, u32[]{:S(2)}, u32[]{:S(2)}) collective-permute-start(f32[78,128]{1,0:T(8,128)S(1)} %get-tuple-element.20), channel_id=1, source_target_pairs={{0,24},{1,29},{2,26},{3,31},{4,28},{5,25},{6,30},{7,27},{8,16},{9,... | collective-permute-start | bytes 119816 | tf_op jit(solution)/shard_map/ppermute | solution.py:265
  15.1 12.2 %collective-permute-start.8 = (f32[148,128]{1,0:T(8,128)S(1)}, f32[148,128]{1,0:T(8,128)S(1)}, u32[]{:S(2)}, u32[]{:S(2)}) collective-permute-start(f32[148,128]{1,0:T(8,128)S(1)} %collective-permute-done.4.refs_1_), channel_id=1, source_target_pairs={{0,1},{1,0},{2,3},{3,2},{4,5},{5,4},{6,7},{7,6},{8,9},{9,8},{10,11... | collective-permute-start | bytes 227336 | tf_op jit(solution)/shard_map/ppermute | solution.py:266
  15.4 11.9 %collective-permute-start.9 = (f32[148,128]{1,0:T(8,128)S(1)}, f32[148,128]{1,0:T(8,128)S(1)}, u32[]{:S(2)}, u32[]{:S(2)}) collective-permute-start(f32[148,128]{1,0:T(8,128)S(1)} %collective-permute-done.5.refs_2_), channel_id=1, source_target_pairs={{0,1},{1,0},{2,3},{3,2},{4,5},{5,4},{6,7},{7,6},{8,9},{9,8},{10,11... | collective-permute-start | bytes 227336 | tf_op jit(solution)/shard_map/ppermute | solution.py:266
  20.7 6.6 %collective-permute-start.10 = (f32[148,128]{1,0:T(8,128)S(1)}, f32[148,128]{1,0:T(8,128)S(1)}, u32[]{:S(2)}, u32[]{:S(2)}) collective-permute-start(f32[148,128]{1,0:T(8,128)S(1)} %collective-permute-done.6.refs_3_), channel_id=1, source_target_pairs={{0,1},{1,0},{2,3},{3,2},{4,5},{5,4},{6,7},{7,6},{8,9},{9,8},{10,11... | collective-permute-start | bytes 227336 | tf_op jit(solution)/shard_map/ppermute | solution.py:266
  20.7 6.6 %collective-permute-start.11 = (f32[78,128]{1,0:T(8,128)S(1)}, f32[78,128]{1,0:T(8,128)S(1)}, u32[]{:S(2)}, u32[]{:S(2)}) collective-permute-start(f32[78,128]{1,0:T(8,128)S(1)} %collective-permute-done.7.refs_4_), channel_id=1, source_target_pairs={{0,1},{1,0},{2,3},{3,2},{4,5},{5,4},{6,7},{7,6},{8,9},{9,8},{10,11... | collective-permute-start | bytes 119816 | tf_op jit(solution)/shard_map/ppermute | solution.py:266
  21.2 6.1 %collective-permute-start = (f32[72,128]{1,0:T(8,128)S(1)}, f32[72,128]{1,0:T(8,128)S(1)}, u32[]{:S(2)}, u32[]{:S(2)}) collective-permute-start(f32[72,128]{1,0:T(8,128)S(1)} %get-tuple-element.13), channel_id=1, source_target_pairs={{0,24},{1,29},{2,26},{3,31},{4,28},{5,25},{6,30},{7,27},{8,16},{9,... | collective-permute-start | bytes 110600 | tf_op jit(solution)/shard_map/ppermute | solution.py:242

commit v8 on v7

--- a/solution.py
+++ b/solution.py
@@ -6,9 +6,6 @@
 from jax.experimental import pallas as pl
 from jax.experimental.pallas import tpu as pltpu
 from jax.sharding import PartitionSpec as P
-
-
-EARLY_ROUNDS = 1
 
 
 def partner_of(here, core, k):
@@ -195,7 +192,7 @@
     vmem = pl.BlockSpec(memory_space=pltpu.VMEM)
     hbm = pl.BlockSpec(memory_space=pltpu.HBM)
     params = pltpu.CompilerParams(vmem_limit_bytes=24 << 20)
-    ahead = range(half - EARLY_ROUNDS, half)
+    ahead = early_rounds(owners)
 
     def local_body(aperture, correlation, illumination, partial, message, handed, *refs):
         early = dict(zip(ahead, refs))
@@ -250,7 +247,7 @@
     light = pltpu.VMEM((2 + sent + 2 * shots, slab), f32)
     blocks = list(pl.pallas_call(
         finish_body,
-        out_shape=(block,) * (half - len(ahead)) + (light,) * len(ahead),
+        out_shape=tuple(light if k in ahead else block for k in range(half)),
         in_specs=[vmem] * (1 + slabs),
         out_specs=(vmem,) * half,
         scratch_shapes=[
@@ -284,6 +281,10 @@
     )(*(in_vmem(v) for v in early + blocks + passed))
 
 
+def early_rounds(owners):
+    return (owners // 2 - 2,)
+
+
 def solution(mesh):
     return jax.shard_map(
         on_device,

time: 28.3 us -> 28.5 us (level)
  waiting for transfers between devices: 12.8 us -> 14.4 us
  starting transfers between devices: 12.4 us -> 10.9 us
    ppermute x1, waiting for transfers between devices: 3.55 us -> 4.47 us  [on_device(): early[at] = lax.ppermute(early[at], ('shot', 'depth'), round_pairs(k))]
    ppermute x1, starting transfers between devices: 2.56 us -> 1.86 us  [on_device(): early[at] = lax.ppermute(early[at], ('shot', 'depth'), round_pairs(k))]
    ppermute x4, waiting for transfers between devices: 5.48 us -> 6.18 us  [on_device(): blocks[k] = lax.ppermute(blocks[k], ('shot', 'depth'), round_pairs(k))]
    ppermute x4, starting transfers between devices: 0.63 us -> 0.08 us  [on_device(): lax.ppermute(blocks[k], 'depth', [(i, i ^ 1) for i in range(slabs)])]
where the time goes in v8:
time: 28.5 us; the launch traced here: 28.3 us
  waiting for transfers between devices  14.4 us (51%)
  starting transfers between devices  10.9 us (38%)
  Pallas kernels  2.94 us (10%)
    ppermute x4, waiting for transfers between devices, on_device(): blocks[k] = lax.ppermute(blocks[k], ('shot', 'depth'), round_pairs(k))  6.18 us
    ppermute x4, starting transfers between devices, on_device(): blocks[k] = lax.ppermute(blocks[k], ('shot', 'depth'), round_pairs(k))  5.8 us
    ppermute x1, waiting for transfers between devices, on_device(): early[at] = lax.ppermute(early[at], ('shot', 'depth'), round_pairs(k))  4.47 us
    ppermute x2, waiting for transfers between devices, on_device(): messages.append(lax.ppermute(message, 'depth', pairs))  3.74 us
    ppermute x2, starting transfers between devices, on_device(): messages.append(lax.ppermute(message, 'depth', pairs))  2.63 us
    ppermute x1, starting transfers between devices, on_device(): early[at] = lax.ppermute(early[at], ('shot', 'depth'), round_pairs(k))  1.86 us
    pallas_call x1, Pallas kernels, on_device(): pl.pallas_call(local_body, out_shape=(pltpu.VMEM(correlation.shape, f32),...  1.83 us
    pallas_call x1, Pallas kernels, on_device(): pl.pallas_call(combine_body, out_shape=jax.ShapeDtypeStruct((own, cols, s...  0.86 us
  transfers between devices with their start and end apart: 12, of which 6 were waited for; matrix products, arithmetic and copies ran while one was open for 0% of the time, Pallas kernels for 0%

profile of v8, /device:TPU:0, one launch (start us, length us, event | category | flops | bytes accessed | tf_op | source)
XLA Modules:
  0.0 28.3 jit_solution(12103926390399056128)
XLA Ops:
  0.0 1.8 %local_filter.1 = (f32[2,16,32,128]{3,2,1,0:T(8,128)S(1)}, f32[36,128]{1,0:T(8,128)S(1)}, f32[324,128]{1,0:T(8,128)S(1)}, f32[72,128]{1,0:T(8,128)S(1)}) custom-call(s32[2,4]{1,0:T(2,128)} %aperture.1, f32[2,16,32,128]{3,2,1,0:T(8,128)} %correlation.1, f32[2,16,32,128]{3,2,1,0:T(8,128)} %illumination.1), custom_call_target="tpu_custom_call" | custom-call | tf_op jit(solution)/shard_map/local_filter/pallas_call | solution.py:201
  1.8 0.6 %collective-permute-start.1 = (f32[324,128]{1,0:T(8,128)S(1)}, f32[324,128]{1,0:T(8,128)S(1)}, u32[]{:S(2)}, u32[]{:S(2)}) collective-permute-start(f32[324,128]{1,0:T(8,128)S(1)} %get-tuple-element.15), channel_id=1, source_target_pairs={{0,1},{1,0},{2,3},{3,2},{4,5},{5,4},{6,7},{7,6},{8,9},{9,8},{10,11... | collective-permute-start | bytes 497672 | tf_op jit(solution)/shard_map/ppermute | solution.py:234
  2.4 2.6 %collective-permute-start.3 = (f32[36,128]{1,0:T(8,128)S(1)}, f32[36,128]{1,0:T(8,128)S(1)}, u32[]{:S(2)}, u32[]{:S(2)}) collective-permute-start(f32[36,128]{1,0:T(8,128)S(1)} %get-tuple-element.16.refs_0_), channel_id=1, source_target_pairs={{0,3},{1,2},{2,1},{3,0},{4,7},{5,6},{6,5},{7,4},{8,11},{9,10},{10,... | collective-permute-start | bytes 55304 | tf_op jit(solution)/shard_map/ppermute | solution.py:237
  5.0 0.0 collective-permute-start.2
  5.0 1.4 %collective-permute-done.3.refs_2_ = f32[36,128]{1,0:T(8,128)S(1)} collective-permute-done((f32[36,128]{1,0:T(8,128)S(1)}, f32[36,128]{1,0:T(8,128)S(1)}, u32[]{:S(2)}, u32[]{:S(2)}) %collective-permute-start.3) | collective-permute-done | bytes 18464 | tf_op jit(solution)/shard_map/ppermute | solution.py:237
  6.5 2.3 %collective-permute-done.2.refs_1_ = f32[36,128]{1,0:T(8,128)S(1)} collective-permute-done((f32[36,128]{1,0:T(8,128)S(1)}, f32[36,128]{1,0:T(8,128)S(1)}, u32[]{:S(2)}, u32[]{:S(2)}) %collective-permute-start.2) | collective-permute-done | bytes 18464 | tf_op jit(solution)/shard_map/ppermute | solution.py:237
  8.8 0.0 collective-permute-done.1.handed
  8.8 0.3 finish_filter.1
  9.0 0.7 %collective-permute-start.4 = (f32[148,128]{1,0:T(8,128)S(1)}, f32[148,128]{1,0:T(8,128)S(1)}, u32[]{:S(2)}, u32[]{:S(2)}) collective-permute-start(f32[148,128]{1,0:T(8,128)S(1)} %get-tuple-element.17), channel_id=1, source_target_pairs={{0,0},{1,5},{2,2},{3,7},{4,4},{5,1},{6,6},{7,3},{8,8},{9,13},{10,1... | collective-permute-start | bytes 227336 | tf_op jit(solution)/shard_map/ppermute | solution.py:262
  9.7 2.6 %collective-permute-start.5 = (f32[148,128]{1,0:T(8,128)S(1)}, f32[148,128]{1,0:T(8,128)S(1)}, u32[]{:S(2)}, u32[]{:S(2)}) collective-permute-start(f32[148,128]{1,0:T(8,128)S(1)} %get-tuple-element.18), channel_id=1, source_target_pairs={{0,12},{1,9},{2,14},{3,11},{4,8},{5,13},{6,10},{7,15},{8,4},{9,1},... | collective-permute-start | bytes 227336 | tf_op jit(solution)/shard_map/ppermute | solution.py:262
  12.3 2.5 %collective-permute-start.7 = (f32[148,128]{1,0:T(8,128)S(1)}, f32[148,128]{1,0:T(8,128)S(1)}, u32[]{:S(2)}, u32[]{:S(2)}) collective-permute-start(f32[148,128]{1,0:T(8,128)S(1)} %get-tuple-element.20), channel_id=1, source_target_pairs={{0,24},{1,29},{2,26},{3,31},{4,28},{5,25},{6,30},{7,27},{8,16},{9,... | collective-permute-start | bytes 227336 | tf_op jit(solution)/shard_map/ppermute | solution.py:262
  14.8 0.1 collective-permute-start.6
  14.8 0.0 collective-permute-done.4.refs_1_
  14.8 0.0 collective-permute-start.8
  14.8 0.5 %collective-permute-done.5.refs_2_ = f32[148,128]{1,0:T(8,128)S(1)} collective-permute-done((f32[148,128]{1,0:T(8,128)S(1)}, f32[148,128]{1,0:T(8,128)S(1)}, u32[]{:S(2)}, u32[]{:S(2)}) %collective-permute-start.5) | collective-permute-done | bytes 75808 | tf_op jit(solution)/shard_map/ppermute | solution.py:262
  15.4 0.0 collective-permute-start.9
  15.4 4.3 %collective-permute-done.7.refs_4_ = f32[148,128]{1,0:T(8,128)S(1)} collective-permute-done((f32[148,128]{1,0:T(8,128)S(1)}, f32[148,128]{1,0:T(8,128)S(1)}, u32[]{:S(2)}, u32[]{:S(2)}) %collective-permute-start.7) | collective-permute-done | bytes 75808 | tf_op jit(solution)/shard_map/ppermute | solution.py:262
  19.7 0.0 collective-permute-start.11
  19.7 1.4 %collective-permute-done.6.refs_3_ = f32[78,128]{1,0:T(8,128)S(1)} collective-permute-done((f32[78,128]{1,0:T(8,128)S(1)}, f32[78,128]{1,0:T(8,128)S(1)}, u32[]{:S(2)}, u32[]{:S(2)}) %collective-permute-start.6) | collective-permute-done | bytes 39968 | tf_op jit(solution)/shard_map/ppermute | solution.py:262
  21.0 0.1 collective-permute-start.10
  21.1 1.9 %collective-permute-start = (f32[72,128]{1,0:T(8,128)S(1)}, f32[72,128]{1,0:T(8,128)S(1)}, u32[]{:S(2)}, u32[]{:S(2)}) collective-permute-start(f32[72,128]{1,0:T(8,128)S(1)} %get-tuple-element.13), channel_id=1, source_target_pairs={{0,20},{1,17},{2,22},{3,19},{4,16},{5,21},{6,18},{7,23},{8,28},{9,... | collective-permute-start | bytes 110600 | tf_op jit(solution)/shard_map/ppermute | solution.py:239
  23.0 4.5 %collective-permute-done.refs_0_ = f32[72,128]{1,0:T(8,128)S(1)} collective-permute-done((f32[72,128]{1,0:T(8,128)S(1)}, f32[72,128]{1,0:T(8,128)S(1)}, u32[]{:S(2)}, u32[]{:S(2)}) %collective-permute-start) | collective-permute-done | bytes 36896 | tf_op jit(solution)/shard_map/ppermute | solution.py:239
  27.4 0.0 collective-permute-done.10.refs_7_
  27.4 0.0 collective-permute-done.8.refs_5_
  27.4 0.0 collective-permute-done.9.refs_6_
  27.5 0.0 collective-permute-done.11.refs_8_
  27.5 0.9 %combine.1 = f32[2,32,128]{2,1,0:T(8,128)} custom-call(f32[72,128]{1,0:T(8,128)S(1)} %collective-permute-done.refs_0_, f32[148,128]{1,0:T(8,128)S(1)} %collective-permute-done.4.refs_1_, f32[148,128]{1,0:T(8,128)S(1)} %collective-permute-done.5.refs_2_, f32[78,128]{1,0:T(8,128)S(1)} %collective-permute-done.6.refs_3_, ...), custom_call_target="tpu_custom_call" | custom-call | tf_op jit(solution)/shard_map/combine/pallas_call | solution.py:273
Async XLA Ops:
  1.8 6.9 %collective-permute-start.1 = (f32[324,128]{1,0:T(8,128)S(1)}, f32[324,128]{1,0:T(8,128)S(1)}, u32[]{:S(2)}, u32[]{:S(2)}) collective-permute-start(f32[324,128]{1,0:T(8,128)S(1)} %get-tuple-element.15), channel_id=1, source_target_pairs={{0,1},{1,0},{2,3},{3,2},{4,5},{5,4},{6,7},{7,6},{8,9},{9,8},{10,11... | collective-permute-start | bytes 497672 | tf_op jit(solution)/shard_map/ppermute | solution.py:234
  2.4 4.1 %collective-permute-start.3 = (f32[36,128]{1,0:T(8,128)S(1)}, f32[36,128]{1,0:T(8,128)S(1)}, u32[]{:S(2)}, u32[]{:S(2)}) collective-permute-start(f32[36,128]{1,0:T(8,128)S(1)} %get-tuple-element.16.refs_0_), channel_id=1, source_target_pairs={{0,3},{1,2},{2,1},{3,0},{4,7},{5,6},{6,5},{7,4},{8,11},{9,10},{10,... | collective-permute-start | bytes 55304 | tf_op jit(solution)/shard_map/ppermute | solution.py:237
  5.0 3.8 %collective-permute-start.2 = (f32[36,128]{1,0:T(8,128)S(1)}, f32[36,128]{1,0:T(8,128)S(1)}, u32[]{:S(2)}, u32[]{:S(2)}) collective-permute-start(f32[36,128]{1,0:T(8,128)S(1)} %get-tuple-element.16.refs_0_), channel_id=1, source_target_pairs={{0,2},{1,3},{2,0},{3,1},{4,6},{5,7},{6,4},{7,5},{8,10},{9,11},{10,... | collective-permute-start | bytes 55304 | tf_op jit(solution)/shard_map/ppermute | solution.py:237
  9.0 5.8 %collective-permute-start.4 = (f32[148,128]{1,0:T(8,128)S(1)}, f32[148,128]{1,0:T(8,128)S(1)}, u32[]{:S(2)}, u32[]{:S(2)}) collective-permute-start(f32[148,128]{1,0:T(8,128)S(1)} %get-tuple-element.17), channel_id=1, source_target_pairs={{0,0},{1,5},{2,2},{3,7},{4,4},{5,1},{6,6},{7,3},{8,8},{9,13},{10,1... | collective-permute-start | bytes 227336 | tf_op jit(solution)/shard_map/ppermute | solution.py:262
  9.7 5.7 %collective-permute-start.5 = (f32[148,128]{1,0:T(8,128)S(1)}, f32[148,128]{1,0:T(8,128)S(1)}, u32[]{:S(2)}, u32[]{:S(2)}) collective-permute-start(f32[148,128]{1,0:T(8,128)S(1)} %get-tuple-element.18), channel_id=1, source_target_pairs={{0,12},{1,9},{2,14},{3,11},{4,8},{5,13},{6,10},{7,15},{8,4},{9,1},... | collective-permute-start | bytes 227336 | tf_op jit(solution)/shard_map/ppermute | solution.py:262
  12.3 7.4 %collective-permute-start.7 = (f32[148,128]{1,0:T(8,128)S(1)}, f32[148,128]{1,0:T(8,128)S(1)}, u32[]{:S(2)}, u32[]{:S(2)}) collective-permute-start(f32[148,128]{1,0:T(8,128)S(1)} %get-tuple-element.20), channel_id=1, source_target_pairs={{0,24},{1,29},{2,26},{3,31},{4,28},{5,25},{6,30},{7,27},{8,16},{9,... | collective-permute-start | bytes 227336 | tf_op jit(solution)/shard_map/ppermute | solution.py:262
  14.8 6.3 %collective-permute-start.6 = (f32[78,128]{1,0:T(8,128)S(1)}, f32[78,128]{1,0:T(8,128)S(1)}, u32[]{:S(2)}, u32[]{:S(2)}) collective-permute-start(f32[78,128]{1,0:T(8,128)S(1)} %get-tuple-element.19), channel_id=1, source_target_pairs={{0,20},{1,17},{2,22},{3,19},{4,16},{5,21},{6,18},{7,23},{8,28},{9,... | collective-permute-start | bytes 119816 | tf_op jit(solution)/shard_map/ppermute | solution.py:262
  14.8 12.6 %collective-permute-start.8 = (f32[148,128]{1,0:T(8,128)S(1)}, f32[148,128]{1,0:T(8,128)S(1)}, u32[]{:S(2)}, u32[]{:S(2)}) collective-permute-start(f32[148,128]{1,0:T(8,128)S(1)} %collective-permute-done.4.refs_1_), channel_id=1, source_target_pairs={{0,1},{1,0},{2,3},{3,2},{4,5},{5,4},{6,7},{7,6},{8,9},{9,8},{10,11... | collective-permute-start | bytes 227336 | tf_op jit(solution)/shard_map/ppermute | solution.py:263
  15.4 12.1 %collective-permute-start.9 = (f32[148,128]{1,0:T(8,128)S(1)}, f32[148,128]{1,0:T(8,128)S(1)}, u32[]{:S(2)}, u32[]{:S(2)}) collective-permute-start(f32[148,128]{1,0:T(8,128)S(1)} %collective-permute-done.5.refs_2_), channel_id=1, source_target_pairs={{0,1},{1,0},{2,3},{3,2},{4,5},{5,4},{6,7},{7,6},{8,9},{9,8},{10,11... | collective-permute-start | bytes 227336 | tf_op jit(solution)/shard_map/ppermute | solution.py:263
  19.7 7.8 %collective-permute-start.11 = (f32[148,128]{1,0:T(8,128)S(1)}, f32[148,128]{1,0:T(8,128)S(1)}, u32[]{:S(2)}, u32[]{:S(2)}) collective-permute-start(f32[148,128]{1,0:T(8,128)S(1)} %collective-permute-done.7.refs_4_), channel_id=1, source_target_pairs={{0,1},{1,0},{2,3},{3,2},{4,5},{5,4},{6,7},{7,6},{8,9},{9,8},{10,11... | collective-permute-start | bytes 227336 | tf_op jit(solution)/shard_map/ppermute | solution.py:263
  21.0 6.4 %collective-permute-start.10 = (f32[78,128]{1,0:T(8,128)S(1)}, f32[78,128]{1,0:T(8,128)S(1)}, u32[]{:S(2)}, u32[]{:S(2)}) collective-permute-start(f32[78,128]{1,0:T(8,128)S(1)} %collective-permute-done.6.refs_3_), channel_id=1, source_target_pairs={{0,1},{1,0},{2,3},{3,2},{4,5},{5,4},{6,7},{7,6},{8,9},{9,8},{10,11... | collective-permute-start | bytes 119816 | tf_op jit(solution)/shard_map/ppermute | solution.py:263
  21.1 6.3 %collective-permute-start = (f32[72,128]{1,0:T(8,128)S(1)}, f32[72,128]{1,0:T(8,128)S(1)}, u32[]{:S(2)}, u32[]{:S(2)}) collective-permute-start(f32[72,128]{1,0:T(8,128)S(1)} %get-tuple-element.13), channel_id=1, source_target_pairs={{0,20},{1,17},{2,22},{3,19},{4,16},{5,21},{6,18},{7,23},{8,28},{9,... | collective-permute-start | bytes 110600 | tf_op jit(solution)/shard_map/ppermute | solution.py:239

commit v9 on v8

--- a/solution.py
+++ b/solution.py
@@ -143,7 +143,7 @@
         blocks[k][blocks[k].shape[0] - 2 * shots :] = tail
 
 
-def combine_kernel(cells, total_shots, shots, parts, stack, weights, halo):
+def combine_kernel(cells, total_shots, shots, parts, stack, weights, halo, sums):
     own, cols, slab = stack.shape
     window = cols // 2 + 2
     tails = [block.shape[0] - 2 * shots for block, _, _ in parts]
@@ -152,7 +152,7 @@
     peak = jnp.max(meansq, axis=0, keepdims=True)
     weight = (1.0 / math.sqrt(total_shots)) / jnp.sqrt(meansq + 0.5 * peak + 1.0)
     weights[...] = jnp.broadcast_to(weight, weights.shape)
-    stack[...] = jnp.zeros(stack.shape, jnp.float32)
+    sums[...] = jnp.zeros(sums.shape, jnp.float32)
     depth = lax.broadcasted_iota(jnp.int32, (slab, shots * own * cols), 0)
     for k, ((block, rows, early), tail) in enumerate(zip(parts, tails)):
         if early is not None:
@@ -167,7 +167,8 @@
                     value = early[i * window : (i + 1) * window] - halo[k, pl.ds(i * cols + start, window)]
                 else:
                     value = block[rows + i * window : rows + (i + 1) * window]
-                stack[j, pl.ds(start, window)] += scale * value
+                sums[k % 2, s, j, pl.ds(start, window)] += scale * value
+    stack[...] = jnp.sum(sums[...], axis=(0, 1))
 
 
 def in_hbm(array):
@@ -275,7 +276,9 @@
         out_shape=jax.ShapeDtypeStruct((own, cols, slab), f32),
         in_specs=[vmem] * (len(ahead) + owners),
         out_specs=vmem,
-        scratch_shapes=[pltpu.VMEM((owners * shots, slab), f32), pltpu.VMEM((half, width, slab), f32)],
+        scratch_shapes=[pltpu.VMEM((owners * shots, slab), f32), pltpu.VMEM((half, width, slab), f32),
+            pltpu.VMEM((2, shots, own, cols, slab), f32),
+        ],
         compiler_params=params,
         name="combine",
     )(*(in_vmem(v) for v in early + blocks + passed))

time: 28.5 us -> 28.4 us (level)
  no operation moved by 1% of the time
where the time goes in v9:
time: 28.4 us; the launch traced here: 28.3 us
  waiting for transfers between devices  14.4 us (51%)
  starting transfers between devices  10.9 us (38%)
  Pallas kernels  2.91 us (10%)
    ppermute x4, waiting for transfers between devices, on_device(): blocks[k] = lax.ppermute(blocks[k], ('shot', 'depth'), round_pairs(k))  6.18 us
    ppermute x4, starting transfers between devices, on_device(): blocks[k] = lax.ppermute(blocks[k], ('shot', 'depth'), round_pairs(k))  5.8 us
    ppermute x1, waiting for transfers between devices, on_device(): early[at] = lax.ppermute(early[at], ('shot', 'depth'), round_pairs(k))  4.47 us
    ppermute x2, waiting for transfers between devices, on_device(): messages.append(lax.ppermute(message, 'depth', pairs))  3.74 us
    ppermute x2, starting transfers between devices, on_device(): messages.append(lax.ppermute(message, 'depth', pairs))  2.63 us
    ppermute x1, starting transfers between devices, on_device(): early[at] = lax.ppermute(early[at], ('shot', 'depth'), round_pairs(k))  1.86 us
    pallas_call x1, Pallas kernels, on_device(): pl.pallas_call(local_body, out_shape=(pltpu.VMEM(correlation.shape, f32),...  1.83 us
    pallas_call x1, Pallas kernels, on_device(): pl.pallas_call(combine_body, out_shape=jax.ShapeDtypeStruct((own, cols, s...  0.82 us
  transfers between devices with their start and end apart: 12, of which 6 were waited for; matrix products, arithmetic and copies ran while one was open for 0% of the time, Pallas kernels for 0%

profile of v9, /device:TPU:0, one launch (start us, length us, event | category | flops | bytes accessed | tf_op | source)
XLA Modules:
  0.0 28.3 jit_solution(7171058829373012945)
XLA Ops:
  0.0 1.8 %local_filter.1 = (f32[2,16,32,128]{3,2,1,0:T(8,128)S(1)}, f32[36,128]{1,0:T(8,128)S(1)}, f32[324,128]{1,0:T(8,128)S(1)}, f32[72,128]{1,0:T(8,128)S(1)}) custom-call(s32[2,4]{1,0:T(2,128)} %aperture.1, f32[2,16,32,128]{3,2,1,0:T(8,128)} %correlation.1, f32[2,16,32,128]{3,2,1,0:T(8,128)} %illumination.1), custom_call_target="tpu_custom_call" | custom-call | tf_op jit(solution)/shard_map/local_filter/pallas_call | solution.py:202
  1.8 0.6 %collective-permute-start.1 = (f32[324,128]{1,0:T(8,128)S(1)}, f32[324,128]{1,0:T(8,128)S(1)}, u32[]{:S(2)}, u32[]{:S(2)}) collective-permute-start(f32[324,128]{1,0:T(8,128)S(1)} %get-tuple-element.15), channel_id=1, source_target_pairs={{0,1},{1,0},{2,3},{3,2},{4,5},{5,4},{6,7},{7,6},{8,9},{9,8},{10,11... | collective-permute-start | bytes 497672 | tf_op jit(solution)/shard_map/ppermute | solution.py:235
  2.4 2.6 %collective-permute-start.3 = (f32[36,128]{1,0:T(8,128)S(1)}, f32[36,128]{1,0:T(8,128)S(1)}, u32[]{:S(2)}, u32[]{:S(2)}) collective-permute-start(f32[36,128]{1,0:T(8,128)S(1)} %get-tuple-element.16.refs_0_), channel_id=1, source_target_pairs={{0,3},{1,2},{2,1},{3,0},{4,7},{5,6},{6,5},{7,4},{8,11},{9,10},{10,... | collective-permute-start | bytes 55304 | tf_op jit(solution)/shard_map/ppermute | solution.py:238
  5.0 0.0 collective-permute-start.2
  5.0 1.4 %collective-permute-done.3.refs_2_ = f32[36,128]{1,0:T(8,128)S(1)} collective-permute-done((f32[36,128]{1,0:T(8,128)S(1)}, f32[36,128]{1,0:T(8,128)S(1)}, u32[]{:S(2)}, u32[]{:S(2)}) %collective-permute-start.3) | collective-permute-done | bytes 18464 | tf_op jit(solution)/shard_map/ppermute | solution.py:238
  6.5 2.3 %collective-permute-done.2.refs_1_ = f32[36,128]{1,0:T(8,128)S(1)} collective-permute-done((f32[36,128]{1,0:T(8,128)S(1)}, f32[36,128]{1,0:T(8,128)S(1)}, u32[]{:S(2)}, u32[]{:S(2)}) %collective-permute-start.2) | collective-permute-done | bytes 18464 | tf_op jit(solution)/shard_map/ppermute | solution.py:238
  8.8 0.0 collective-permute-done.1.handed
  8.8 0.3 finish_filter.1
  9.0 0.7 %collective-permute-start.4 = (f32[148,128]{1,0:T(8,128)S(1)}, f32[148,128]{1,0:T(8,128)S(1)}, u32[]{:S(2)}, u32[]{:S(2)}) collective-permute-start(f32[148,128]{1,0:T(8,128)S(1)} %get-tuple-element.17), channel_id=1, source_target_pairs={{0,0},{1,5},{2,2},{3,7},{4,4},{5,1},{6,6},{7,3},{8,8},{9,13},{10,1... | collective-permute-start | bytes 227336 | tf_op jit(solution)/shard_map/ppermute | solution.py:263
  9.7 2.6 %collective-permute-start.5 = (f32[148,128]{1,0:T(8,128)S(1)}, f32[148,128]{1,0:T(8,128)S(1)}, u32[]{:S(2)}, u32[]{:S(2)}) collective-permute-start(f32[148,128]{1,0:T(8,128)S(1)} %get-tuple-element.18), channel_id=1, source_target_pairs={{0,12},{1,9},{2,14},{3,11},{4,8},{5,13},{6,10},{7,15},{8,4},{9,1},... | collective-permute-start | bytes 227336 | tf_op jit(solution)/shard_map/ppermute | solution.py:263
  12.3 2.5 %collective-permute-start.7 = (f32[148,128]{1,0:T(8,128)S(1)}, f32[148,128]{1,0:T(8,128)S(1)}, u32[]{:S(2)}, u32[]{:S(2)}) collective-permute-start(f32[148,128]{1,0:T(8,128)S(1)} %get-tuple-element.20), channel_id=1, source_target_pairs={{0,24},{1,29},{2,26},{3,31},{4,28},{5,25},{6,30},{7,27},{8,16},{9,... | collective-permute-start | bytes 227336 | tf_op jit(solution)/shard_map/ppermute | solution.py:263
  14.8 0.1 collective-permute-start.6
  14.8 0.0 collective-permute-done.4.refs_1_
  14.8 0.0 collective-permute-start.8
  14.8 0.5 %collective-permute-done.5.refs_2_ = f32[148,128]{1,0:T(8,128)S(1)} collective-permute-done((f32[148,128]{1,0:T(8,128)S(1)}, f32[148,128]{1,0:T(8,128)S(1)}, u32[]{:S(2)}, u32[]{:S(2)}) %collective-permute-start.5) | collective-permute-done | bytes 75808 | tf_op jit(solution)/shard_map/ppermute | solution.py:263
  15.4 0.0 collective-permute-start.9
  15.4 4.3 %collective-permute-done.7.refs_4_ = f32[148,128]{1,0:T(8,128)S(1)} collective-permute-done((f32[148,128]{1,0:T(8,128)S(1)}, f32[148,128]{1,0:T(8,128)S(1)}, u32[]{:S(2)}, u32[]{:S(2)}) %collective-permute-start.7) | collective-permute-done | bytes 75808 | tf_op jit(solution)/shard_map/ppermute | solution.py:263
  19.7 0.0 collective-permute-start.11
  19.7 1.4 %collective-permute-done.6.refs_3_ = f32[78,128]{1,0:T(8,128)S(1)} collective-permute-done((f32[78,128]{1,0:T(8,128)S(1)}, f32[78,128]{1,0:T(8,128)S(1)}, u32[]{:S(2)}, u32[]{:S(2)}) %collective-permute-start.6) | collective-permute-done | bytes 39968 | tf_op jit(solution)/shard_map/ppermute | solution.py:263
  21.0 0.1 collective-permute-start.10
  21.1 1.9 %collective-permute-start = (f32[72,128]{1,0:T(8,128)S(1)}, f32[72,128]{1,0:T(8,128)S(1)}, u32[]{:S(2)}, u32[]{:S(2)}) collective-permute-start(f32[72,128]{1,0:T(8,128)S(1)} %get-tuple-element.13), channel_id=1, source_target_pairs={{0,20},{1,17},{2,22},{3,19},{4,16},{5,21},{6,18},{7,23},{8,28},{9,... | collective-permute-start | bytes 110600 | tf_op jit(solution)/shard_map/ppermute | solution.py:240
  23.0 4.5 %collective-permute-done.refs_0_ = f32[72,128]{1,0:T(8,128)S(1)} collective-permute-done((f32[72,128]{1,0:T(8,128)S(1)}, f32[72,128]{1,0:T(8,128)S(1)}, u32[]{:S(2)}, u32[]{:S(2)}) %collective-permute-start) | collective-permute-done | bytes 36896 | tf_op jit(solution)/shard_map/ppermute | solution.py:240
  27.4 0.0 collective-permute-done.10.refs_7_
  27.4 0.0 collective-permute-done.8.refs_5_
  27.4 0.0 collective-permute-done.9.refs_6_
  27.5 0.0 collective-permute-done.11.refs_8_
  27.5 0.8 %combine.1 = f32[2,32,128]{2,1,0:T(8,128)} custom-call(f32[72,128]{1,0:T(8,128)S(1)} %collective-permute-done.refs_0_, f32[148,128]{1,0:T(8,128)S(1)} %collective-permute-done.4.refs_1_, f32[148,128]{1,0:T(8,128)S(1)} %collective-permute-done.5.refs_2_, f32[78,128]{1,0:T(8,128)S(1)} %collective-permute-done.6.refs_3_, ...), custom_call_target="tpu_custom_call" | custom-call | tf_op jit(solution)/shard_map/combine/pallas_call | solution.py:274
Async XLA Ops:
  1.8 6.9 %collective-permute-start.1 = (f32[324,128]{1,0:T(8,128)S(1)}, f32[324,128]{1,0:T(8,128)S(1)}, u32[]{:S(2)}, u32[]{:S(2)}) collective-permute-start(f32[324,128]{1,0:T(8,128)S(1)} %get-tuple-element.15), channel_id=1, source_target_pairs={{0,1},{1,0},{2,3},{3,2},{4,5},{5,4},{6,7},{7,6},{8,9},{9,8},{10,11... | collective-permute-start | bytes 497672 | tf_op jit(solution)/shard_map/ppermute | solution.py:235
  2.4 4.1 %collective-permute-start.3 = (f32[36,128]{1,0:T(8,128)S(1)}, f32[36,128]{1,0:T(8,128)S(1)}, u32[]{:S(2)}, u32[]{:S(2)}) collective-permute-start(f32[36,128]{1,0:T(8,128)S(1)} %get-tuple-element.16.refs_0_), channel_id=1, source_target_pairs={{0,3},{1,2},{2,1},{3,0},{4,7},{5,6},{6,5},{7,4},{8,11},{9,10},{10,... | collective-permute-start | bytes 55304 | tf_op jit(solution)/shard_map/ppermute | solution.py:238
  5.0 3.8 %collective-permute-start.2 = (f32[36,128]{1,0:T(8,128)S(1)}, f32[36,128]{1,0:T(8,128)S(1)}, u32[]{:S(2)}, u32[]{:S(2)}) collective-permute-start(f32[36,128]{1,0:T(8,128)S(1)} %get-tuple-element.16.refs_0_), channel_id=1, source_target_pairs={{0,2},{1,3},{2,0},{3,1},{4,6},{5,7},{6,4},{7,5},{8,10},{9,11},{10,... | collective-permute-start | bytes 55304 | tf_op jit(solution)/shard_map/ppermute | solution.py:238
  9.0 5.8 %collective-permute-start.4 = (f32[148,128]{1,0:T(8,128)S(1)}, f32[148,128]{1,0:T(8,128)S(1)}, u32[]{:S(2)}, u32[]{:S(2)}) collective-permute-start(f32[148,128]{1,0:T(8,128)S(1)} %get-tuple-element.17), channel_id=1, source_target_pairs={{0,0},{1,5},{2,2},{3,7},{4,4},{5,1},{6,6},{7,3},{8,8},{9,13},{10,1... | collective-permute-start | bytes 227336 | tf_op jit(solution)/shard_map/ppermute | solution.py:263
  9.7 5.7 %collective-permute-start.5 = (f32[148,128]{1,0:T(8,128)S(1)}, f32[148,128]{1,0:T(8,128)S(1)}, u32[]{:S(2)}, u32[]{:S(2)}) collective-permute-start(f32[148,128]{1,0:T(8,128)S(1)} %get-tuple-element.18), channel_id=1, source_target_pairs={{0,12},{1,9},{2,14},{3,11},{4,8},{5,13},{6,10},{7,15},{8,4},{9,1},... | collective-permute-start | bytes 227336 | tf_op jit(solution)/shard_map/ppermute | solution.py:263
  12.3 7.4 %collective-permute-start.7 = (f32[148,128]{1,0:T(8,128)S(1)}, f32[148,128]{1,0:T(8,128)S(1)}, u32[]{:S(2)}, u32[]{:S(2)}) collective-permute-start(f32[148,128]{1,0:T(8,128)S(1)} %get-tuple-element.20), channel_id=1, source_target_pairs={{0,24},{1,29},{2,26},{3,31},{4,28},{5,25},{6,30},{7,27},{8,16},{9,... | collective-permute-start | bytes 227336 | tf_op jit(solution)/shard_map/ppermute | solution.py:263
  14.8 6.3 %collective-permute-start.6 = (f32[78,128]{1,0:T(8,128)S(1)}, f32[78,128]{1,0:T(8,128)S(1)}, u32[]{:S(2)}, u32[]{:S(2)}) collective-permute-start(f32[78,128]{1,0:T(8,128)S(1)} %get-tuple-element.19), channel_id=1, source_target_pairs={{0,20},{1,17},{2,22},{3,19},{4,16},{5,21},{6,18},{7,23},{8,28},{9,... | collective-permute-start | bytes 119816 | tf_op jit(solution)/shard_map/ppermute | solution.py:263
  14.8 12.6 %collective-permute-start.8 = (f32[148,128]{1,0:T(8,128)S(1)}, f32[148,128]{1,0:T(8,128)S(1)}, u32[]{:S(2)}, u32[]{:S(2)}) collective-permute-start(f32[148,128]{1,0:T(8,128)S(1)} %collective-permute-done.4.refs_1_), channel_id=1, source_target_pairs={{0,1},{1,0},{2,3},{3,2},{4,5},{5,4},{6,7},{7,6},{8,9},{9,8},{10,11... | collective-permute-start | bytes 227336 | tf_op jit(solution)/shard_map/ppermute | solution.py:264
  15.4 12.1 %collective-permute-start.9 = (f32[148,128]{1,0:T(8,128)S(1)}, f32[148,128]{1,0:T(8,128)S(1)}, u32[]{:S(2)}, u32[]{:S(2)}) collective-permute-start(f32[148,128]{1,0:T(8,128)S(1)} %collective-permute-done.5.refs_2_), channel_id=1, source_target_pairs={{0,1},{1,0},{2,3},{3,2},{4,5},{5,4},{6,7},{7,6},{8,9},{9,8},{10,11... | collective-permute-start | bytes 227336 | tf_op jit(solution)/shard_map/ppermute | solution.py:264
  19.7 7.8 %collective-permute-start.11 = (f32[148,128]{1,0:T(8,128)S(1)}, f32[148,128]{1,0:T(8,128)S(1)}, u32[]{:S(2)}, u32[]{:S(2)}) collective-permute-start(f32[148,128]{1,0:T(8,128)S(1)} %collective-permute-done.7.refs_4_), channel_id=1, source_target_pairs={{0,1},{1,0},{2,3},{3,2},{4,5},{5,4},{6,7},{7,6},{8,9},{9,8},{10,11... | collective-permute-start | bytes 227336 | tf_op jit(solution)/shard_map/ppermute | solution.py:264
  21.0 6.4 %collective-permute-start.10 = (f32[78,128]{1,0:T(8,128)S(1)}, f32[78,128]{1,0:T(8,128)S(1)}, u32[]{:S(2)}, u32[]{:S(2)}) collective-permute-start(f32[78,128]{1,0:T(8,128)S(1)} %collective-permute-done.6.refs_3_), channel_id=1, source_target_pairs={{0,1},{1,0},{2,3},{3,2},{4,5},{5,4},{6,7},{7,6},{8,9},{9,8},{10,11... | collective-permute-start | bytes 119816 | tf_op jit(solution)/shard_map/ppermute | solution.py:264
  21.1 6.3 %collective-permute-start = (f32[72,128]{1,0:T(8,128)S(1)}, f32[72,128]{1,0:T(8,128)S(1)}, u32[]{:S(2)}, u32[]{:S(2)}) collective-permute-start(f32[72,128]{1,0:T(8,128)S(1)} %get-tuple-element.13), channel_id=1, source_target_pairs={{0,20},{1,17},{2,22},{3,19},{4,16},{5,21},{6,18},{7,23},{8,28},{9,... | collective-permute-start | bytes 110600 | tf_op jit(solution)/shard_map/ppermute | solution.py:240

commit v10 on v9

--- a/solution.py
+++ b/solution.py
@@ -13,7 +13,7 @@
 
 
 def local_filter_kernel(
-    aperture_hbm, correlation_hbm, illumination_hbm, partial, message, handed, early,
+    aperture_hbm, correlation_hbm, illumination_hbm, partial, message,
     padded, correlation, illumination, aperture, arrived, read,
 ):
     shots, rows, cols, slab = correlation.shape
@@ -67,6 +67,15 @@
             turned = jnp.concatenate(held, axis=0).T
             message[at + r : at + r + 1] = turned[0:1]
             message[at + owners + r : at + owners + r + 1] = turned[slab - 1 : slab]
+
+
+def windows_kernel(partial, message, handed, early):
+    shots, rows, cols, _ = partial.shape
+    own = message.shape[1] // (shots * cols)
+    owners = rows // own
+    window = cols // 2 + 2
+    at = 4 * owners + shots
+    starts = [jnp.max(message[at + s : at + s + 1]).astype(jnp.int32) for s in range(shots)]
     edges = message.shape[0]
     handed[0:edges] = message[...]
     mine, core = lax.axis_index("shot"), lax.axis_index("depth") % 2
@@ -195,20 +204,14 @@
     params = pltpu.CompilerParams(vmem_limit_bytes=24 << 20)
     ahead = early_rounds(owners)
 
-    def local_body(aperture, correlation, illumination, partial, message, handed, *refs):
-        early = dict(zip(ahead, refs))
-        local_filter_kernel(aperture, correlation, illumination, partial, message, handed, early, *refs[len(ahead) :])
-
-    partial, message, handed, *early = pl.pallas_call(
-        local_body,
+    partial, message = pl.pallas_call(
+        local_filter_kernel,
         out_shape=(
             pltpu.VMEM(correlation.shape, f32),
             pltpu.VMEM((edges, width), f32),
-            pltpu.VMEM((edges + half * sent, width), f32),
-            *(pltpu.VMEM((sent, width), f32) for _ in ahead),
         ),
         in_specs=[hbm, hbm, hbm],
-        out_specs=(vmem,) * (3 + len(ahead)),
+        out_specs=(vmem, vmem),
         scratch_shapes=[
             pltpu.VMEM((shots, rows + 2, cols + 16, slab), f32),
             pltpu.VMEM(correlation.shape, f32),
@@ -220,6 +223,21 @@
         compiler_params=params,
         name="local_filter",
     )(in_hbm(aperture), in_hbm(correlation), in_hbm(illumination))
+
+    def windows_body(partial, message, handed, *refs):
+        windows_kernel(partial, message, handed, dict(zip(ahead, refs)))
+
+    handed, *early = pl.pallas_call(
+        windows_body,
+        out_shape=(
+            pltpu.VMEM((edges + half * sent, width), f32),
+            *(pltpu.VMEM((sent, width), f32) for _ in ahead),
+        ),
+        in_specs=[vmem, vmem],
+        out_specs=(vmem,) * (1 + len(ahead)),
+        compiler_params=params,
+        name="windows",
+    )(in_vmem(partial), in_vmem(message))
 
     def round_pairs(k):
         pairs = []

time: 28.4 us -> 28.6 us (level)
    pallas_call x1 -> x2, Pallas kernels: 1.83 us -> 1.95 us  [the longest x1 1.81 us: on_device(): pl.pallas_call(local_filter_kernel, out_shape=(pltpu.VMEM(correlation.sha...]
where the time goes in v10:
time: 28.6 us; the launch traced here: 28.4 us
  waiting for transfers between devices  14.4 us (50%)
  starting transfers between devices  10.9 us (38%)
  Pallas kernels  3.03 us (11%)
    ppermute x4, waiting for transfers between devices, on_device(): blocks[k] = lax.ppermute(blocks[k], ('shot', 'depth'), round_pairs(k))  6.18 us
    ppermute x4, starting transfers between devices, on_device(): blocks[k] = lax.ppermute(blocks[k], ('shot', 'depth'), round_pairs(k))  5.8 us
    ppermute x1, waiting for transfers between devices, on_device(): early[at] = lax.ppermute(early[at], ('shot', 'depth'), round_pairs(k))  4.47 us
    ppermute x2, waiting for transfers between devices, on_device(): messages.append(lax.ppermute(message, 'depth', pairs))  3.74 us
    ppermute x2, starting transfers between devices, on_device(): messages.append(lax.ppermute(message, 'depth', pairs))  2.63 us
    ppermute x1, starting transfers between devices, on_device(): early[at] = lax.ppermute(early[at], ('shot', 'depth'), round_pairs(k))  1.86 us
    pallas_call x1, Pallas kernels, on_device(): pl.pallas_call(local_filter_kernel, out_shape=(pltpu.VMEM(correlation.sha...  1.81 us
    pallas_call x1, Pallas kernels, on_device(): pl.pallas_call(combine_body, out_shape=jax.ShapeDtypeStruct((own, cols, s...  0.82 us
  transfers between devices with their start and end apart: 12, of which 6 were waited for; matrix products, arithmetic and copies ran while one was open for 0% of the time, Pallas kernels for 0%

profile of v10, /device:TPU:0, one launch (start us, length us, event | category | flops | bytes accessed | tf_op | source)
XLA Modules:
  0.0 28.4 jit_solution(8607138762322830600)
XLA Ops:
  0.0 1.8 %local_filter.1 = (f32[2,16,32,128]{3,2,1,0:T(8,128)S(1)}, f32[36,128]{1,0:T(8,128)S(1)}) custom-call(s32[2,4]{1,0:T(2,128)} %aperture_hbm.1, f32[2,16,32,128]{3,2,1,0:T(8,128)} %correlation_hbm.1, f32[2,16,32,128]{3,2,1,0:T(8,128)} %illumination_hbm.1), custom_call_target="tpu_custom_call" | custom-call | tf_op jit(solution)/shard_map/local_filter/pallas_call | solution.py:207
  1.8 0.1 windows.1
  2.0 0.6 %collective-permute-start.1 = (f32[324,128]{1,0:T(8,128)S(1)}, f32[324,128]{1,0:T(8,128)S(1)}, u32[]{:S(2)}, u32[]{:S(2)}) collective-permute-start(f32[324,128]{1,0:T(8,128)S(1)} %get-tuple-element.16), channel_id=1, source_target_pairs={{0,1},{1,0},{2,3},{3,2},{4,5},{5,4},{6,7},{7,6},{8,9},{9,8},{10,11... | collective-permute-start | bytes 497672 | tf_op jit(solution)/shard_map/ppermute | solution.py:253
  2.5 2.6 %collective-permute-start.3 = (f32[36,128]{1,0:T(8,128)S(1)}, f32[36,128]{1,0:T(8,128)S(1)}, u32[]{:S(2)}, u32[]{:S(2)}) collective-permute-start(f32[36,128]{1,0:T(8,128)S(1)} %get-tuple-element.14.message.refs_0_), channel_id=1, source_target_pairs={{0,3},{1,2},{2,1},{3,0},{4,7},{5,6},{6,5},{7,4},{8,11},{9,10},{10,... | collective-permute-start | bytes 55304 | tf_op jit(solution)/shard_map/ppermute | solution.py:256
  5.1 0.0 collective-permute-start.2
  5.2 1.4 %collective-permute-done.3.refs_2_ = f32[36,128]{1,0:T(8,128)S(1)} collective-permute-done((f32[36,128]{1,0:T(8,128)S(1)}, f32[36,128]{1,0:T(8,128)S(1)}, u32[]{:S(2)}, u32[]{:S(2)}) %collective-permute-start.3) | collective-permute-done | bytes 18464 | tf_op jit(solution)/shard_map/ppermute | solution.py:256
  6.6 2.3 %collective-permute-done.2.refs_1_ = f32[36,128]{1,0:T(8,128)S(1)} collective-permute-done((f32[36,128]{1,0:T(8,128)S(1)}, f32[36,128]{1,0:T(8,128)S(1)}, u32[]{:S(2)}, u32[]{:S(2)}) %collective-permute-start.2) | collective-permute-done | bytes 18464 | tf_op jit(solution)/shard_map/ppermute | solution.py:256
  8.9 0.0 collective-permute-done.1.handed
  8.9 0.3 finish_filter.1
  9.2 0.7 %collective-permute-start.4 = (f32[148,128]{1,0:T(8,128)S(1)}, f32[148,128]{1,0:T(8,128)S(1)}, u32[]{:S(2)}, u32[]{:S(2)}) collective-permute-start(f32[148,128]{1,0:T(8,128)S(1)} %get-tuple-element.17), channel_id=1, source_target_pairs={{0,0},{1,5},{2,2},{3,7},{4,4},{5,1},{6,6},{7,3},{8,8},{9,13},{10,1... | collective-permute-start | bytes 227336 | tf_op jit(solution)/shard_map/ppermute | solution.py:281
  9.8 2.6 %collective-permute-start.5 = (f32[148,128]{1,0:T(8,128)S(1)}, f32[148,128]{1,0:T(8,128)S(1)}, u32[]{:S(2)}, u32[]{:S(2)}) collective-permute-start(f32[148,128]{1,0:T(8,128)S(1)} %get-tuple-element.18), channel_id=1, source_target_pairs={{0,12},{1,9},{2,14},{3,11},{4,8},{5,13},{6,10},{7,15},{8,4},{9,1},... | collective-permute-start | bytes 227336 | tf_op jit(solution)/shard_map/ppermute | solution.py:281
  12.4 2.5 %collective-permute-start.7 = (f32[148,128]{1,0:T(8,128)S(1)}, f32[148,128]{1,0:T(8,128)S(1)}, u32[]{:S(2)}, u32[]{:S(2)}) collective-permute-start(f32[148,128]{1,0:T(8,128)S(1)} %get-tuple-element.20), channel_id=1, source_target_pairs={{0,24},{1,29},{2,26},{3,31},{4,28},{5,25},{6,30},{7,27},{8,16},{9,... | collective-permute-start | bytes 227336 | tf_op jit(solution)/shard_map/ppermute | solution.py:281
  14.9 0.1 collective-permute-start.6
  15.0 0.0 collective-permute-done.4.refs_1_
  15.0 0.0 collective-permute-start.8
  15.0 0.5 %collective-permute-done.5.refs_2_ = f32[148,128]{1,0:T(8,128)S(1)} collective-permute-done((f32[148,128]{1,0:T(8,128)S(1)}, f32[148,128]{1,0:T(8,128)S(1)}, u32[]{:S(2)}, u32[]{:S(2)}) %collective-permute-start.5) | collective-permute-done | bytes 75808 | tf_op jit(solution)/shard_map/ppermute | solution.py:281
  15.5 0.0 collective-permute-start.9
  15.5 4.3 %collective-permute-done.7.refs_4_ = f32[148,128]{1,0:T(8,128)S(1)} collective-permute-done((f32[148,128]{1,0:T(8,128)S(1)}, f32[148,128]{1,0:T(8,128)S(1)}, u32[]{:S(2)}, u32[]{:S(2)}) %collective-permute-start.7) | collective-permute-done | bytes 75808 | tf_op jit(solution)/shard_map/ppermute | solution.py:281
  19.8 0.0 collective-permute-start.11
  19.8 1.4 %collective-permute-done.6.refs_3_ = f32[78,128]{1,0:T(8,128)S(1)} collective-permute-done((f32[78,128]{1,0:T(8,128)S(1)}, f32[78,128]{1,0:T(8,128)S(1)}, u32[]{:S(2)}, u32[]{:S(2)}) %collective-permute-start.6) | collective-permute-done | bytes 39968 | tf_op jit(solution)/shard_map/ppermute | solution.py:281
  21.2 0.1 collective-permute-start.10
  21.2 1.9 %collective-permute-start = (f32[72,128]{1,0:T(8,128)S(1)}, f32[72,128]{1,0:T(8,128)S(1)}, u32[]{:S(2)}, u32[]{:S(2)}) collective-permute-start(f32[72,128]{1,0:T(8,128)S(1)} %get-tuple-element.15), channel_id=1, source_target_pairs={{0,20},{1,17},{2,22},{3,19},{4,16},{5,21},{6,18},{7,23},{8,28},{9,... | collective-permute-start | bytes 110600 | tf_op jit(solution)/shard_map/ppermute | solution.py:258
  23.1 4.5 %collective-permute-done.refs_0_ = f32[72,128]{1,0:T(8,128)S(1)} collective-permute-done((f32[72,128]{1,0:T(8,128)S(1)}, f32[72,128]{1,0:T(8,128)S(1)}, u32[]{:S(2)}, u32[]{:S(2)}) %collective-permute-start) | collective-permute-done | bytes 36896 | tf_op jit(solution)/shard_map/ppermute | solution.py:258
  27.6 0.0 collective-permute-done.10.refs_7_
  27.6 0.0 collective-permute-done.8.refs_5_
  27.6 0.0 collective-permute-done.9.refs_6_
  27.6 0.0 collective-permute-done.11.refs_8_
  27.6 0.8 %combine.1 = f32[2,32,128]{2,1,0:T(8,128)} custom-call(f32[72,128]{1,0:T(8,128)S(1)} %collective-permute-done.refs_0_, f32[148,128]{1,0:T(8,128)S(1)} %collective-permute-done.4.refs_1_, f32[148,128]{1,0:T(8,128)S(1)} %collective-permute-done.5.refs_2_, f32[78,128]{1,0:T(8,128)S(1)} %collective-permute-done.6.refs_3_, ...), custom_call_target="tpu_custom_call" | custom-call | tf_op jit(solution)/shard_map/combine/pallas_call | solution.py:292
Async XLA Ops:
  2.0 6.9 %collective-permute-start.1 = (f32[324,128]{1,0:T(8,128)S(1)}, f32[324,128]{1,0:T(8,128)S(1)}, u32[]{:S(2)}, u32[]{:S(2)}) collective-permute-start(f32[324,128]{1,0:T(8,128)S(1)} %get-tuple-element.16), channel_id=1, source_target_pairs={{0,1},{1,0},{2,3},{3,2},{4,5},{5,4},{6,7},{7,6},{8,9},{9,8},{10,11... | collective-permute-start | bytes 497672 | tf_op jit(solution)/shard_map/ppermute | solution.py:253
  2.5 4.1 %collective-permute-start.3 = (f32[36,128]{1,0:T(8,128)S(1)}, f32[36,128]{1,0:T(8,128)S(1)}, u32[]{:S(2)}, u32[]{:S(2)}) collective-permute-start(f32[36,128]{1,0:T(8,128)S(1)} %get-tuple-element.14.message.refs_0_), channel_id=1, source_target_pairs={{0,3},{1,2},{2,1},{3,0},{4,7},{5,6},{6,5},{7,4},{8,11},{9,10},{10,... | collective-permute-start | bytes 55304 | tf_op jit(solution)/shard_map/ppermute | solution.py:256
  5.1 3.8 %collective-permute-start.2 = (f32[36,128]{1,0:T(8,128)S(1)}, f32[36,128]{1,0:T(8,128)S(1)}, u32[]{:S(2)}, u32[]{:S(2)}) collective-permute-start(f32[36,128]{1,0:T(8,128)S(1)} %get-tuple-element.14.message.refs_0_), channel_id=1, source_target_pairs={{0,2},{1,3},{2,0},{3,1},{4,6},{5,7},{6,4},{7,5},{8,10},{9,11},{10,... | collective-permute-start | bytes 55304 | tf_op jit(solution)/shard_map/ppermute | solution.py:256
  9.2 5.8 %collective-permute-start.4 = (f32[148,128]{1,0:T(8,128)S(1)}, f32[148,128]{1,0:T(8,128)S(1)}, u32[]{:S(2)}, u32[]{:S(2)}) collective-permute-start(f32[148,128]{1,0:T(8,128)S(1)} %get-tuple-element.17), channel_id=1, source_target_pairs={{0,0},{1,5},{2,2},{3,7},{4,4},{5,1},{6,6},{7,3},{8,8},{9,13},{10,1... | collective-permute-start | bytes 227336 | tf_op jit(solution)/shard_map/ppermute | solution.py:281
  9.8 5.7 %collective-permute-start.5 = (f32[148,128]{1,0:T(8,128)S(1)}, f32[148,128]{1,0:T(8,128)S(1)}, u32[]{:S(2)}, u32[]{:S(2)}) collective-permute-start(f32[148,128]{1,0:T(8,128)S(1)} %get-tuple-element.18), channel_id=1, source_target_pairs={{0,12},{1,9},{2,14},{3,11},{4,8},{5,13},{6,10},{7,15},{8,4},{9,1},... | collective-permute-start | bytes 227336 | tf_op jit(solution)/shard_map/ppermute | solution.py:281
  12.4 7.4 %collective-permute-start.7 = (f32[148,128]{1,0:T(8,128)S(1)}, f32[148,128]{1,0:T(8,128)S(1)}, u32[]{:S(2)}, u32[]{:S(2)}) collective-permute-start(f32[148,128]{1,0:T(8,128)S(1)} %get-tuple-element.20), channel_id=1, source_target_pairs={{0,24},{1,29},{2,26},{3,31},{4,28},{5,25},{6,30},{7,27},{8,16},{9,... | collective-permute-start | bytes 227336 | tf_op jit(solution)/shard_map/ppermute | solution.py:281
  14.9 6.3 %collective-permute-start.6 = (f32[78,128]{1,0:T(8,128)S(1)}, f32[78,128]{1,0:T(8,128)S(1)}, u32[]{:S(2)}, u32[]{:S(2)}) collective-permute-start(f32[78,128]{1,0:T(8,128)S(1)} %get-tuple-element.19), channel_id=1, source_target_pairs={{0,20},{1,17},{2,22},{3,19},{4,16},{5,21},{6,18},{7,23},{8,28},{9,... | collective-permute-start | bytes 119816 | tf_op jit(solution)/shard_map/ppermute | solution.py:281
  15.0 12.6 %collective-permute-start.8 = (f32[148,128]{1,0:T(8,128)S(1)}, f32[148,128]{1,0:T(8,128)S(1)}, u32[]{:S(2)}, u32[]{:S(2)}) collective-permute-start(f32[148,128]{1,0:T(8,128)S(1)} %collective-permute-done.4.refs_1_), channel_id=1, source_target_pairs={{0,1},{1,0},{2,3},{3,2},{4,5},{5,4},{6,7},{7,6},{8,9},{9,8},{10,11... | collective-permute-start | bytes 227336 | tf_op jit(solution)/shard_map/ppermute | solution.py:282
  15.5 12.1 %collective-permute-start.9 = (f32[148,128]{1,0:T(8,128)S(1)}, f32[148,128]{1,0:T(8,128)S(1)}, u32[]{:S(2)}, u32[]{:S(2)}) collective-permute-start(f32[148,128]{1,0:T(8,128)S(1)} %collective-permute-done.5.refs_2_), channel_id=1, source_target_pairs={{0,1},{1,0},{2,3},{3,2},{4,5},{5,4},{6,7},{7,6},{8,9},{9,8},{10,11... | collective-permute-start | bytes 227336 | tf_op jit(solution)/shard_map/ppermute | solution.py:282
  19.8 7.8 %collective-permute-start.11 = (f32[148,128]{1,0:T(8,128)S(1)}, f32[148,128]{1,0:T(8,128)S(1)}, u32[]{:S(2)}, u32[]{:S(2)}) collective-permute-start(f32[148,128]{1,0:T(8,128)S(1)} %collective-permute-done.7.refs_4_), channel_id=1, source_target_pairs={{0,1},{1,0},{2,3},{3,2},{4,5},{5,4},{6,7},{7,6},{8,9},{9,8},{10,11... | collective-permute-start | bytes 227336 | tf_op jit(solution)/shard_map/ppermute | solution.py:282
  21.2 6.4 %collective-permute-start.10 = (f32[78,128]{1,0:T(8,128)S(1)}, f32[78,128]{1,0:T(8,128)S(1)}, u32[]{:S(2)}, u32[]{:S(2)}) collective-permute-start(f32[78,128]{1,0:T(8,128)S(1)} %collective-permute-done.6.refs_3_), channel_id=1, source_target_pairs={{0,1},{1,0},{2,3},{3,2},{4,5},{5,4},{6,7},{7,6},{8,9},{9,8},{10,11... | collective-permute-start | bytes 119816 | tf_op jit(solution)/shard_map/ppermute | solution.py:282
  21.2 6.3 %collective-permute-start = (f32[72,128]{1,0:T(8,128)S(1)}, f32[72,128]{1,0:T(8,128)S(1)}, u32[]{:S(2)}, u32[]{:S(2)}) collective-permute-start(f32[72,128]{1,0:T(8,128)S(1)} %get-tuple-element.15), channel_id=1, source_target_pairs={{0,20},{1,17},{2,22},{3,19},{4,16},{5,21},{6,18},{7,23},{8,28},{9,... | collective-permute-start | bytes 110600 | tf_op jit(solution)/shard_map/ppermute | solution.py:258
